TPU v7x, 512 devices: a whole 4x8x8 slice. The times are simulated.
512 devices in a mesh: section: 4 (over x), shard: 128 (over y, z, core).
Axes of the slice: x: 4, y: 8, z: 8, core: 2. Of those that a mesh axis runs over, the one named last changes fastest.
Arguments:
- user_dense: bfloat16 [128, 1024], P('shard'), may hold values from -6 to 6
- tables: bfloat16 [4, 262144, 128], P('section', 'shard'), may hold values from -3 to 3
- feat_owner: int32 [4, 128, 1024, 1], P('section', 'shard'), may hold values from 0 to 127; in each aligned block of 1024 rows (0 to 1023, 1024 to 2047, ..., all dimensions but the last counted through in order) at most 16 rows name the same one
- feat_row: int32 [4, 128, 1024], P('section', 'shard'), may hold values from 0 to 2047
- keep_first: int32 [128, 256], P('shard'), may hold values from 0 to 1023, all different within a row
- keep_second: int32 [128, 32], P('shard'), may hold values from 0 to 255, all different within a row
- section_weight: bfloat16 [4, 1024, 1024], P('section'), may hold values from -0.1875 to 0.1875
- section_head: float32 [4, 1024], P('section'), may hold values from -5 to 5
- user_proj: bfloat16 [1024, 128], replicated, may hold values from -0.1875 to 0.1875
- item_in: bfloat16 [128, 512], replicated, may hold values from -0.5 to 0.5
- item_out: bfloat16 [512, 128], replicated, may hold values from -0.25 to 0.25
- prerank_feat: bfloat16 [512, 1024], replicated, may hold values from -0.25 to 0.25
- prerank_item: bfloat16 [128, 1024], replicated, may hold values from -0.5 to 0.5
Outputs:
- section_scores: float32 [4, 128, 32], P('section', 'shard')
Inputs may be any that keep to these rules, and one draw needn't show every extreme that they name: `feat_owner`: among the 1024 requests of one user in one section, no shard index occurs more than 16 times, and 16 times in some of them. `keep_first`: the 256 entries of a row are distinct. `keep_second`: the 32 entries of a row are distinct.
All inputs are finite; a program needn't handle non-finite values.
Results may differ from a plain program's by a relative error of at most 0.007.
Values may be sent and summed in bfloat16 or wider, within the bound.
No kernel may reach another device: no remote copies, remote signals or barrier semaphores. Data moves between devices by JAX's collectives and lax.ppermute only.
A program may use at most 64 MiB of HBM per device.

v0:
```python
import functools
import math

import jax
import jax.numpy as jnp
from jax import lax
from jax.sharding import PartitionSpec as P


def shortened(array):
    return jax.tree.map(lambda a: a.astype(jnp.bfloat16) if a.dtype == jnp.float32 else a, array)


def shifted(array, axis, by):
    length = lax.axis_size(axis)
    pairs = [(i, i + by) for i in range(length) if 0 <= i + by < length]
    return lax.ppermute(array, axis, pairs)


def fetch(table_local, owners, local_rows):
    shard_count = lax.axis_size("shard")
    user_count, cand_count = owners.shape
    slot_count = 2 * cand_count // shard_count
    ordering = jnp.argsort(owners, axis=1, stable=True)
    sorted_owner = jnp.take_along_axis(owners, ordering, axis=1)
    sorted_local = jnp.take_along_axis(local_rows, ordering, axis=1)
    matches = owners[:, :, None] == jnp.arange(shard_count, dtype=jnp.int32)[None, None, :]
    tallies = jnp.sum(matches.astype(jnp.int32), axis=1)
    offsets = jnp.cumsum(tallies, axis=1) - tallies
    leading = jnp.take_along_axis(offsets, sorted_owner, axis=1)
    position = jnp.arange(cand_count, dtype=jnp.int32)[None, :] - leading
    slot_sorted = sorted_owner * slot_count + position
    user_rows = jnp.arange(user_count, dtype=jnp.int32)[:, None]
    request = (
        jnp.zeros((user_count, shard_count * slot_count), jnp.int32)
        .at[user_rows, slot_sorted]
        .set(sorted_local)
    )
    slot_index = (
        jnp.zeros((user_count, cand_count), jnp.int32).at[user_rows, ordering].set(slot_sorted)
    )
    served = table_local[
        lax.all_to_all(
            request.reshape(user_count, shard_count, slot_count),
            "shard",
            split_axis=1,
            concat_axis=1,
            tiled=True,
        )
    ]
    returned = lax.all_to_all(served, "shard", split_axis=1, concat_axis=1, tiled=True)
    returned = returned.reshape(user_count, shard_count * slot_count, -1)
    return jnp.take_along_axis(returned, slot_index[:, :, None], axis=1)


def pad_logits(kept_logits, kept_count):
    widened = jnp.pad(kept_logits, ((0, 0), (0, kept_count - kept_logits.shape[1])))
    return widened.astype(jnp.bfloat16)


def section_zero(operands, weights):
    embedded, packet, prior, user_part, first_keep, second_keep = operands
    main_weight, head_vec, user_proj, item_in, item_out, prerank_feat, prerank_item = weights
    micro_size = user_part.shape[0]
    emb_width = item_in.shape[0]
    active = jax.nn.relu(jnp.dot(user_part, main_weight, preferred_element_type=jnp.float32))
    user_query = (active * head_vec).astype(jnp.bfloat16)
    user_vec = jnp.dot(user_query, user_proj, preferred_element_type=jnp.float32)
    hidden = jax.nn.relu(
        jnp.dot(embedded.reshape(-1, emb_width), item_in, preferred_element_type=jnp.float32)
    ).astype(jnp.bfloat16)
    tower_out = (
        jnp.dot(hidden, item_out, preferred_element_type=jnp.float32)
        .astype(jnp.bfloat16)
        .reshape(micro_size, -1, emb_width)
    )
    logits = jnp.einsum(
        "bcd,bd->bc", tower_out.astype(jnp.float32), user_vec, precision=lax.Precision.HIGHEST
    )
    kept_rows = jnp.take_along_axis(tower_out, first_keep[:, :, None], axis=1)
    kept_logits = jnp.take_along_axis(logits, first_keep, axis=1)
    scored = jnp.take_along_axis(kept_logits, second_keep, axis=1)
    return (kept_rows, kept_logits.astype(jnp.bfloat16), scored)


def section_one(operands, weights):
    embedded, packet, prior, user_part, first_keep, second_keep = operands
    main_weight, head_vec, user_proj, item_in, item_out, prerank_feat, prerank_item = weights
    micro_size, kept_count, emb_width = packet.shape
    hid_width = main_weight.shape[1]
    features = embedded.reshape(micro_size * kept_count, -1)
    pre_act = jnp.dot(features, prerank_feat, preferred_element_type=jnp.float32)
    pre_act = pre_act + jnp.dot(
        packet.reshape(-1, emb_width), prerank_item, preferred_element_type=jnp.float32
    )
    inner_act = jax.nn.relu(pre_act).astype(jnp.bfloat16)
    hidden = jax.nn.relu(jnp.dot(inner_act, main_weight, preferred_element_type=jnp.float32))
    logits = jnp.sum(hidden * head_vec, axis=1).reshape(micro_size, kept_count) / math.sqrt(
        hid_width
    ) + prior.astype(jnp.float32)
    carried = hidden.astype(jnp.bfloat16).reshape(micro_size, kept_count, hid_width)
    kept_rows = jnp.take_along_axis(carried, second_keep[:, :, None], axis=1)
    kept_logits = jnp.take_along_axis(logits, second_keep, axis=1)
    return (kept_rows.reshape(packet.shape), pad_logits(kept_logits, kept_count), kept_logits)


def section_rank(operands, weights):
    embedded, packet, prior, user_part, first_keep, second_keep = operands
    main_weight, head_vec, user_proj, item_in, item_out, prerank_feat, prerank_item = weights
    micro_size, kept_count, emb_width = packet.shape
    hid_width = main_weight.shape[1]
    final_count = second_keep.shape[1]
    features = embedded.reshape(micro_size, final_count, -1, emb_width)
    gram_flat = jnp.einsum(
        "bkfd,bkgd->bkfg", features, features, preferred_element_type=jnp.float32
    ) / math.sqrt(emb_width)
    gram_flat = gram_flat.astype(jnp.bfloat16).reshape(micro_size * final_count, -1)
    carried = packet.reshape(micro_size * final_count, hid_width).astype(jnp.float32)
    hidden = jax.nn.relu(
        jnp.dot(gram_flat, main_weight, preferred_element_type=jnp.float32) + carried
    )
    logits = jnp.sum(hidden * head_vec, axis=1).reshape(micro_size, final_count) / math.sqrt(
        hid_width
    )
    logits = logits + prior[:, :final_count].astype(jnp.float32)
    out_packet = hidden.astype(jnp.bfloat16).reshape(packet.shape)
    return (out_packet, pad_logits(logits, kept_count), logits)


def per_device(
    user_dense,
    tables,
    feat_owner,
    feat_row,
    keep_first,
    keep_second,
    section_weight,
    section_head,
    user_proj,
    item_in,
    item_out,
    prerank_feat,
    prerank_item,
):
    section_idx = lax.axis_index("section")
    section_count = lax.axis_size("section")
    table_local = tables[0]
    owners = feat_owner[0, :, :, 0]
    local_rows = feat_row[0]
    weights = (
        section_weight[0],
        section_head[0],
        user_proj,
        item_in,
        item_out,
        prerank_feat,
        prerank_item,
    )
    user_count = user_dense.shape[0]
    kept_count = keep_first.shape[1]
    final_count = keep_second.shape[1]
    emb_width = tables.shape[2]
    batch_count = user_count // user_count
    tick_count = batch_count + section_count - 1
    fetched = fetch(table_local, owners, local_rows)
    branches = [
        functools.partial(section_zero, weights=weights),
        functools.partial(section_one, weights=weights),
        functools.partial(section_rank, weights=weights),
        functools.partial(section_rank, weights=weights),
    ]

    def tick(tick_num, loop_state):
        packet, prior, scores = loop_state
        batch_idx = tick_num - section_idx
        active_tick = (batch_idx >= 0) & (batch_idx < batch_count)
        row_start = jnp.clip(batch_idx, 0, batch_count - 1) * user_count
        operands = (fetched, packet, prior, user_dense, keep_first, keep_second)

        def working():
            return lax.switch(section_idx, branches, operands)

        def resting():
            return (
                jnp.zeros_like(packet),
                jnp.zeros_like(prior),
                jnp.zeros((user_count, final_count), jnp.float32),
            )

        out_packet, out_prior, scored = lax.cond(active_tick, working, resting)
        updated = lax.dynamic_update_slice_in_dim(scores, scored, row_start, 0)
        scores = jnp.where(active_tick, updated, scores)
        packet, prior = (
            shifted(shortened(out_packet), "section", 1).astype(out_packet.dtype),
            shifted(shortened(out_prior), "section", 1).astype(out_prior.dtype),
        )
        return (packet, prior, scores)

    initial = (
        jnp.zeros((user_count, kept_count, emb_width), jnp.bfloat16),
        jnp.zeros((user_count, kept_count), jnp.bfloat16),
        jnp.zeros((user_count, final_count), jnp.float32),
    )
    packet, prior, scores = lax.fori_loop(0, tick_count, tick, initial)
    return scores[None]


def solution(mesh):
    placed = (
        P("shard", None),
        P("section", "shard", None),
        P("section", "shard", None, None),
        P("section", "shard", None),
        P("shard", None),
        P("shard", None),
        P("section", None, None),
        P("section", None),
        P(),
        P(),
        P(),
        P(),
        P(),
    )
    return jax.shard_map(
        per_device,
        mesh=mesh,
        in_specs=placed,
        out_specs=P("section", "shard", None),
        check_vma=False,
    )
```

profile of v0, /device:TPU:2, one launch (start us, length us, event | category | flops | bytes accessed | tf_op | source)
XLA Modules:
  0.0 161.9 jit_solution(11421001093318712278)
XLA Ops:
  7.3 0.9 convert_reduce_fusion
  8.5 4.9 %sort.19.cloned.1.call-done = (s32[1,1024]{1,0:T(1,128)}, s32[1,1024]{1,0:T(1,128)}) async-done(((s32[1,1024]{1,0:T(1,128)}, s32[1,1024]{1,0:T(1,128)}), (s32[1,1024]{1,0:T(1,128)}, s32[1,1024]{1,0:T(1,128)})) %sort.19.cloned.1.call-update) | async-done | bytes 8208 | tf_op jit(solution)/shard_map/jit(argsort)/sort | solution.py:24
  13.4 0.7 compare_select_fusion.11
  14.1 4.5 %gather_fusion.8 = s32[1024]{0:T(1024)S(1)} fusion(s32[1024]{0:T(1024)S(1)} %bitcast.120, s32[1024]{0:T(1024)S(1)} %broadcast_clamp_fusion.3), kind=kCustom, calls=%fused_computation.clone | custom fusion | bytes 12288 | tf_op jit(solution)/shard_map/jit(take_along_axis)/gather | solution.py:25
  18.6 4.5 %gather_fusion.9 = s32[1024]{0:T(1024)S(1)} fusion(s32[1024]{0:T(1024)S(1)} %bitcast.121, s32[1024]{0:T(1024)S(1)} %broadcast_clamp_fusion.3), kind=kCustom, calls=%fused_computation.4.clone | custom fusion | bytes 12288 | tf_op jit(solution)/shard_map/jit(take_along_axis)/gather | solution.py:26
  23.3 6.6 %gather_fusion.5 = s32[1024]{0:T(1024)S(1)} fusion(s32[128]{0:T(128)S(1)} %subtract_bitcast_fusion, s32[1024]{0:T(1024)S(1)} %broadcast_clamp_fusion.2), kind=kCustom, calls=%fused_computation.7 | custom fusion | bytes 12288 | tf_op jit(solution)/shard_map/jit(take_along_axis)/gather | solution.py:30
  30.1 4.3 %scatter_custom_fusion.1 = s32[2048]{0:T(1024)S(1)} fusion(s32[1024]{0:T(1024)S(1)} %broadcast_select_fusion.5, s32[1024]{0:T(1024)S(1)} %bitcast.146, s32[]{:T(128)} %constant.178.clone.1), kind=kCustom, calls=%fused_computation.92 | custom fusion | bytes 8196
  34.4 0.7 reshape.510
  35.1 17.8 %all-to-all-start = ((s32[1,128,16]{2,0,1:T(1,128)}), s32[1,128,16]{2,0,1:T(1,128)S(1)}, u32[]{:S(2)}, u32[]{:S(2)}) async-start(s32[1,128,16]{2,0,1:T(1,128)} %bitcast.48), calls=%async_computation | async-start | bytes 131072 | tf_op jit(solution)/shard_map/all_to_all | solution.py:43
  52.9 11.2 %all-to-all-done = s32[1,128,16]{2,0,1:T(1,128)S(1)} async-done(((s32[1,128,16]{2,0,1:T(1,128)}), s32[1,128,16]{2,0,1:T(1,128)S(1)}, u32[]{:S(2)}, u32[]{:S(2)}) %all-to-all-start) | async-done | bytes 8224 | tf_op jit(solution)/shard_map/all_to_all | solution.py:43
  64.4 8.0 %gather_fusion.6 = bf16[2048,128]{1,0:T(8,128)(2,1)} fusion(bf16[2048,128]{1,0:T(8,128)(2,1)S(1)} %bitcast.114, s32[2048]{0:T(1024)S(1)} %broadcast_clamp_fusion), kind=kCustom, calls=%fused_computation.8 | custom fusion | bytes 1056768 | tf_op jit(solution)/shard_map/gather | solution.py:42
  72.4 6.3 %all-to-all-start.1 = ((bf16[1,128,16,128]{3,2,0,1:T(8,128)(2,1)}), bf16[1,128,16,128]{3,2,0,1:T(8,128)(2,1)S(1)}, u32[]{:S(2)}, u32[]{:S(2)}) async-start(bf16[1,128,16,128]{3,2,0,1:T(8,128)(2,1)} %bitcast.126), calls=%async_computation.1 | async-start | bytes 1048576 | tf_op jit(solution)/shard_map/all_to_all | solution.py:51
  79.0 4.5 %scatter_custom_fusion = s32[1024]{0:T(1024)S(1)} fusion(s32[1024]{0:T(1024)S(1)} %broadcast_select_fusion.6, s32[1024]{0:T(1024)S(1)} %bitcast.145, s32[]{:T(128)} %constant.178.clone.1), kind=kCustom, calls=%fused_computation.103 | custom fusion | bytes 4100 | tf_op jit(solution)/shard_map/broadcast_in_dim | solution.py:53
  83.5 15.7 %all-to-all-done.1 = bf16[1,128,16,128]{3,2,0,1:T(8,128)(2,1)S(1)} async-done(((bf16[1,128,16,128]{3,2,0,1:T(8,128)(2,1)}), bf16[1,128,16,128]{3,2,0,1:T(8,128)(2,1)S(1)}, u32[]{:S(2)}, u32[]{:S(2)}) %all-to-all-start.1) | async-done | bytes 524320 | tf_op jit(solution)/shard_map/all_to_all | solution.py:51
  99.2 3.2 %gather_fusion.7 = bf16[1024,128]{1,0:T(8,128)(2,1)S(1)} fusion(bf16[2048,128]{1,0:T(8,128)(2,1)S(1)} %bitcast.125, s32[1024]{0:T(1024)S(1)} %broadcast_clamp_fusion.1), kind=kCustom, calls=%fused_computation.9 | custom fusion | bytes 528384 | tf_op jit(solution)/shard_map/jit(take_along_axis)/gather | solution.py:53
  102.7 52.3 %while.18 = (s32[]{:T(128)}, bf16[1,256,128]{2,1,0:T(8,128)(2,1)S(1)}, bf16[1,256]{1,0:T(2,128)(2,1)S(1)}, f32[1,32]{1,0:T(1,128)}, s32[]{:T(128)}, /*index=5*/s...) while((s32[]{:T(128)}, ...), condition=%wide.region_15.18_spmd.clone, body=%wide.region_5.17_spmd.clone.sunk | while | flops 874286272 | bytes 7691208 | solution.py:204
  102.7 1.8 %conditional.6 = (bf16[1,256,128]{2,1,0:T(8,128)(2,1)}, bf16[1,256]{1,0:T(2,128)(2,1)}, f32[1,32]{1,0:T(1,128)}) conditional(s32[]{:T(128)} %convert_element_type.123, () %tuple.95, (s32[]{:T(128)}, s32[1,256]{1,0:T(1,128)S(1)}, bf16[1,1024,128]{2,1,0:T(8,128)(2,1)S(1)}, bf16[128,512]{1,0:T(8,128)(2,1)}, bf16[512,128]{1,0:T(8,128)(2,1)}, ...), branch_computations={%region_6.7_spmd, %region_7.16_spmd} | conditional | flops 874286208 | bytes 7426226 | solution.py:190
  102.8 0.6 broadcast.300
  104.6 3.4 %collective-permute-start = (bf16[1,256,128]{2,1,0:T(8,128)(2,1)}, bf16[1,256,128]{2,1,0:T(8,128)(2,1)S(1)}, u32[]{:S(2)}, u32[]{:S(2)}) collective-permute-start(bf16[1,256,128]{2,1,0:T(8,128)(2,1)} %get-tuple-element.615), channel_id=1, source_target_pairs={{0,128},{128,256},{256,384},{1,129},{129,257},{257,385},{2,130},{1... | collective-permute-start | bytes 196616 | tf_op jit(solution)/shard_map/while/body/eval_jaxpr/ppermute | solution.py:17
  108.0 3.1 %collective-permute-start.1 = (bf16[1,256]{1,0:T(2,128)(2,1)}, bf16[1,256]{1,0:T(2,128)(2,1)S(1)}, u32[]{:S(2)}, u32[]{:S(2)}) collective-permute-start(bf16[1,256]{1,0:T(2,128)(2,1)} %get-tuple-element.616), channel_id=1, source_target_pairs={{0,128},{128,256},{256,384},{1,129},{129,257},{257,385},{2,130},{1... | collective-permute-start | bytes 1544 | tf_op jit(solution)/shard_map/while/body/eval_jaxpr/ppermute | solution.py:17
  111.6 4.8 %collective-permute-done.1 = bf16[1,256]{1,0:T(2,128)(2,1)S(1)} collective-permute-done((bf16[1,256]{1,0:T(2,128)(2,1)}, bf16[1,256]{1,0:T(2,128)(2,1)S(1)}, u32[]{:S(2)}, u32[]{:S(2)}) %collective-permute-start.1) | collective-permute-done | bytes 544 | tf_op jit(solution)/shard_map/while/body/eval_jaxpr/ppermute | solution.py:17
  116.4 11.0 %conditional.6 = (bf16[1,256,128]{2,1,0:T(8,128)(2,1)}, bf16[1,256]{1,0:T(2,128)(2,1)}, f32[1,32]{1,0:T(1,128)}) conditional(s32[]{:T(128)} %convert_element_type.123, () %tuple.95, (s32[]{:T(128)}, s32[1,256]{1,0:T(1,128)S(1)}, bf16[1,1024,128]{2,1,0:T(8,128)(2,1)S(1)}, bf16[128,512]{1,0:T(8,128)(2,1)}, bf16[512,128]{1,0:T(8,128)(2,1)}, ...), branch_computations={%region_6.7_spmd, %region_7.16_spmd} | conditional | flops 874286208 | bytes 7426226 | solution.py:190
  116.4 11.0 %conditional.2 = (bf16[1,256,128]{2,1,0:T(8,128)(2,1)}, f32[1,32]{1,0:T(1,128)}, bf16[1,256]{1,0:T(2,128)(2,1)}) conditional(s32[]{:T(128)} %clamp.2, (s32[1,256]{1,0:T(1,128)S(1)}, bf16[1,1024,128]{2,1,0:T(8,128)(2,1)S(1)}, bf16[128,512]{1,0:T(8,128)(2,1)}, bf16[512,128]{1,0:T(8,128)(2,1)}, ...), branch_computations={%region_8.9_spmd, %region_9.11_spmd, %region_11.13_spmd, %region_1... | conditional | flops 874286208 | bytes 7426010
  116.4 0.7 fusion.23
  117.3 2.6 %fusion.42 = f32[256,1024]{1,0:T(8,128)} fusion(bf16[256,512]{1,0:T(8,128)(2,1)S(1)} %reshape.497, bf16[512,1024]{1,0:T(8,128)(2,1)} %get-tuple-element.351), kind=kOutput, calls=%fused_computation.111 | convolution fusion | flops 268435456 | bytes 2359296 | tf_op jit(solution)/shard_map/while/body/eval_jaxpr/cond/branch_1_fun/cond/branch_1_fun/dot_general | solution.py:92
  119.9 2.2 %multiply_reduce_fusion.2 = (f32[256]{0:T(256)S(1)}, bf16[256,1024]{1,0:T(8,128)(2,1)S(1)}) fusion(f32[1024]{0:T(1024)S(1)} %bitcast.128, bf16[1024,1024]{1,0:T(8,128)(2,1)S(1)} %get-tuple-element.354, f32[256,1024]{1,0:T(8,128)} %fusion.42, bf16[128,1024]{1,0:T(8,128)(2,1)} %get-tuple-element.353, bf16[1,256,128]{2,1,0:T(8,128)(2,1)S(1)} %get-tuple-element.352), kind=kOutput, calls=%fused_computation.53 | convolution fusion | flops 605814528 | bytes 4002816 | tf_op jit(solution)/shard_map/while/body/eval_jaxpr/cond/branch_1_fun/cond/branch_1_fun/dot_general | solution.py:97
  122.2 0.7 gather_fusion.4
  122.9 1.3 fusion.37
  124.7 0.7 fusion.21
  125.4 0.6 gather_fusion.3
  126.1 0.7 compare_and_fusion.1
  126.9 0.6 broadcast_select_fusion
  127.5 1.9 %collective-permute-start = (bf16[1,256,128]{2,1,0:T(8,128)(2,1)}, bf16[1,256,128]{2,1,0:T(8,128)(2,1)S(1)}, u32[]{:S(2)}, u32[]{:S(2)}) collective-permute-start(bf16[1,256,128]{2,1,0:T(8,128)(2,1)} %get-tuple-element.615), channel_id=1, source_target_pairs={{0,128},{128,256},{256,384},{1,129},{129,257},{257,385},{2,130},{1... | collective-permute-start | bytes 196616 | tf_op jit(solution)/shard_map/while/body/eval_jaxpr/ppermute | solution.py:17
  129.4 1.9 %collective-permute-start.1 = (bf16[1,256]{1,0:T(2,128)(2,1)}, bf16[1,256]{1,0:T(2,128)(2,1)S(1)}, u32[]{:S(2)}, u32[]{:S(2)}) collective-permute-start(bf16[1,256]{1,0:T(2,128)(2,1)} %get-tuple-element.616), channel_id=1, source_target_pairs={{0,128},{128,256},{256,384},{1,129},{129,257},{257,385},{2,130},{1... | collective-permute-start | bytes 1544 | tf_op jit(solution)/shard_map/while/body/eval_jaxpr/ppermute | solution.py:17
  131.3 1.2 broadcast_select_fusion.8
  132.5 2.5 %collective-permute-done.1 = bf16[1,256]{1,0:T(2,128)(2,1)S(1)} collective-permute-done((bf16[1,256]{1,0:T(2,128)(2,1)}, bf16[1,256]{1,0:T(2,128)(2,1)S(1)}, u32[]{:S(2)}, u32[]{:S(2)}) %collective-permute-start.1) | collective-permute-done | bytes 544 | tf_op jit(solution)/shard_map/while/body/eval_jaxpr/ppermute | solution.py:17
  135.1 1.8 %conditional.6 = (bf16[1,256,128]{2,1,0:T(8,128)(2,1)}, bf16[1,256]{1,0:T(2,128)(2,1)}, f32[1,32]{1,0:T(1,128)}) conditional(s32[]{:T(128)} %convert_element_type.123, () %tuple.95, (s32[]{:T(128)}, s32[1,256]{1,0:T(1,128)S(1)}, bf16[1,1024,128]{2,1,0:T(8,128)(2,1)S(1)}, bf16[128,512]{1,0:T(8,128)(2,1)}, bf16[512,128]{1,0:T(8,128)(2,1)}, ...), branch_computations={%region_6.7_spmd, %region_7.16_spmd} | conditional | flops 874286208 | bytes 7426226 | solution.py:190
  135.1 0.6 broadcast.300
  136.9 3.1 %collective-permute-start = (bf16[1,256,128]{2,1,0:T(8,128)(2,1)}, bf16[1,256,128]{2,1,0:T(8,128)(2,1)S(1)}, u32[]{:S(2)}, u32[]{:S(2)}) collective-permute-start(bf16[1,256,128]{2,1,0:T(8,128)(2,1)} %get-tuple-element.615), channel_id=1, source_target_pairs={{0,128},{128,256},{256,384},{1,129},{129,257},{257,385},{2,130},{1... | collective-permute-start | bytes 196616 | tf_op jit(solution)/shard_map/while/body/eval_jaxpr/ppermute | solution.py:17
  140.0 1.9 %collective-permute-start.1 = (bf16[1,256]{1,0:T(2,128)(2,1)}, bf16[1,256]{1,0:T(2,128)(2,1)S(1)}, u32[]{:S(2)}, u32[]{:S(2)}) collective-permute-start(bf16[1,256]{1,0:T(2,128)(2,1)} %get-tuple-element.616), channel_id=1, source_target_pairs={{0,128},{128,256},{256,384},{1,129},{129,257},{257,385},{2,130},{1... | collective-permute-start | bytes 1544 | tf_op jit(solution)/shard_map/while/body/eval_jaxpr/ppermute | solution.py:17
  141.9 1.2 broadcast_select_fusion.8
  143.1 2.6 %collective-permute-done.1 = bf16[1,256]{1,0:T(2,128)(2,1)S(1)} collective-permute-done((bf16[1,256]{1,0:T(2,128)(2,1)}, bf16[1,256]{1,0:T(2,128)(2,1)S(1)}, u32[]{:S(2)}, u32[]{:S(2)}) %collective-permute-start.1) | collective-permute-done | bytes 544 | tf_op jit(solution)/shard_map/while/body/eval_jaxpr/ppermute | solution.py:17
  145.7 1.8 %conditional.6 = (bf16[1,256,128]{2,1,0:T(8,128)(2,1)}, bf16[1,256]{1,0:T(2,128)(2,1)}, f32[1,32]{1,0:T(1,128)}) conditional(s32[]{:T(128)} %convert_element_type.123, () %tuple.95, (s32[]{:T(128)}, s32[1,256]{1,0:T(1,128)S(1)}, bf16[1,1024,128]{2,1,0:T(8,128)(2,1)S(1)}, bf16[128,512]{1,0:T(8,128)(2,1)}, bf16[512,128]{1,0:T(8,128)(2,1)}, ...), branch_computations={%region_6.7_spmd, %region_7.16_spmd} | conditional | flops 874286208 | bytes 7426226 | solution.py:190
  145.7 0.6 broadcast.300
  147.5 1.9 %collective-permute-start = (bf16[1,256,128]{2,1,0:T(8,128)(2,1)}, bf16[1,256,128]{2,1,0:T(8,128)(2,1)S(1)}, u32[]{:S(2)}, u32[]{:S(2)}) collective-permute-start(bf16[1,256,128]{2,1,0:T(8,128)(2,1)} %get-tuple-element.615), channel_id=1, source_target_pairs={{0,128},{128,256},{256,384},{1,129},{129,257},{257,385},{2,130},{1... | collective-permute-start | bytes 196616 | tf_op jit(solution)/shard_map/while/body/eval_jaxpr/ppermute | solution.py:17
  149.4 3.1 %collective-permute-start.1 = (bf16[1,256]{1,0:T(2,128)(2,1)}, bf16[1,256]{1,0:T(2,128)(2,1)S(1)}, u32[]{:S(2)}, u32[]{:S(2)}) collective-permute-start(bf16[1,256]{1,0:T(2,128)(2,1)} %get-tuple-element.616), channel_id=1, source_target_pairs={{0,128},{128,256},{256,384},{1,129},{129,257},{257,385},{2,130},{1... | collective-permute-start | bytes 1544 | tf_op jit(solution)/shard_map/while/body/eval_jaxpr/ppermute | solution.py:17
  152.5 1.2 broadcast_select_fusion.8
  153.7 1.4 collective-permute-done.1
  (70 shorter events, 7.0 us)
Async XLA Ops:
  6.5 57.9 %copy-start = (bf16[1,2048,128]{2,1,0:T(8,128)(2,1)S(1)}, bf16[1,2048,128]{2,1,0:T(8,128)(2,1)}, u32[]{:S(2)}) copy-start(bf16[1,2048,128]{2,1,0:T(8,128)(2,1)} %param.26) | copy-start | bytes 1572868
  6.5 7.5 %copy-start.1 = (s32[1,1,1024,1]{2,3,1,0:T(1,128)S(1)}, s32[1,1,1024,1]{2,3,1,0:T(1,128)}, u32[]{:S(2)}) copy-start(s32[1,1,1024,1]{2,3,1,0:T(1,128)} %param.27) | copy-start | bytes 12292
  6.5 6.8 %sort.19.cloned.1.call-start = ((), (), s32[]{:S(2)}) async-start(), calls=%async_computation.2 | async-start | bytes 24608 | tf_op jit(solution)/shard_map/jit(argsort)/sort | solution.py:24
  14.1 4.6 %copy-start.2 = (s32[1,1,1024]{2,1,0:T(1,128)S(1)}, s32[1,1,1024]{2,1,0:T(1,128)}, u32[]{:S(2)}) copy-start(s32[1,1,1024]{2,1,0:T(1,128)} %param.28) | copy-start | bytes 12292
  18.6 4.5 %copy-start.7 = (s32[1,1024]{1,0:T(1,128)S(1)}, s32[1,1024]{1,0:T(1,128)}, u32[]{:S(2)}) copy-start(s32[1,1024]{1,0:T(1,128)} %get-tuple-element.406) | copy-start | bytes 12292
  23.2 6.6 %copy-start.9 = (s32[2]{0:T(128)S(1)}, s32[2]{0:T(128)}, u32[]{:S(2)}) copy-start(s32[2]{0:T(128)} %constant.215) | copy-start | bytes 28
  23.2 6.7 %copy-start.11 = (s32[2]{0:T(128)S(1)}, s32[2]{0:T(128)}, u32[]{:S(2)}) copy-start(s32[2]{0:T(128)} %constant.218) | copy-start | bytes 28
  35.1 29.0 %all-to-all-start = ((s32[1,128,16]{2,0,1:T(1,128)}), s32[1,128,16]{2,0,1:T(1,128)S(1)}, u32[]{:S(2)}, u32[]{:S(2)}) async-start(s32[1,128,16]{2,0,1:T(1,128)} %bitcast.48), calls=%async_computation | async-start | bytes 131072 | tf_op jit(solution)/shard_map/all_to_all | solution.py:43
  64.4 14.3 %copy-start.8 = (s32[2]{0:T(128)S(1)}, s32[2]{0:T(128)}, u32[]{:S(2)}) copy-start(s32[2]{0:T(128)} %constant.209) | copy-start | bytes 28
  64.4 14.4 %copy-start.10 = (s32[2]{0:T(128)S(1)}, s32[2]{0:T(128)}, u32[]{:S(2)}) copy-start(s32[2]{0:T(128)} %constant.212) | copy-start | bytes 28
  72.4 30.3 %copy-start.3 = (bf16[1,1024,1024]{2,1,0:T(8,128)(2,1)S(1)}, bf16[1,1024,1024]{2,1,0:T(8,128)(2,1)}, u32[]{:S(2)}) copy-start(bf16[1,1024,1024]{2,1,0:T(8,128)(2,1)} %param.31) | copy-start | bytes 6291460
  72.4 30.3 %copy-start.4 = (f32[1,1024]{1,0:T(1,128)S(1)}, f32[1,1024]{1,0:T(1,128)}, u32[]{:S(2)}) copy-start(f32[1,1024]{1,0:T(1,128)} %param.32) | copy-start | bytes 12292
  72.4 30.3 %copy-start.5 = (s32[1,256]{1,0:T(1,128)S(1)}, s32[1,256]{1,0:T(1,128)}, u32[]{:S(2)}) copy-start(s32[1,256]{1,0:T(1,128)} %param.29) | copy-start | bytes 3076
  72.4 30.3 %copy-start.6 = (bf16[1,1024]{1,0:T(2,128)(2,1)S(1)}, bf16[1,1024]{1,0:T(2,128)(2,1)}, u32[]{:S(2)}) copy-start(bf16[1,1024]{1,0:T(2,128)(2,1)} %param.25) | copy-start | bytes 6148
  72.4 26.8 %all-to-all-start.1 = ((bf16[1,128,16,128]{3,2,0,1:T(8,128)(2,1)}), bf16[1,128,16,128]{3,2,0,1:T(8,128)(2,1)S(1)}, u32[]{:S(2)}, u32[]{:S(2)}) async-start(bf16[1,128,16,128]{3,2,0,1:T(8,128)(2,1)} %bitcast.126), calls=%async_computation.1 | async-start | bytes 1048576 | tf_op jit(solution)/shard_map/all_to_all | solution.py:51
  104.6 11.9 %collective-permute-start = (bf16[1,256,128]{2,1,0:T(8,128)(2,1)}, bf16[1,256,128]{2,1,0:T(8,128)(2,1)S(1)}, u32[]{:S(2)}, u32[]{:S(2)}) collective-permute-start(bf16[1,256,128]{2,1,0:T(8,128)(2,1)} %get-tuple-element.615), channel_id=1, source_target_pairs={{0,128},{128,256},{256,384},{1,129},{129,257},{257,385},{2,130},{1... | collective-permute-start | bytes 196616 | tf_op jit(solution)/shard_map/while/body/eval_jaxpr/ppermute | solution.py:17
  108.0 8.5 %collective-permute-start.1 = (bf16[1,256]{1,0:T(2,128)(2,1)}, bf16[1,256]{1,0:T(2,128)(2,1)S(1)}, u32[]{:S(2)}, u32[]{:S(2)}) collective-permute-start(bf16[1,256]{1,0:T(2,128)(2,1)} %get-tuple-element.616), channel_id=1, source_target_pairs={{0,128},{128,256},{256,384},{1,129},{129,257},{257,385},{2,130},{1... | collective-permute-start | bytes 1544 | tf_op jit(solution)/shard_map/while/body/eval_jaxpr/ppermute | solution.py:17
  127.5 7.6 %collective-permute-start = (bf16[1,256,128]{2,1,0:T(8,128)(2,1)}, bf16[1,256,128]{2,1,0:T(8,128)(2,1)S(1)}, u32[]{:S(2)}, u32[]{:S(2)}) collective-permute-start(bf16[1,256,128]{2,1,0:T(8,128)(2,1)} %get-tuple-element.615), channel_id=1, source_target_pairs={{0,128},{128,256},{256,384},{1,129},{129,257},{257,385},{2,130},{1... | collective-permute-start | bytes 196616 | tf_op jit(solution)/shard_map/while/body/eval_jaxpr/ppermute | solution.py:17
  129.4 5.7 %collective-permute-start.1 = (bf16[1,256]{1,0:T(2,128)(2,1)}, bf16[1,256]{1,0:T(2,128)(2,1)S(1)}, u32[]{:S(2)}, u32[]{:S(2)}) collective-permute-start(bf16[1,256]{1,0:T(2,128)(2,1)} %get-tuple-element.616), channel_id=1, source_target_pairs={{0,128},{128,256},{256,384},{1,129},{129,257},{257,385},{2,130},{1... | collective-permute-start | bytes 1544 | tf_op jit(solution)/shard_map/while/body/eval_jaxpr/ppermute | solution.py:17
  136.9 8.8 %collective-permute-start = (bf16[1,256,128]{2,1,0:T(8,128)(2,1)}, bf16[1,256,128]{2,1,0:T(8,128)(2,1)S(1)}, u32[]{:S(2)}, u32[]{:S(2)}) collective-permute-start(bf16[1,256,128]{2,1,0:T(8,128)(2,1)} %get-tuple-element.615), channel_id=1, source_target_pairs={{0,128},{128,256},{256,384},{1,129},{129,257},{257,385},{2,130},{1... | collective-permute-start | bytes 196616 | tf_op jit(solution)/shard_map/while/body/eval_jaxpr/ppermute | solution.py:17
  140.0 5.7 %collective-permute-start.1 = (bf16[1,256]{1,0:T(2,128)(2,1)}, bf16[1,256]{1,0:T(2,128)(2,1)S(1)}, u32[]{:S(2)}, u32[]{:S(2)}) collective-permute-start(bf16[1,256]{1,0:T(2,128)(2,1)} %get-tuple-element.616), channel_id=1, source_target_pairs={{0,128},{128,256},{256,384},{1,129},{129,257},{257,385},{2,130},{1... | collective-permute-start | bytes 1544 | tf_op jit(solution)/shard_map/while/body/eval_jaxpr/ppermute | solution.py:17
  147.5 7.6 %collective-permute-start = (bf16[1,256,128]{2,1,0:T(8,128)(2,1)}, bf16[1,256,128]{2,1,0:T(8,128)(2,1)S(1)}, u32[]{:S(2)}, u32[]{:S(2)}) collective-permute-start(bf16[1,256,128]{2,1,0:T(8,128)(2,1)} %get-tuple-element.615), channel_id=1, source_target_pairs={{0,128},{128,256},{256,384},{1,129},{129,257},{257,385},{2,130},{1... | collective-permute-start | bytes 196616 | tf_op jit(solution)/shard_map/while/body/eval_jaxpr/ppermute | solution.py:17
  149.4 5.7 %collective-permute-start.1 = (bf16[1,256]{1,0:T(2,128)(2,1)}, bf16[1,256]{1,0:T(2,128)(2,1)S(1)}, u32[]{:S(2)}, u32[]{:S(2)}) collective-permute-start(bf16[1,256]{1,0:T(2,128)(2,1)} %get-tuple-element.616), channel_id=1, source_target_pairs={{0,128},{128,256},{256,384},{1,129},{129,257},{257,385},{2,130},{1... | collective-permute-start | bytes 1544 | tf_op jit(solution)/shard_map/while/body/eval_jaxpr/ppermute | solution.py:17
Sparse Core Ops, SparseCore 0:
  9.8 3.3 sort.21.cloned.1.call-done
  (1 shorter events, 0.0 us)
where the time goes:
time: 163 us; the launch traced here: 162 us
  local copies, waits for them, and re-layouts  49.7 us (30%)
  starting transfers between devices  44.5 us (27%)
  waiting for transfers between devices  38.2 us (23%)
  between operations  13.7 us (8%)
  other arithmetic  10.8 us (7%)
  matrix products  4.88 us (3%)
    ppermute x8, starting transfers between devices, shifted(): return lax.ppermute(array, axis, pairs)  20.4 us
    all_to_all x1, starting transfers between devices, fetch(): lax.all_to_all(request.reshape(user_count, shard_count, slot_count), 'sha...  17.8 us
    all_to_all x1, waiting for transfers between devices, fetch(): lax.all_to_all(served, 'shard', split_axis=1, concat_axis=1, tiled=True)  15.7 us
    ppermute x8, waiting for transfers between devices, shifted(): return lax.ppermute(array, axis, pairs)  11.3 us
    all_to_all x1, waiting for transfers between devices, fetch(): lax.all_to_all(request.reshape(user_count, shard_count, slot_count), 'sha...  11.2 us
    gather x1, local copies, waits for them, and re-layouts, fetch(): table_local[lax.all_to_all(request.reshape(user_count, shard_count, slot_...  7.98 us
    gather x1, local copies, waits for them, and re-layouts, fetch(): leading = jnp.take_along_axis(offsets, sorted_owner, axis=1)  6.57 us
    all_to_all x1, starting transfers between devices, fetch(): lax.all_to_all(served, 'shard', split_axis=1, concat_axis=1, tiled=True)  6.31 us
  transfers between devices with their start and end apart: 10, of which 6 were waited for; matrix products, arithmetic and copies ran while one was open for 5% of the time, Pallas kernels for 0%

commit v1 on v0

v1 whole, which is shorter than its diff:
```python
import math

import jax
import jax.numpy as jnp
from jax import lax
from jax.experimental import pallas as pl
from jax.experimental.pallas import tpu as pltpu
from jax.sharding import PartitionSpec as P

F32 = jnp.float32
BF16 = jnp.bfloat16
NT = (((1,), (1,)), ((), ()))


def call(kernel, out_shape, *operands, smem=0):
    specs = [pl.BlockSpec(memory_space=pltpu.SMEM)] * smem
    specs += [pl.BlockSpec(memory_space=pltpu.VMEM)] * (len(operands) - smem)
    return pl.pallas_call(kernel, out_shape=out_shape, in_specs=specs)(*operands)


def iota(shape, axis):
    return lax.broadcasted_iota(jnp.int32, shape, axis)


def ones_where(mask):
    return jnp.where(mask, 1.0, 0.0).astype(BF16)


def dot(a, b):
    return jnp.dot(a, b, preferred_element_type=F32)


def dot_nt(a, b):
    return lax.dot_general(a, b, NT, preferred_element_type=F32)


def column(row):
    return jnp.broadcast_to(row, (128, 128)).T


def request_kernel(owner_ref, row_ref, req_ref, slot_ref):
    shards, slots = req_ref.shape
    cands = owner_ref.shape[1]
    owner = owner_ref[...]
    hits = owner == iota((shards, cands), 0)
    hot = ones_where(hits)
    earlier = ones_where((iota((128, 256), 0) < iota((128, 256), 1)) | (iota((128, 256), 1) >= 128))
    seen = jnp.zeros((shards, 128), F32)
    ranks = []
    for b in range(cands // 128):
        part = slice(b * 128, b * 128 + 128)
        counts = dot(hot[:, part], earlier)
        ranks.append(jnp.sum(jnp.where(hits[:, part], counts[:, :128] + seen, 0.0), axis=0, keepdims=True))
        seen = seen + counts[:, 128:]
    rank = jnp.concatenate(ranks, axis=1).astype(jnp.int32)
    slot_ref[...] = owner * slots + rank
    row = row_ref[...]
    at_slot = rank == iota((slots, cands), 0)
    high = jnp.where(at_slot, (row >> 4).astype(F32), 0.0).astype(BF16)
    low = jnp.where(at_slot, (row & 15).astype(F32), 0.0).astype(BF16)
    req_ref[...] = (dot_nt(hot, high) * 16.0 + dot_nt(hot, low)).astype(jnp.int32)


def serve_kernel(ids_ref, table_ref, out_ref):
    blocks = ids_ref.shape[0]
    rows = table_ref.shape[0]
    step = 4
    ids = ids_ref[...].astype(F32)
    lanes = iota((128, 128), 1).astype(F32)
    table = table_ref[...]
    for first in range(0, blocks, step):
        tall = []
        for b in range(first, first + step):
            col = column(ids[b:b + 1, :])
            tall.append(jnp.concatenate(
                [ones_where(col - 128.0 * r == lanes) for r in range(rows // 128)], axis=1))
        hot = jnp.concatenate(tall, axis=0)
        out_ref[first * 128:(first + step) * 128, :] = dot(hot, table).astype(BF16)


def prepare_kernel(sec_ref, slot_ref, first_ref, second_ref, dense_ref, weight_ref, head_ref, proj_ref,
                   pick_ref, vec_ref):
    sec = sec_ref[0]
    slot = slot_ref[...].astype(F32)
    cands = slot.shape[1]
    spots = pick_ref.shape[1]
    final = second_ref.shape[1]

    def second_column():
        wide = jnp.concatenate([second_ref[...].astype(F32), jnp.zeros((1, 128 - final), F32)], axis=1)
        return column(wide)[:final, :1]

    def lookup(at, row):
        lanes = iota((at.shape[0], row.shape[1]), 1).astype(F32)
        return jnp.sum(jnp.where(lanes == at, row, 0.0), axis=1, keepdims=True)

    @pl.when(sec == 0)
    def _():
        at = lookup(second_column(), first_ref[...].astype(F32))
        where = lookup(at, slot)
        pick_ref[:final, :] = ones_where(iota((final, spots), 1).astype(F32) == where)
        active = jax.nn.relu(dot(dense_ref[...], weight_ref[...]))
        query = (active * head_ref[...]).astype(BF16)
        vec_ref[...] = dot(query, proj_ref[...])

    @pl.when(sec == 1)
    def _():
        at = second_column() * 4.0
        where = jnp.concatenate([lookup(at + float(f), slot) for f in range(4)], axis=0)
        pick_ref[:4 * final, :] = ones_where(iota((4 * final, spots), 1).astype(F32) == where)

    @pl.when(sec >= 2)
    def _():
        lanes = iota((128, 128), 1).astype(F32)
        for b in range(cands // 128):
            col = column(slot[:, b * 128:b * 128 + 128])
            for s in range(spots // 128):
                pick_ref[b * 128:b * 128 + 128, s * 128:s * 128 + 128] = ones_where(col - 128.0 * s == lanes)


def as_row(col, lanes):
    n = col.shape[0]
    return jnp.sum(jnp.where(iota((n, lanes), 0) == iota((n, lanes), 1), col, 0.0), axis=0, keepdims=True)


def tower_kernel(sec_ref, pick_ref, rows_ref, vec_ref, in_ref, out_ref, packet_ref, score_ref):
    @pl.when(sec_ref[0] == 0)
    def _():
        n = packet_ref.shape[0] // 2
        embed = dot(pick_ref[:n, :], rows_ref[...]).astype(BF16)
        hidden = jax.nn.relu(dot(embed, in_ref[...])).astype(BF16)
        tower = dot(hidden, out_ref[...]).astype(BF16)
        logit = jnp.sum(tower.astype(F32) * vec_ref[...], axis=1, keepdims=True)
        packet_ref[:n, :] = tower
        packet_ref[n:, :] = jnp.broadcast_to(logit, (n, 128)).astype(BF16)
        score_ref[...] = as_row(logit, 128)


def features_kernel(sec_ref, pick_ref, rows_ref, feat_ref, weight_ref, part_ref):
    sec = sec_ref[0]
    n = part_ref.shape[0]
    width = rows_ref.shape[1]

    @pl.when(sec == 1)
    def _():
        embed = dot(pick_ref[:4 * n, :], rows_ref[...]).astype(BF16)
        wide = jnp.concatenate([embed[f * n:(f + 1) * n, :] for f in range(4)], axis=1)
        part_ref[...] = dot(wide, feat_ref[...])

    @pl.when(sec >= 2)
    def _():
        embed = dot(pick_ref[...], rows_ref[...]).astype(BF16)
        r, c = iota((128, 128), 0), iota((128, 128), 1)
        same_item = (r // 32) == (c // 32)
        spread = ones_where((r % 32) == (c % 32))
        own_lanes = (r % 4) == (c // 32)
        grams = []
        for b in range(embed.shape[0] // 128):
            block = embed[b * 128:b * 128 + 128, :]
            gram = dot_nt(block, block) * (1.0 / math.sqrt(width))
            gram = jnp.where(same_item, gram, 0.0).astype(BF16)
            grams.append(jnp.where(own_lanes, dot(gram, spread), 0.0).astype(BF16))
        tall = jnp.concatenate(grams, axis=0)
        i, k = iota((8 * n, 32 * n), 0), iota((8 * n, 32 * n), 1)
        choose = ones_where(((k // 32) == (i % n)) & (((k % 32) // 4) == (i // n)))
        flat = dot(choose, tall).astype(BF16)
        flat = jnp.concatenate([flat[q * n:(q + 1) * n, :] for q in range(8)], axis=1)
        part_ref[...] = dot(flat, weight_ref[...])


def prerank_kernel(sec_ref, packet_ref, part_ref, item_ref, weight_ref, head_ref, carry_ref, score_ref):
    @pl.when(sec_ref[0] == 1)
    def _():
        n, hid = part_ref.shape
        pre = part_ref[...] + dot(packet_ref[:n, :], item_ref[...])
        inner = jax.nn.relu(pre).astype(BF16)
        hidden = jax.nn.relu(dot(inner, weight_ref[...]))
        prior = packet_ref[n:, :].astype(F32)[:, :1]
        logit = jnp.sum(hidden * head_ref[...], axis=1, keepdims=True) / math.sqrt(hid) + prior
        carry_ref[:, :hid] = hidden.astype(BF16)
        carry_ref[:, hid:] = jnp.broadcast_to(logit, (n, 128)).astype(BF16)
        score_ref[...] = as_row(logit, 128)


def final_kernel(sec_ref, near_ref, far_ref, part_ref, before_ref, head_ref, head_before_ref,
                 score0_ref, score1_ref, score_ref):
    sec = sec_ref[0]
    n, hid = part_ref.shape
    scale = 1.0 / math.sqrt(hid)

    def rank(part, carry, prior, head):
        hidden = jax.nn.relu(part + carry)
        return hidden, jnp.sum(hidden * head, axis=1, keepdims=True) * scale + prior

    @pl.when(sec == 0)
    def _():
        score_ref[...] = score0_ref[...]

    @pl.when(sec == 1)
    def _():
        score_ref[...] = score1_ref[...]

    @pl.when(sec == 2)
    def _():
        near = near_ref[...].astype(F32)
        _, logit = rank(part_ref[...], near[:, :hid], near[:, hid:hid + 1], head_ref[...])
        score_ref[...] = as_row(logit, 128)

    @pl.when(sec == 3)
    def _():
        far = far_ref[...].astype(F32)
        hidden, logit = rank(before_ref[...], far[:, :hid], far[:, hid:hid + 1], head_before_ref[...])
        prior = logit.astype(BF16).astype(F32)
        _, logit = rank(part_ref[...], hidden.astype(BF16).astype(F32), prior, head_ref[...])
        score_ref[...] = as_row(logit, 128)


def per_device(
    user_dense,
    tables,
    feat_owner,
    feat_row,
    keep_first,
    keep_second,
    section_weight,
    section_head,
    user_proj,
    item_in,
    item_out,
    prerank_feat,
    prerank_item,
):
    shape = jax.ShapeDtypeStruct
    shards = lax.axis_size("shard")
    cands = feat_row.shape[2]
    slots = 2 * cands // shards
    spots = shards * slots
    width = tables.shape[2]
    hid = section_weight.shape[1]
    final = keep_second.shape[1]
    sec = lax.axis_index("section").reshape(1).astype(jnp.int32)
    weight = section_weight[0]

    head_before = lax.ppermute(section_head, "section", [(2, 3)])

    request, slot = call(
        request_kernel,
        (shape((shards, slots), jnp.int32), shape((1, cands), jnp.int32)),
        feat_owner.reshape(1, cands),
        feat_row.reshape(1, cands),
    )
    asked = lax.all_to_all(request, "shard", 0, 0, tiled=True)
    pick, user_vec = call(
        prepare_kernel,
        (shape((cands, spots), BF16), shape((1, width), F32)),
        sec, slot, keep_first, keep_second, user_dense, weight, section_head, user_proj,
        smem=1,
    )
    served = call(
        serve_kernel,
        shape((spots, width), BF16),
        asked.reshape(spots // 128, 128),
        tables[0],
    )
    rows = lax.all_to_all(served.reshape(shards, slots, width), "shard", 0, 0, tiled=True)
    rows = rows.reshape(spots, width)
    packet, score0 = call(
        tower_kernel,
        (shape((2 * final, width), BF16), shape((1, 128), F32)),
        sec, pick, rows, user_vec, item_in, item_out,
        smem=1,
    )
    packet = lax.ppermute(packet, "section", [(0, 1)])
    part = call(
        features_kernel,
        shape((final, hid), F32),
        sec, pick, rows, prerank_feat, weight,
        smem=1,
    )
    before = lax.ppermute(part, "section", [(2, 3)])
    carry, score1 = call(
        prerank_kernel,
        (shape((final, hid + 128), BF16), shape((1, 128), F32)),
        sec, packet, part, prerank_item, weight, section_head,
        smem=1,
    )
    near = lax.ppermute(carry, "section", [(1, 2)])
    far = lax.ppermute(carry, "section", [(1, 3)])
    scores = call(
        final_kernel,
        shape((1, 128), F32),
        sec, near, far, part, before, section_head, head_before, score0, score1,
        smem=1,
    )
    return scores[None, :, :final]


def solution(mesh):
    placed = (
        P("shard", None),
        P("section", "shard", None),
        P("section", "shard", None, None),
        P("section", "shard", None),
        P("shard", None),
        P("shard", None),
        P("section", None, None),
        P("section", None),
        P(),
        P(),
        P(),
        P(),
        P(),
    )
    return jax.shard_map(
        per_device,
        mesh=mesh,
        in_specs=placed,
        out_specs=P("section", "shard", None),
        check_vma=False,
    )
```

time: 163 us -> 93.3 us (0.57)
  the two profiles are of different devices: /device:TPU:2 before, /device:TPU:4 now
where the time goes in v1:
time: 93.3 us; the launch traced here: 92.8 us
  blocking collectives  29 us (31%)
  Pallas kernels  25.7 us (28%)
  waiting for transfers between devices  19.5 us (21%)
  starting transfers between devices  13.3 us (14%)
  local copies, waits for them, and re-layouts  4.38 us (5%)
    all_to_all x1, blocking collectives, per_device(): asked = lax.all_to_all(request, 'shard', 0, 0, tiled=True)  29 us
    pallas_call x7, Pallas kernels, call(): pl.pallas_call(kernel, out_shape=out_shape, in_specs=specs)(*operands)  25.7 us
    all_to_all x1, waiting for transfers between devices, per_device(): lax.all_to_all(served.reshape(shards, slots, width), 'shard', 0, 0, tiled...  15.7 us
    all_to_all x1, starting transfers between devices, per_device(): lax.all_to_all(served.reshape(shards, slots, width), 'shard', 0, 0, tiled...  6.16 us
    ppermute x1, starting transfers between devices, per_device(): before = lax.ppermute(part, 'section', [(2, 3)])  3.22 us
    ppermute x1, waiting for transfers between devices, per_device(): near = lax.ppermute(carry, 'section', [(1, 2)])  2.53 us
    unnamed x14, local copies, waits for them, and re-layouts  2.06 us
  transfers between devices with their start and end apart: 6, of which 3 were waited for; matrix products, arithmetic and copies ran while one was open for 0% of the time, Pallas kernels for 11%

profile of v1, /device:TPU:4, one launch (start us, length us, event | category | flops | bytes accessed | tf_op | source)
XLA Modules:
  0.0 92.8 jit_solution(5091392667647107912)
XLA Ops:
  0.0 1.8 %shard_map.127 = (s32[128,16]{1,0:T(8,128)}, s32[1,1024]{1,0:T(1,128)}) custom-call(s32[1,1024]{1,0:T(1,128)} %bitcast.20, s32[1,1024]{1,0:T(1,128)} %bitcast.21), custom_call_target="tpu_custom_call" | custom-call | tf_op jit(solution)/shard_map/pallas_call | solution.py:18
  1.8 29.0 %all_to_all.14 = s32[128,1,16]{2,1,0:T(1,128)S(1)} all-to-all(s32[128,1,16]{2,1,0:T(1,128)} %bitcast.19), channel_id=1, replica_groups=mesh['section'=4,'shard'=128] {'shard'}, dimensions={0} | all-to-all | bytes 16384 | tf_op jit(solution)/shard_map/all_to_all | solution.py:252
  30.9 0.5 broadcast.3
  31.4 0.8 reduce.3
  32.2 0.7 reshape.24.ids_ref
  32.9 4.2 %shard_map.129 = bf16[2048,128]{1,0:T(8,128)(2,1)} custom-call(s32[16,128]{1,0:T(8,128)} %reshape.24.ids_ref, bf16[2048,128]{1,0:T(8,128)(2,1)} %bitcast.18), custom_call_target="tpu_custom_call" | custom-call | tf_op jit(solution)/shard_map/pallas_call | solution.py:18
  37.1 6.2 %all-to-all-start.1 = ((bf16[128,16,128]{2,1,0:T(8,128)(2,1)}), bf16[128,16,128]{2,1,0:T(8,128)(2,1)S(1)}, u32[]{:S(2)}, u32[]{:S(2)}) async-start(bf16[128,16,128]{2,1,0:T(8,128)(2,1)} %bitcast.17), calls=%async_computation.1 | async-start | bytes 1048576 | tf_op jit(solution)/shard_map/all_to_all | solution.py:265
  43.3 4.8 %shard_map.128 = (bf16[1024,2048]{1,0:T(8,128)(2,1)}, f32[1,128]{1,0:T(1,128)}) custom-call(s32[1]{0:T(128)} %bitcast.sec_ref, s32[1,1024]{1,0:T(1,128)} %get-tuple-element.13.slot_ref, s32[1,256]{1,0:T(1,128)} %first_ref.1, s32[1,32]{1,0:T(1,128)} %second_ref.1, bf16[1,1024]{1,0:T(2,128)(2,1)} %dense_ref.1, bf16[1024,1024]{1,0:T(8,128)(2,1)} %bitcast.12, ...), custom_call_target="tpu_custom_call" | custom-call | tf_op jit(solution)/shard_map/pallas_call | solution.py:18
  48.1 15.7 %all-to-all-done.1 = bf16[128,16,128]{2,1,0:T(8,128)(2,1)S(1)} async-done(((bf16[128,16,128]{2,1,0:T(8,128)(2,1)}), bf16[128,16,128]{2,1,0:T(8,128)(2,1)S(1)}, u32[]{:S(2)}, u32[]{:S(2)}) %all-to-all-start.1) | async-done | bytes 524320 | tf_op jit(solution)/shard_map/all_to_all | solution.py:265
  63.7 0.0 copy-start
  63.8 0.8 copy-done
  64.5 7.7 %shard_map.131.part_ref = f32[32,1024]{1,0:T(8,128)} custom-call(s32[1]{0:T(128)} %bitcast.sec_ref, bf16[1024,2048]{1,0:T(8,128)(2,1)} %get-tuple-element.14.pick_ref, bf16[2048,128]{1,0:T(8,128)(2,1)} %bitcast.15, bf16[512,1024]{1,0:T(8,128)(2,1)} %feat_ref.1, bf16[1024,1024]{1,0:T(8,128)(2,1)} %bitcast.13), custom_call_target="tpu_custom_call" | custom-call | tf_op jit(solution)/shard_map/pallas_call | solution.py:18
  72.3 0.0 copy-start.4
  72.3 3.2 %collective-permute-start.3 = (f32[32,1024]{1,0:T(8,128)}, f32[32,1024]{1,0:T(8,128)S(1)}, u32[]{:S(2)}, u32[]{:S(2)}) collective-permute-start(f32[32,1024]{1,0:T(8,128)} %shard_map.131.part_ref), channel_id=1, source_target_pairs={{256,384},{257,385},{258,386},{259,387},{260,388},{261,389},{262,3... | collective-permute-start | bytes 393224 | tf_op jit(solution)/shard_map/ppermute | solution.py:280
  75.5 3.0 %shard_map.130 = (bf16[64,128]{1,0:T(8,128)(2,1)}, f32[1,128]{1,0:T(1,128)}) custom-call(s32[1]{0:T(128)} %bitcast.sec_ref, bf16[1024,2048]{1,0:T(8,128)(2,1)} %get-tuple-element.14.pick_ref, bf16[2048,128]{1,0:T(8,128)(2,1)} %bitcast.16, f32[1,128]{1,0:T(1,128)} %get-tuple-element.16.vec_ref, bf16[128,512]{1,0:T(8,128)(2,1)} %in_ref.1, bf16[512,128]{1,0:T(8,128)(2,1)} %out_ref.1), custom_call_target="tpu_custom_call" | custom-call | tf_op jit(solution)/shard_map/pallas_call | solution.py:18
  78.5 0.7 collective-permute-start
  79.2 0.0 collective-permute-done.packet_ref
  79.2 0.0 copy-start.5
  79.2 0.6 copy-done.5
  79.8 2.3 %shard_map.132 = (bf16[32,1152]{1,0:T(8,128)(2,1)}, f32[1,128]{1,0:T(1,128)}) custom-call(s32[1]{0:T(128)} %bitcast.sec_ref, bf16[64,128]{1,0:T(8,128)(2,1)} %copy-done.5, f32[32,1024]{1,0:T(8,128)} %shard_map.131.part_ref, bf16[128,1024]{1,0:T(8,128)(2,1)} %item_ref.1, bf16[1024,1024]{1,0:T(8,128)(2,1)} %bitcast.14, f32[1,1024]{1,0:T(1,128)} %head_ref.5), custom_call_target="tpu_custom_call" | custom-call | tf_op jit(solution)/shard_map/pallas_call | solution.py:18
  82.1 0.7 collective-permute-start.2
  82.8 1.3 %collective-permute-start.1 = (bf16[32,1152]{1,0:T(8,128)(2,1)}, bf16[32,1152]{1,0:T(8,128)(2,1)S(1)}, u32[]{:S(2)}, u32[]{:S(2)}) collective-permute-start(bf16[32,1152]{1,0:T(8,128)(2,1)} %get-tuple-element.18), channel_id=1, source_target_pairs={{128,256},{129,257},{130,258},{131,259},{132,260},{133,261},{134,2... | collective-permute-start | bytes 221192 | tf_op jit(solution)/shard_map/ppermute | solution.py:287
  84.1 0.0 copy-done.4
  84.1 1.3 %collective-permute-start.4 = (f32[1,1024]{1,0:T(1,128)S(1)}, f32[1,1024]{1,0:T(1,128)S(1)}, u32[]{:S(2)}, u32[]{:S(2)}) collective-permute-start(f32[1,1024]{1,0:T(1,128)S(1)} %copy-done.4), channel_id=1, source_target_pairs={{256,384},{257,385},{258,386},{259,387},{260,388},{261,389},{262,3... | collective-permute-start | bytes 12296 | tf_op jit(solution)/shard_map/ppermute | solution.py:244
  85.4 1.3 %collective-permute-done.4.head_before_ref = f32[1,1024]{1,0:T(1,128)S(1)} collective-permute-done((f32[1,1024]{1,0:T(1,128)S(1)}, f32[1,1024]{1,0:T(1,128)S(1)}, u32[]{:S(2)}, u32[]{:S(2)}) %collective-permute-start.4) | collective-permute-done | bytes 4128 | tf_op jit(solution)/shard_map/ppermute | solution.py:244
  86.7 0.0 copy-start.6
  86.7 0.0 collective-permute-done.2.far_ref
  86.7 0.0 copy-start.2
  86.7 2.5 %collective-permute-done.1.near_ref = bf16[32,1152]{1,0:T(8,128)(2,1)S(1)} collective-permute-done((bf16[32,1152]{1,0:T(8,128)(2,1)}, bf16[32,1152]{1,0:T(8,128)(2,1)S(1)}, u32[]{:S(2)}, u32[]{:S(2)}) %collective-permute-start.1) | collective-permute-done | bytes 73760 | tf_op jit(solution)/shard_map/ppermute | solution.py:287
  89.2 0.0 copy-start.3
  89.2 0.0 collective-permute-done.3.before_ref
  89.2 0.0 copy-start.1
  89.2 0.0 copy-done.6
  89.2 0.0 copy-done.2
  89.2 0.6 copy-done.3
  89.8 0.1 copy-done.1
  89.9 1.8 %shard_map.133 = f32[1,128]{1,0:T(1,128)} custom-call(s32[1]{0:T(128)} %bitcast.sec_ref, bf16[32,1152]{1,0:T(8,128)(2,1)} %copy-done.3, bf16[32,1152]{1,0:T(8,128)(2,1)} %copy-done.2, f32[32,1024]{1,0:T(8,128)} %shard_map.131.part_ref, f32[32,1024]{1,0:T(8,128)} %copy-done.1, f32[1,1024]{1,0:T(1,128)} %head_ref.5, f32[1,1024]{1,0:T(1,128)} %copy-done.6, ...), custom_call_target="tpu_custom_call" | custom-call | tf_op jit(solution)/shard_map/pallas_call | solution.py:18
  91.7 1.1 %slice_bitcast_fusion = f32[1,1,32]{2,1,0:T(1,128)} fusion(f32[1,128]{1,0:T(1,128)} %shard_map.133), kind=kLoop, calls=%fused_computation | loop fusion | bytes 256 | tf_op jit(solution)/shard_map/broadcast_in_dim | solution.py:295
Async XLA Ops:
  37.1 26.7 %all-to-all-start.1 = ((bf16[128,16,128]{2,1,0:T(8,128)(2,1)}), bf16[128,16,128]{2,1,0:T(8,128)(2,1)S(1)}, u32[]{:S(2)}, u32[]{:S(2)}) async-start(bf16[128,16,128]{2,1,0:T(8,128)(2,1)} %bitcast.17), calls=%async_computation.1 | async-start | bytes 1048576 | tf_op jit(solution)/shard_map/all_to_all | solution.py:265
  63.7 0.8 copy-start
  72.3 11.8 %copy-start.4 = (f32[1,1024]{1,0:T(1,128)S(1)}, f32[1,1024]{1,0:T(1,128)}, u32[]{:S(2)}) copy-start(f32[1,1024]{1,0:T(1,128)} %head_ref.5) | copy-start | bytes 12292
  72.3 16.9 %collective-permute-start.3 = (f32[32,1024]{1,0:T(8,128)}, f32[32,1024]{1,0:T(8,128)S(1)}, u32[]{:S(2)}, u32[]{:S(2)}) collective-permute-start(f32[32,1024]{1,0:T(8,128)} %shard_map.131.part_ref), channel_id=1, source_target_pairs={{256,384},{257,385},{258,386},{259,387},{260,388},{261,389},{262,3... | collective-permute-start | bytes 393224 | tf_op jit(solution)/shard_map/ppermute | solution.py:280
  78.5 0.7 collective-permute-start
  79.2 0.6 copy-start.5
  82.1 4.6 %collective-permute-start.2 = (bf16[32,1152]{1,0:T(8,128)(2,1)}, bf16[32,1152]{1,0:T(8,128)(2,1)S(1)}, u32[]{:S(2)}, u32[]{:S(2)}) collective-permute-start(bf16[32,1152]{1,0:T(8,128)(2,1)} %get-tuple-element.18), channel_id=1, source_target_pairs={{128,384},{129,385},{130,386},{131,387},{132,388},{133,389},{134,3... | collective-permute-start | bytes 221192 | tf_op jit(solution)/shard_map/ppermute | solution.py:288
  82.8 6.5 %collective-permute-start.1 = (bf16[32,1152]{1,0:T(8,128)(2,1)}, bf16[32,1152]{1,0:T(8,128)(2,1)S(1)}, u32[]{:S(2)}, u32[]{:S(2)}) collective-permute-start(bf16[32,1152]{1,0:T(8,128)(2,1)} %get-tuple-element.18), channel_id=1, source_target_pairs={{128,256},{129,257},{130,258},{131,259},{132,260},{133,261},{134,2... | collective-permute-start | bytes 221192 | tf_op jit(solution)/shard_map/ppermute | solution.py:287
  84.1 2.6 %collective-permute-start.4 = (f32[1,1024]{1,0:T(1,128)S(1)}, f32[1,1024]{1,0:T(1,128)S(1)}, u32[]{:S(2)}, u32[]{:S(2)}) collective-permute-start(f32[1,1024]{1,0:T(1,128)S(1)} %copy-done.4), channel_id=1, source_target_pairs={{256,384},{257,385},{258,386},{259,387},{260,388},{261,389},{262,3... | collective-permute-start | bytes 12296 | tf_op jit(solution)/shard_map/ppermute | solution.py:244
  86.7 2.5 %copy-start.6 = (f32[1,1024]{1,0:T(1,128)}, f32[1,1024]{1,0:T(1,128)S(1)}, u32[]{:S(2)}) copy-start(f32[1,1024]{1,0:T(1,128)S(1)} %collective-permute-done.4.head_before_ref) | copy-start | bytes 12292
  86.7 2.5 %copy-start.2 = (bf16[32,1152]{1,0:T(8,128)(2,1)}, bf16[32,1152]{1,0:T(8,128)(2,1)S(1)}, u32[]{:S(2)}) copy-start(bf16[32,1152]{1,0:T(8,128)(2,1)S(1)} %collective-permute-done.2.far_ref) | copy-start | bytes 221188
  89.2 0.6 copy-start.3
  89.2 0.7 copy-start.1

commit v2 on v1

v2 whole, which is shorter than its diff:
```python
import math

import jax
import jax.numpy as jnp
from jax import lax
from jax.experimental import pallas as pl
from jax.experimental.pallas import tpu as pltpu
from jax.sharding import PartitionSpec as P


F32 = jnp.float32
BF16 = jnp.bfloat16
NT = (((1,), (1,)), ((), ()))


def call(kernel, out_shape, *operands, smem=0, hbm=0, sems=0, flops=0, scratch=()):
    specs = [pl.BlockSpec(memory_space=pltpu.SMEM)] * smem
    specs += [pl.BlockSpec(memory_space=pltpu.HBM)] * hbm
    specs += [pl.BlockSpec(memory_space=pltpu.VMEM)] * (len(operands) - smem - hbm)
    return pl.pallas_call(
        kernel,
        out_shape=out_shape,
        in_specs=specs,
        scratch_shapes=[*scratch, *([pltpu.SemaphoreType.DMA((sems,))] if sems else [])],
        cost_estimate=pl.CostEstimate(flops=flops, transcendentals=0, bytes_accessed=0),
        compiler_params=pltpu.CompilerParams(vmem_limit_bytes=20 << 20),
    )(*operands)


def copies(sources, targets, sem):
    return [pltpu.make_async_copy(a, b, sem.at[i]) for i, (a, b) in enumerate(zip(sources, targets))]


def in_hbm(*arrays):
    return [pltpu.with_memory_space_constraint(a, pltpu.HBM) for a in arrays]


def iota(shape, axis):
    return lax.broadcasted_iota(jnp.int32, shape, axis)


def ones_where(mask):
    return jnp.where(mask, 1.0, 0.0).astype(BF16)


def dot(a, b):
    return jnp.dot(a, b, preferred_element_type=F32)


def dot_nt(a, b):
    return lax.dot_general(a, b, NT, preferred_element_type=F32)


def column(row):
    return jnp.broadcast_to(row, (128, 128)).T


def request_kernel(user_ref, owner_hbm, row_hbm, table_hbm, req_ref, slot_ref, table_ref, owner_ref, row_ref, sem):
    moves = copies((owner_hbm, row_hbm, table_hbm), (owner_ref, row_ref, table_ref), sem)
    for move in moves:
        move.start()
    shards = req_ref.shape[0]
    cands = owner_ref.shape[1]
    slots = 2 * cands // shards
    earlier = ones_where((iota((128, 256), 0) < iota((128, 256), 1)) | (iota((128, 256), 1) >= 128))
    seen = jnp.zeros((shards, 128), F32)
    ranks = []
    moves[0].wait()
    owner = owner_ref[...]
    hits = owner == iota((shards, cands), 0)
    hot = ones_where(hits)
    for b in range(cands // 128):
        part = slice(b * 128, b * 128 + 128)
        counts = dot(hot[:, part], earlier)
        ranks.append(jnp.sum(jnp.where(hits[:, part], counts[:, :128] + seen, 0.0), axis=0, keepdims=True))
        seen = seen + counts[:, 128:]
    rank = jnp.concatenate(ranks, axis=1).astype(jnp.int32)
    slot_ref[...] = owner * slots + rank
    moves[1].wait()
    row = row_ref[...]
    at_slot = rank + (user_ref[0] % (128 // slots)) * slots == iota((128, cands), 0)
    high = jnp.where(at_slot, (row >> 4).astype(F32), 0.0).astype(BF16)
    low = jnp.where(at_slot, (row & 15).astype(F32), 0.0).astype(BF16)
    req_ref[...] = (dot_nt(hot, high) * 16.0 + dot_nt(hot, low)).astype(jnp.int32)
    moves[2].wait()


def serve_kernel(ids_ref, table_ref, out_ref):
    users = ids_ref.shape[0]
    slots = 2048 // users
    group = 128 // slots
    rows = table_ref.shape[0]
    step = 4
    lanes = iota((128, 128), 1)
    table = table_ref[...]
    for first in range(0, users // group, step):
        tall = []
        for b in range(first, first + step):
            ids = jnp.sum(ids_ref[b * group:(b + 1) * group, :], axis=0, keepdims=True)
            col = column(ids)
            fine = ones_where((col & 127) == lanes)
            coarse = (col >> 7).astype(F32).astype(BF16)
            tall.append(jnp.concatenate(
                [jnp.where(coarse == float(r), fine, jnp.zeros_like(fine)) for r in range(rows // 128)], axis=1))
        hot = jnp.concatenate(tall, axis=0)
        out_ref[first * 128:(first + step) * 128, :] = dot(hot, table).astype(BF16)


def prepare_kernel(sec_ref, in_hbm, out_hbm, weight_hbm, head_hbm,
                   slot_ref, first_ref, second_ref, dense_ref, proj_ref,
                   spot_ref, vec_ref, in_ref, out_ref, weight_ref, head_ref, sem):
    moves = copies((in_hbm, out_hbm, weight_hbm, head_hbm),
                   (in_ref, out_ref, weight_ref, head_ref), sem)
    for move in moves:
        move.start()
    sec = sec_ref[0]
    slot = slot_ref[...].astype(F32)
    final = second_ref.shape[1]

    def second_column():
        wide = jnp.concatenate([second_ref[...].astype(F32), jnp.zeros((1, 128 - final), F32)], axis=1)
        return column(wide)[:final, :1]

    def lookup(at, row):
        lanes = iota((at.shape[0], row.shape[1]), 1).astype(F32)
        return jnp.sum(jnp.where(lanes == at, row, 0.0), axis=1, keepdims=True)

    @pl.when(sec == 0)
    def _():
        at = lookup(second_column(), first_ref[...].astype(F32))
        spot_ref[:final, :] = jnp.broadcast_to(lookup(at, slot), (final, 128))

    @pl.when(sec == 1)
    def _():
        at = second_column() * 4.0
        for f in range(4):
            spot_ref[f * final:f * final + final, :] = jnp.broadcast_to(lookup(at + float(f), slot), (final, 128))

    for move in moves:
        move.wait()

    @pl.when(sec == 0)
    def _():
        active = jax.nn.relu(dot(dense_ref[...], weight_ref[...]))
        query = (active * head_ref[...]).astype(BF16)
        vec_ref[...] = dot(query, proj_ref[...])


def picked(col, rows):
    col = col.astype(jnp.int32)
    fine = ones_where((col & 127) == iota(col.shape, 1))
    coarse = (col >> 7).astype(F32).astype(BF16)
    hot = [jnp.where(coarse == float(r), fine, jnp.zeros_like(fine)) for r in range(rows.shape[0] // 128)]
    return dot(jnp.concatenate(hot, axis=1), rows).astype(BF16)


def as_row(col, lanes):
    n = col.shape[0]
    return jnp.sum(jnp.where(iota((n, lanes), 0) == iota((n, lanes), 1), col, 0.0), axis=0, keepdims=True)


def tower_kernel(sec_ref, spot_ref, rows_ref, vec_ref, in_ref, out_ref, packet_ref, score_ref):
    @pl.when(sec_ref[0] == 0)
    def _():
        n = packet_ref.shape[0] // 2
        embed = picked(spot_ref[:n, :], rows_ref[...])
        hidden = jax.nn.relu(dot(embed, in_ref[...])).astype(BF16)
        tower = dot(hidden, out_ref[...]).astype(BF16)
        logit = jnp.sum(tower.astype(F32) * vec_ref[...], axis=1, keepdims=True)
        packet_ref[:n, :] = tower
        packet_ref[n:, :] = jnp.broadcast_to(logit, (n, 128)).astype(BF16)
        score_ref[...] = as_row(logit, n)


def features_kernel(sec_ref, feat_hbm, item_hbm, slot_ref, spot_ref, rows_ref, weight_ref, head_ref,
                    part_ref, item_ref, feat_ref, sem):
    sec = sec_ref[0]
    n = part_ref.shape[0] - 8
    cands = slot_ref.shape[1]
    width = rows_ref.shape[1]

    @pl.when(sec == 1)
    def _():
        moves = copies((feat_hbm, item_hbm), (feat_ref, item_ref), sem)
        for move in moves:
            move.start()
        embed = picked(spot_ref[:4 * n, :], rows_ref[...])
        for move in moves:
            move.wait()
        wide = jnp.concatenate([embed[f * n:(f + 1) * n, :] for f in range(4)], axis=1)
        part_ref[:n, :] = dot(wide, feat_ref[...])

    @pl.when(sec >= 2)
    def _():
        rows = rows_ref[...]
        embed = jnp.concatenate(
            [picked(jnp.concatenate([column(slot_ref[:, b:b + 128]) for b in range(h, h + 512, 128)], axis=0), rows)
             for h in range(0, cands, 512)], axis=0)
        r, c = iota((128, 128), 0), iota((128, 128), 1)
        same_item = (r // 32) == (c // 32)
        spread = ones_where((r % 32) == (c % 32))
        own_lanes = (r % 4) == (c // 32)
        grams = []
        for b in range(embed.shape[0] // 128):
            block = embed[b * 128:b * 128 + 128, :]
            gram = dot_nt(block, block) * (1.0 / math.sqrt(width))
            gram = jnp.where(same_item, gram, 0.0).astype(BF16)
            grams.append(jnp.where(own_lanes, dot(gram, spread), 0.0).astype(BF16))
        tall = jnp.concatenate(grams, axis=0)
        i, k = iota((8 * n, 32 * n), 0), iota((8 * n, 32 * n), 1)
        choose = ones_where(((k // 32) == (i % n)) & (((k % 32) // 4) == (i // n)))
        flat = dot(choose, tall).astype(BF16)
        flat = jnp.concatenate([flat[q * n:(q + 1) * n, :] for q in range(8)], axis=1)
        part_ref[:n, :] = dot(flat, weight_ref[...])
        part_ref[n:n + 1, :] = head_ref[...]


def prerank_kernel(sec_ref, packet_ref, part_ref, item_ref, weight_ref, head_ref, carry_ref, score_ref):
    @pl.when(sec_ref[0] == 1)
    def _():
        n, hid = part_ref.shape[0] - 8, part_ref.shape[1]
        pre = part_ref[:n, :] + dot(packet_ref[:n, :], item_ref[...])
        inner = jax.nn.relu(pre).astype(BF16)
        hidden = jax.nn.relu(dot(inner, weight_ref[...]))
        prior = packet_ref[n:, :].astype(F32)[:, :1]
        logit = jnp.sum(hidden * head_ref[...], axis=1, keepdims=True) / math.sqrt(hid) + prior
        carry_ref[:, :hid] = hidden.astype(BF16)
        carry_ref[:, hid:] = jnp.broadcast_to(logit, (n, 128)).astype(BF16)
        score_ref[...] = as_row(logit, n)


def final_kernel(sec_ref, near_ref, far_ref, part_ref, before_ref, score0_ref, score1_ref, score_ref):
    sec = sec_ref[0]
    n, hid = part_ref.shape[0] - 8, part_ref.shape[1]
    scale = 1.0 / math.sqrt(hid)

    def rank(from_ref, carry, prior):
        hidden = jax.nn.relu(from_ref[:n, :] + carry)
        return hidden, jnp.sum(hidden * from_ref[n:n + 1, :], axis=1, keepdims=True) * scale + prior

    @pl.when(sec == 0)
    def _():
        score_ref[...] = score0_ref[...]

    @pl.when(sec == 1)
    def _():
        score_ref[...] = score1_ref[...]

    @pl.when(sec == 2)
    def _():
        near = near_ref[...].astype(F32)
        _, logit = rank(part_ref, near[:, :hid], near[:, hid:hid + 1])
        score_ref[...] = as_row(logit, n)

    @pl.when(sec == 3)
    def _():
        far = far_ref[...].astype(F32)
        hidden, logit = rank(before_ref, far[:, :hid], far[:, hid:hid + 1])
        prior = logit.astype(BF16).astype(F32)
        _, logit = rank(part_ref, hidden.astype(BF16).astype(F32), prior)
        score_ref[...] = as_row(logit, n)


def cascade(
    user_dense,
    tables,
    feat_owner,
    feat_row,
    keep_first,
    keep_second,
    section_weight,
    section_head,
    user_proj,
    item_in,
    item_out,
    prerank_feat,
    prerank_item,
):
    shape = pltpu.VMEM
    shards = lax.axis_size("shard")
    cands = feat_row.shape[2]
    slots = 2 * cands // shards
    spots = shards * slots
    width = tables.shape[2]
    hid = section_weight.shape[1]
    final = keep_second.shape[1]
    sec = lax.axis_index("section").reshape(1).astype(jnp.int32)
    user = lax.axis_index("shard").reshape(1).astype(jnp.int32)
    like = lambda a: shape(a.shape, a.dtype)

    request, slot, table, _, _ = call(
        request_kernel,
        (shape((shards, 128), jnp.int32), shape((1, cands), jnp.int32), like(tables[0]),
         shape((1, cands), jnp.int32), shape((1, cands), jnp.int32)),
        user, *in_hbm(feat_owner.reshape(1, cands), feat_row.reshape(1, cands), tables[0]),
        smem=1, hbm=3, sems=3, flops=10**8,
    )
    asked = lax.all_to_all(request.reshape(shards, 1, 128), "shard", 0, 0, tiled=True)
    spot, user_vec, item_in, item_out, weight, head = call(
        prepare_kernel,
        (shape((128, 128), F32), shape((1, width), F32), like(item_in), like(item_out),
         like(section_weight[0]), like(section_head)),
        sec, *in_hbm(item_in, item_out, section_weight[0], section_head),
        slot, keep_first, keep_second, user_dense, user_proj,
        smem=1, hbm=4, sems=4, flops=10**9,
    )
    served = call(
        serve_kernel,
        shape((spots, width), BF16),
        asked.reshape(shards, 128), table,
        flops=10**9,
    )
    rows = lax.all_to_all(served.reshape(shards, slots, width), "shard", 0, 0, tiled=True)
    rows = rows.reshape(spots, width)
    packet, score0 = call(
        tower_kernel,
        (shape((2 * final, width), BF16), shape((1, final), F32)),
        sec, spot, rows, user_vec, item_in, item_out,
        smem=1, flops=10**6,
    )
    packet = lax.ppermute(packet, "section", [(0, 1)])
    part, prerank_item = call(
        features_kernel,
        (shape((final + 8, hid), F32), like(prerank_item)),
        sec, *in_hbm(prerank_feat, prerank_item), slot, spot, rows, weight, head,
        smem=1, hbm=2, sems=2, scratch=[pltpu.VMEM(prerank_feat.shape, BF16)], flops=10**9,
    )
    before = lax.ppermute(part, "section", [(2, 3)])
    carry, score1 = call(
        prerank_kernel,
        (shape((final, hid + 128), BF16), shape((1, final), F32)),
        sec, packet, part, prerank_item, weight, head,
        smem=1, flops=10**8,
    )
    near = lax.ppermute(carry, "section", [(1, 2)])
    far = lax.ppermute(carry, "section", [(1, 3)])
    scores = call(
        final_kernel,
        jax.ShapeDtypeStruct((1, final), F32),
        sec, near, far, part, before, score0, score1,
        smem=1, flops=10**6,
    )
    return scores[None]


def solution(mesh):
    placed = (
        P("shard", None),
        P("section", "shard", None),
        P("section", "shard", None, None),
        P("section", "shard", None),
        P("shard", None),
        P("shard", None),
        P("section", None, None),
        P("section", None),
        P(),
        P(),
        P(),
        P(),
        P(),
    )
    return jax.shard_map(
        cascade,
        mesh=mesh,
        in_specs=placed,
        out_specs=P("section", "shard", None),
        check_vma=False,
    )
```

time: 93.3 us -> 75.7 us (0.81)
  Pallas kernels: 25.7 us -> 10.6 us
  waiting for transfers between devices: 19.5 us -> 23.9 us
  local copies, waits for them, and re-layouts: 4.38 us -> 0.01 us
  starting transfers between devices: 13.3 us -> 11.9 us
    pallas_call x7, Pallas kernels: 25.7 us -> 10.6 us  [call(): pl.pallas_call(kernel, out_shape=out_shape, in_specs=specs, scratch_shape...]
    all_to_all x1, waiting for transfers between devices: 15.7 us -> 18.6 us  [cascade(): lax.all_to_all(served.reshape(shards, slots, width), 'shard', 0, 0, tiled...]
    unnamed x14 -> x8, local copies, waits for them, and re-layouts: 2.06 us -> 0.01 us
    ppermute x5 -> x4, waiting for transfers between devices: 3.85 us -> 5.29 us  [the longest x1 5.29 us: cascade(): near = lax.ppermute(carry, 'section', [(1, 2)])]
    ppermute x5 -> x4, starting transfers between devices: 7.11 us -> 5.73 us  [the longest x1 3.11 us: cascade(): before = lax.ppermute(part, 'section', [(2, 3)])]
    broadcast_in_dim x1 -> x0, local copies, waits for them, and re-layouts: 1.14 us -> none  [per_device(): return scores[None, :, :final]]
  transfers between devices with their start and end apart: 6 -> 5, of which waited for: 3 -> 2; matrix products, arithmetic and copies ran while one was open for 0% -> 0% of each run, Pallas kernels for 11% -> 2%
where the time goes in v2:
time: 75.7 us; the launch traced here: 75.4 us
  blocking collectives  28.8 us (38%)
  waiting for transfers between devices  23.9 us (32%)
  starting transfers between devices  11.9 us (16%)
  Pallas kernels  10.6 us (14%)
    all_to_all x1, blocking collectives, cascade(): lax.all_to_all(request.reshape(shards, 1, 128), 'shard', 0, 0, tiled=True)  28.8 us
    all_to_all x1, waiting for transfers between devices, cascade(): lax.all_to_all(served.reshape(shards, slots, width), 'shard', 0, 0, tiled...  18.6 us
    pallas_call x7, Pallas kernels, call(): pl.pallas_call(kernel, out_shape=out_shape, in_specs=specs, scratch_shape...  10.6 us
    all_to_all x1, starting transfers between devices, cascade(): lax.all_to_all(served.reshape(shards, slots, width), 'shard', 0, 0, tiled...  6.17 us
    ppermute x1, waiting for transfers between devices, cascade(): near = lax.ppermute(carry, 'section', [(1, 2)])  5.29 us
    ppermute x1, starting transfers between devices, cascade(): before = lax.ppermute(part, 'section', [(2, 3)])  3.11 us
  transfers between devices with their start and end apart: 5, of which 2 were waited for; matrix products, arithmetic and copies ran while one was open for 0% of the time, Pallas kernels for 2%

profile of v2, /device:TPU:4, one launch (start us, length us, event | category | flops | bytes accessed | tf_op | source)
XLA Modules:
  0.0 75.4 jit_solution(16802751660936284750)
XLA Ops:
  0.0 1.9 %shard_map.127 = (s32[128,128]{1,0:T(8,128)S(1)}, s32[1,1024]{1,0:T(1,128)S(1)}, bf16[2048,128]{1,0:T(8,128)(2,1)S(1)}, s32[1,1024]{1,0:T(1,128)}, s32[1,1024]{1,0:T(1,128)}) custom-call(s32[1]{0:T(128)} %bitcast.2.user_ref, s32[1,1024]{1,0:T(1,128)} %bitcast.18, s32[1,1024]{1,0:T(1,128)} %bitcast.19, bf16[2048,128]{1,0:T(8,128)(2,1)} %bitcast.17), custom_call_target="tpu_custom_call" | custom-call | flops 100000000 | tf_op jit(solution)/shard_map/pallas_call | solution.py:20
  1.9 28.8 %all_to_all.10 = s32[128,1,128]{2,1,0:T(1,128)S(1)} all-to-all(s32[128,1,128]{2,1,0:T(1,128)S(1)} %bitcast.15), channel_id=1, replica_groups=mesh['section'=4,'shard'=128] {'shard'}, dimensions={0} | all-to-all | bytes 131072 | tf_op jit(solution)/shard_map/all_to_all | solution.py:298
  30.8 0.0 copy-start
  30.8 0.0 copy-start.1
  30.8 0.0 copy-start.2
  30.8 0.0 copy-start.3
  30.8 3.2 %shard_map.129 = bf16[2048,128]{1,0:T(8,128)(2,1)} custom-call(s32[128,128]{1,0:T(8,128)S(1)} %bitcast.16, bf16[2048,128]{1,0:T(8,128)(2,1)S(1)} %get-tuple-element.23.table_ref), custom_call_target="tpu_custom_call" | custom-call | flops 1000000000 | tf_op jit(solution)/shard_map/pallas_call | solution.py:20
  34.0 6.2 %all-to-all-start.1 = ((bf16[128,16,128]{2,1,0:T(8,128)(2,1)}), bf16[128,16,128]{2,1,0:T(8,128)(2,1)S(1)}, u32[]{:S(2)}, u32[]{:S(2)}) async-start(bf16[128,16,128]{2,1,0:T(8,128)(2,1)} %bitcast.9), calls=%async_computation.1 | async-start | bytes 1048576 | tf_op jit(solution)/shard_map/all_to_all | solution.py:313
  40.1 0.0 copy-done
  40.2 0.0 copy-done.1
  40.2 0.0 copy-done.2
  40.2 0.0 copy-done.3
  40.2 1.8 %shard_map.128 = (f32[128,128]{1,0:T(8,128)S(1)}, f32[1,128]{1,0:T(1,128)S(1)}, bf16[128,512]{1,0:T(8,128)(2,1)S(1)}, bf16[512,128]{1,0:T(8,128)(2,1)S(1)}, bf16...) custom-call(s32[1]{0:T(128)} %bitcast.sec_ref, bf16[128,512]{1,0:T(8,128)(2,1)} %in_hbm.1, bf16[512,128]{1,0:T(8,128)(2,1)} %out_hbm.1, ...), custom_call_target="tpu_custom_call" | custom-call | flops 1000000000 | tf_op jit(solution)/shard_map/pallas_call | solution.py:20
  42.0 18.6 %all-to-all-done.1 = bf16[128,16,128]{2,1,0:T(8,128)(2,1)S(1)} async-done(((bf16[128,16,128]{2,1,0:T(8,128)(2,1)}), bf16[128,16,128]{2,1,0:T(8,128)(2,1)S(1)}, u32[]{:S(2)}, u32[]{:S(2)}) %all-to-all-start.1) | async-done | bytes 524320 | tf_op jit(solution)/shard_map/all_to_all | solution.py:313
  60.6 3.0 %shard_map.131 = (f32[40,1024]{1,0:T(8,128)S(1)}, bf16[128,1024]{1,0:T(8,128)(2,1)S(1)}) custom-call(s32[1]{0:T(128)} %bitcast.sec_ref, bf16[512,1024]{1,0:T(8,128)(2,1)} %feat_hbm.1, bf16[128,1024]{1,0:T(8,128)(2,1)} %item_hbm.1, s32[1,1024]{1,0:T(1,128)S(1)} %get-tuple-element.20.slot_ref, f32[128,128]{1,0:T(8,128)S(1)} %get-tuple-element.21.spot_ref, ...), custom_call_target="tpu_custom_call" | custom-call | flops 1000000000 | tf_op jit(solution)/shard_map/pallas_call | solution.py:20
  63.6 3.1 %collective-permute-start.3 = (f32[40,1024]{1,0:T(8,128)S(1)}, f32[40,1024]{1,0:T(8,128)S(1)}, u32[]{:S(2)}, u32[]{:S(2)}) collective-permute-start(f32[40,1024]{1,0:T(8,128)S(1)} %get-tuple-element.30.part_ref), channel_id=1, source_target_pairs={{256,384},{257,385},{258,386},{259,387},{260,388},{261,389},{262,3... | collective-permute-start | bytes 491528 | tf_op jit(solution)/shard_map/ppermute | solution.py:328
  66.7 0.7 collective-permute-start
  67.4 0.0 collective-permute-done.packet_ref
  67.4 0.7 collective-permute-start.2
  68.1 1.3 %collective-permute-start.1 = (bf16[32,1152]{1,0:T(8,128)(2,1)S(1)}, bf16[32,1152]{1,0:T(8,128)(2,1)S(1)}, u32[]{:S(2)}, u32[]{:S(2)}) collective-permute-start(bf16[32,1152]{1,0:T(8,128)(2,1)S(1)} %get-tuple-element.32), channel_id=1, source_target_pairs={{128,256},{129,257},{130,258},{131,259},{132,260},{133,261},{134,2... | collective-permute-start | bytes 221192 | tf_op jit(solution)/shard_map/ppermute | solution.py:335
  69.4 0.0 collective-permute-done.2.far_ref
  69.4 5.3 %collective-permute-done.1.near_ref = bf16[32,1152]{1,0:T(8,128)(2,1)S(1)} collective-permute-done((bf16[32,1152]{1,0:T(8,128)(2,1)S(1)}, bf16[32,1152]{1,0:T(8,128)(2,1)S(1)}, u32[]{:S(2)}, u32[]{:S(2)}) %collective-permute-start.1) | collective-permute-done | bytes 73760 | tf_op jit(solution)/shard_map/ppermute | solution.py:335
  74.7 0.0 collective-permute-done.3.before_ref
  74.7 0.7 shard_map.133
  (2 shorter events, 0.0 us)
Async XLA Ops:
  30.8 9.4 %copy-start = (bf16[1024,128]{1,0:T(8,128)(2,1)S(1)}, bf16[1024,128]{1,0:T(8,128)(2,1)}, u32[]{:S(2)}) copy-start(bf16[1024,128]{1,0:T(8,128)(2,1)} %proj_ref.1) | copy-start | bytes 786436
  30.8 9.4 %copy-start.1 = (bf16[1,1024]{1,0:T(2,128)(2,1)S(1)}, bf16[1,1024]{1,0:T(2,128)(2,1)}, u32[]{:S(2)}) copy-start(bf16[1,1024]{1,0:T(2,128)(2,1)} %dense_ref.1) | copy-start | bytes 6148
  30.8 9.4 %copy-start.2 = (s32[1,256]{1,0:T(1,128)S(1)}, s32[1,256]{1,0:T(1,128)}, u32[]{:S(2)}) copy-start(s32[1,256]{1,0:T(1,128)} %first_ref.1) | copy-start | bytes 3076
  30.8 9.4 %copy-start.3 = (s32[1,32]{1,0:T(1,128)S(1)}, s32[1,32]{1,0:T(1,128)}, u32[]{:S(2)}) copy-start(s32[1,32]{1,0:T(1,128)} %second_ref.1) | copy-start | bytes 388
  34.0 26.7 %all-to-all-start.1 = ((bf16[128,16,128]{2,1,0:T(8,128)(2,1)}), bf16[128,16,128]{2,1,0:T(8,128)(2,1)S(1)}, u32[]{:S(2)}, u32[]{:S(2)}) async-start(bf16[128,16,128]{2,1,0:T(8,128)(2,1)} %bitcast.9), calls=%async_computation.1 | async-start | bytes 1048576 | tf_op jit(solution)/shard_map/all_to_all | solution.py:313
  63.6 11.1 %collective-permute-start.3 = (f32[40,1024]{1,0:T(8,128)S(1)}, f32[40,1024]{1,0:T(8,128)S(1)}, u32[]{:S(2)}, u32[]{:S(2)}) collective-permute-start(f32[40,1024]{1,0:T(8,128)S(1)} %get-tuple-element.30.part_ref), channel_id=1, source_target_pairs={{256,384},{257,385},{258,386},{259,387},{260,388},{261,389},{262,3... | collective-permute-start | bytes 491528 | tf_op jit(solution)/shard_map/ppermute | solution.py:328
  66.7 0.7 collective-permute-start
  67.4 2.0 %collective-permute-start.2 = (bf16[32,1152]{1,0:T(8,128)(2,1)S(1)}, bf16[32,1152]{1,0:T(8,128)(2,1)S(1)}, u32[]{:S(2)}, u32[]{:S(2)}) collective-permute-start(bf16[32,1152]{1,0:T(8,128)(2,1)S(1)} %get-tuple-element.32), channel_id=1, source_target_pairs={{128,384},{129,385},{130,386},{131,387},{132,388},{133,389},{134,3... | collective-permute-start | bytes 221192 | tf_op jit(solution)/shard_map/ppermute | solution.py:336
  68.1 6.6 %collective-permute-start.1 = (bf16[32,1152]{1,0:T(8,128)(2,1)S(1)}, bf16[32,1152]{1,0:T(8,128)(2,1)S(1)}, u32[]{:S(2)}, u32[]{:S(2)}) collective-permute-start(bf16[32,1152]{1,0:T(8,128)(2,1)S(1)} %get-tuple-element.32), channel_id=1, source_target_pairs={{128,256},{129,257},{130,258},{131,259},{132,260},{133,261},{134,2... | collective-permute-start | bytes 221192 | tf_op jit(solution)/shard_map/ppermute | solution.py:335

commit v3 on v2

--- a/solution.py
+++ b/solution.py
@@ -85,35 +85,43 @@
     moves[2].wait()
 
 
+def halves(table):
+    half = table.shape[0] // 2
+    return jnp.concatenate([table[:half, :], table[half:, :]], axis=1)
+
+
+def picked(col, wide):
+    half, width = wide.shape[0], wide.shape[1] // 2
+    fine = ones_where((col & 127) == iota(col.shape, 1))
+    coarse = ((col & (half - 1)) >> 7).astype(F32).astype(BF16)
+    hot = [jnp.where(coarse == float(r), fine, jnp.zeros_like(fine)) for r in range(half // 128)]
+    both = dot(jnp.concatenate(hot, axis=1), wide)
+    return jnp.where(col < half, both[:, :width], both[:, width:]).astype(BF16)
+
+
 def serve_kernel(ids_ref, table_ref, out_ref):
     users = ids_ref.shape[0]
-    slots = 2048 // users
-    group = 128 // slots
-    rows = table_ref.shape[0]
+    rows = out_ref.shape[0]
+    group = 128 * users // rows
     step = 4
-    lanes = iota((128, 128), 1)
-    table = table_ref[...]
+    wide = halves(table_ref[...])
     for first in range(0, users // group, step):
-        tall = []
-        for b in range(first, first + step):
-            ids = jnp.sum(ids_ref[b * group:(b + 1) * group, :], axis=0, keepdims=True)
-            col = column(ids)
-            fine = ones_where((col & 127) == lanes)
-            coarse = (col >> 7).astype(F32).astype(BF16)
-            tall.append(jnp.concatenate(
-                [jnp.where(coarse == float(r), fine, jnp.zeros_like(fine)) for r in range(rows // 128)], axis=1))
-        hot = jnp.concatenate(tall, axis=0)
-        out_ref[first * 128:(first + step) * 128, :] = dot(hot, table).astype(BF16)
-
-
-def prepare_kernel(sec_ref, in_hbm, out_hbm, weight_hbm, head_hbm,
-                   slot_ref, first_ref, second_ref, dense_ref, proj_ref,
-                   spot_ref, vec_ref, in_ref, out_ref, weight_ref, head_ref, sem):
-    moves = copies((in_hbm, out_hbm, weight_hbm, head_hbm),
-                   (in_ref, out_ref, weight_ref, head_ref), sem)
-    for move in moves:
-        move.start()
+        cols = [column(jnp.sum(ids_ref[b * group:(b + 1) * group, :], axis=0, keepdims=True))
+                for b in range(first, first + step)]
+        out_ref[first * 128:(first + step) * 128, :] = picked(jnp.concatenate(cols, axis=0), wide)
+
+
+def prepare_kernel(sec_ref, in_hbm, out_hbm, weight_hbm, proj_hbm,
+                   slot_ref, first_ref, second_ref, dense_ref, head_ref,
+                   spot_ref, vec_ref, in_ref, out_ref, weight_ref, proj_ref, sem):
     sec = sec_ref[0]
+    moves = copies((in_hbm, out_hbm, weight_hbm, proj_hbm), (in_ref, out_ref, weight_ref, proj_ref), sem)
+
+    @pl.when(sec == 0)
+    def _():
+        for move in moves:
+            move.start()
+
     slot = slot_ref[...].astype(F32)
     final = second_ref.shape[1]
 
@@ -128,32 +136,23 @@
     @pl.when(sec == 0)
     def _():
         at = lookup(second_column(), first_ref[...].astype(F32))
-        spot_ref[:final, :] = jnp.broadcast_to(lookup(at, slot), (final, 128))
+        spot_ref[:final, :] = jnp.broadcast_to(lookup(at, slot), (final, 128)).astype(jnp.int32)
 
     @pl.when(sec == 1)
     def _():
         at = second_column() * 4.0
         for f in range(4):
-            spot_ref[f * final:f * final + final, :] = jnp.broadcast_to(lookup(at + float(f), slot), (final, 128))
-
-    for move in moves:
-        move.wait()
+            spot_ref[f * final:f * final + final, :] = jnp.broadcast_to(lookup(at + float(f), slot), (final, 128)).astype(jnp.int32)
 
     @pl.when(sec == 0)
     def _():
+        for move in moves:
+            move.wait()
         active = jax.nn.relu(dot(dense_ref[...], weight_ref[...]))
         query = (active * head_ref[...]).astype(BF16)
         vec_ref[...] = dot(query, proj_ref[...])
 
 
-def picked(col, rows):
-    col = col.astype(jnp.int32)
-    fine = ones_where((col & 127) == iota(col.shape, 1))
-    coarse = (col >> 7).astype(F32).astype(BF16)
-    hot = [jnp.where(coarse == float(r), fine, jnp.zeros_like(fine)) for r in range(rows.shape[0] // 128)]
-    return dot(jnp.concatenate(hot, axis=1), rows).astype(BF16)
-
-
 def as_row(col, lanes):
     n = col.shape[0]
     return jnp.sum(jnp.where(iota((n, lanes), 0) == iota((n, lanes), 1), col, 0.0), axis=0, keepdims=True)
@@ -163,7 +162,7 @@
     @pl.when(sec_ref[0] == 0)
     def _():
         n = packet_ref.shape[0] // 2
-        embed = picked(spot_ref[:n, :], rows_ref[...])
+        embed = picked(spot_ref[:n, :], halves(rows_ref[...]))
         hidden = jax.nn.relu(dot(embed, in_ref[...])).astype(BF16)
         tower = dot(hidden, out_ref[...]).astype(BF16)
         logit = jnp.sum(tower.astype(F32) * vec_ref[...], axis=1, keepdims=True)
@@ -172,37 +171,42 @@
         score_ref[...] = as_row(logit, n)
 
 
-def features_kernel(sec_ref, feat_hbm, item_hbm, slot_ref, spot_ref, rows_ref, weight_ref, head_ref,
-                    part_ref, item_ref, feat_ref, sem):
-    sec = sec_ref[0]
-    n = part_ref.shape[0] - 8
-    cands = slot_ref.shape[1]
-    width = rows_ref.shape[1]
-
-    @pl.when(sec == 1)
-    def _():
-        moves = copies((feat_hbm, item_hbm), (feat_ref, item_ref), sem)
+def features_kernel(sec_ref, feat_hbm, item_hbm, weight_hbm, spot_ref, rows_ref,
+                    part_ref, item_ref, weight_ref, feat_ref, sem):
+    @pl.when(sec_ref[0] == 1)
+    def _():
+        n = part_ref.shape[0]
+        moves = copies((feat_hbm, item_hbm, weight_hbm), (feat_ref, item_ref, weight_ref), sem)
         for move in moves:
             move.start()
-        embed = picked(spot_ref[:4 * n, :], rows_ref[...])
-        for move in moves:
+        embed = picked(spot_ref[:4 * n, :], halves(rows_ref[...]))
+        tall = jnp.concatenate([embed[f * n:(f + 1) * n, :] for f in range(4)], axis=1)
+        moves[0].wait()
+        part_ref[...] = dot(tall, feat_ref[...])
+        for move in moves[1:]:
             move.wait()
-        wide = jnp.concatenate([embed[f * n:(f + 1) * n, :] for f in range(4)], axis=1)
-        part_ref[:n, :] = dot(wide, feat_ref[...])
-
-    @pl.when(sec >= 2)
-    def _():
-        rows = rows_ref[...]
-        embed = jnp.concatenate(
-            [picked(jnp.concatenate([column(slot_ref[:, b:b + 128]) for b in range(h, h + 512, 128)], axis=0), rows)
-             for h in range(0, cands, 512)], axis=0)
+
+
+def gram_kernel(sec_ref, weight_hbm, slot_ref, rows_ref, head_ref, part_ref, weight_ref, sem):
+    @pl.when(sec_ref[0] >= 2)
+    def _():
+        n = part_ref.shape[0] - 8
+        cands = slot_ref.shape[1]
+        width = rows_ref.shape[1]
+        move = pltpu.make_async_copy(weight_hbm, weight_ref, sem.at[0])
+        move.start()
+        wide = halves(rows_ref[...])
+        embed = [
+            picked(jnp.concatenate([column(slot_ref[:, b:b + 128]) for b in range(h, h + 512, 128)], axis=0), wide)
+            for h in range(0, cands, 512)
+        ]
         r, c = iota((128, 128), 0), iota((128, 128), 1)
         same_item = (r // 32) == (c // 32)
         spread = ones_where((r % 32) == (c % 32))
         own_lanes = (r % 4) == (c // 32)
         grams = []
-        for b in range(embed.shape[0] // 128):
-            block = embed[b * 128:b * 128 + 128, :]
+        for b in range(cands // 128):
+            block = embed[b // 4][b % 4 * 128:b % 4 * 128 + 128, :]
             gram = dot_nt(block, block) * (1.0 / math.sqrt(width))
             gram = jnp.where(same_item, gram, 0.0).astype(BF16)
             grams.append(jnp.where(own_lanes, dot(gram, spread), 0.0).astype(BF16))
@@ -211,6 +215,7 @@
         choose = ones_where(((k // 32) == (i % n)) & (((k % 32) // 4) == (i // n)))
         flat = dot(choose, tall).astype(BF16)
         flat = jnp.concatenate([flat[q * n:(q + 1) * n, :] for q in range(8)], axis=1)
+        move.wait()
         part_ref[:n, :] = dot(flat, weight_ref[...])
         part_ref[n:n + 1, :] = head_ref[...]
 
@@ -218,8 +223,8 @@
 def prerank_kernel(sec_ref, packet_ref, part_ref, item_ref, weight_ref, head_ref, carry_ref, score_ref):
     @pl.when(sec_ref[0] == 1)
     def _():
-        n, hid = part_ref.shape[0] - 8, part_ref.shape[1]
-        pre = part_ref[:n, :] + dot(packet_ref[:n, :], item_ref[...])
+        n, hid = part_ref.shape
+        pre = part_ref[...] + dot(packet_ref[:n, :], item_ref[...])
         inner = jax.nn.relu(pre).astype(BF16)
         hidden = jax.nn.relu(dot(inner, weight_ref[...]))
         prior = packet_ref[n:, :].astype(F32)[:, :1]
@@ -296,13 +301,13 @@
         smem=1, hbm=3, sems=3, flops=10**8,
     )
     asked = lax.all_to_all(request.reshape(shards, 1, 128), "shard", 0, 0, tiled=True)
-    spot, user_vec, item_in, item_out, weight, head = call(
+    weight = in_hbm(section_weight[0])[0]
+    spot, user_vec, item_in, item_out = call(
         prepare_kernel,
-        (shape((128, 128), F32), shape((1, width), F32), like(item_in), like(item_out),
-         like(section_weight[0]), like(section_head)),
-        sec, *in_hbm(item_in, item_out, section_weight[0], section_head),
-        slot, keep_first, keep_second, user_dense, user_proj,
-        smem=1, hbm=4, sems=4, flops=10**9,
+        (shape((128, 128), jnp.int32), shape((1, width), F32), like(item_in), like(item_out)),
+        sec, *in_hbm(item_in, item_out), weight, *in_hbm(user_proj),
+        slot, keep_first, keep_second, user_dense, section_head,
+        smem=1, hbm=4, sems=4, scratch=[pltpu.VMEM(weight.shape, BF16), pltpu.VMEM(user_proj.shape, BF16)], flops=10**9,
     )
     served = call(
         serve_kernel,
@@ -319,21 +324,27 @@
         smem=1, flops=10**6,
     )
     packet = lax.ppermute(packet, "section", [(0, 1)])
-    part, prerank_item = call(
+    pre, prerank_item, weight_near = call(
         features_kernel,
-        (shape((final + 8, hid), F32), like(prerank_item)),
-        sec, *in_hbm(prerank_feat, prerank_item), slot, spot, rows, weight, head,
-        smem=1, hbm=2, sems=2, scratch=[pltpu.VMEM(prerank_feat.shape, BF16)], flops=10**9,
-    )
-    before = lax.ppermute(part, "section", [(2, 3)])
+        (shape((final, hid), F32), like(prerank_item), like(weight)),
+        sec, *in_hbm(prerank_feat, prerank_item), weight, spot, rows,
+        smem=1, hbm=3, sems=3, scratch=[pltpu.VMEM(prerank_feat.shape, BF16)], flops=10**8,
+    )
     carry, score1 = call(
         prerank_kernel,
         (shape((final, hid + 128), BF16), shape((1, final), F32)),
-        sec, packet, part, prerank_item, weight, head,
+        sec, packet, pre, prerank_item, weight_near, section_head,
         smem=1, flops=10**8,
     )
+    far = lax.ppermute(carry, "section", [(1, 3)])
     near = lax.ppermute(carry, "section", [(1, 2)])
-    far = lax.ppermute(carry, "section", [(1, 3)])
+    part = call(
+        gram_kernel,
+        shape((final + 8, hid), F32),
+        sec, weight, slot, rows, section_head,
+        smem=1, hbm=1, sems=1, scratch=[pltpu.VMEM(weight.shape, BF16)], flops=10**9,
+    )
+    before = lax.ppermute(part, "section", [(2, 3)])
     scores = call(
         final_kernel,
         jax.ShapeDtypeStruct((1, final), F32),

time: 75.7 us -> 75.5 us (level)
  the two profiles are of different devices: /device:TPU:4 before, /device:TPU:6 now
where the time goes in v3:
time: 75.5 us; the launch traced here: 75.2 us
  blocking collectives  28.8 us (38%)
  waiting for transfers between devices  28.7 us (38%)
  starting transfers between devices  10.1 us (13%)
  Pallas kernels  7.43 us (10%)
    all_to_all x1, blocking collectives, cascade(): lax.all_to_all(request.reshape(shards, 1, 128), 'shard', 0, 0, tiled=True)  28.8 us
    all_to_all x1, waiting for transfers between devices, cascade(): lax.all_to_all(served.reshape(shards, slots, width), 'shard', 0, 0, tiled...  20.4 us
    ppermute x1, waiting for transfers between devices, cascade(): far = lax.ppermute(carry, 'section', [(1, 3)])  8.25 us
    pallas_call x8, Pallas kernels, call(): pl.pallas_call(kernel, out_shape=out_shape, in_specs=specs, scratch_shape...  7.43 us
    all_to_all x1, starting transfers between devices, cascade(): lax.all_to_all(served.reshape(shards, slots, width), 'shard', 0, 0, tiled...  6.17 us
  transfers between devices with their start and end apart: 5, of which 2 were waited for; matrix products, arithmetic and copies ran while one was open for 0% of the time, Pallas kernels for 0%

profile of v3, /device:TPU:6, one launch (start us, length us, event | category | flops | bytes accessed | tf_op | source)
XLA Modules:
  0.0 75.2 jit_solution(11579588757054434915)
XLA Ops:
  0.0 1.9 %shard_map.127 = (s32[128,128]{1,0:T(8,128)S(1)}, s32[1,1024]{1,0:T(1,128)S(1)}, bf16[2048,128]{1,0:T(8,128)(2,1)S(1)}, s32[1,1024]{1,0:T(1,128)}, s32[1,1024]{1,0:T(1,128)}) custom-call(s32[1]{0:T(128)} %bitcast.2.user_ref, s32[1,1024]{1,0:T(1,128)} %bitcast.22, s32[1,1024]{1,0:T(1,128)} %bitcast.23, bf16[2048,128]{1,0:T(8,128)(2,1)} %bitcast.21), custom_call_target="tpu_custom_call" | custom-call | flops 100000000 | tf_op jit(solution)/shard_map/pallas_call | solution.py:20
  1.9 28.8 %all_to_all.10 = s32[128,1,128]{2,1,0:T(1,128)S(1)} all-to-all(s32[128,1,128]{2,1,0:T(1,128)S(1)} %bitcast.16), channel_id=1, replica_groups=mesh['section'=4,'shard'=128] {'shard'}, dimensions={0} | all-to-all | bytes 131072 | tf_op jit(solution)/shard_map/all_to_all | solution.py:303
  30.8 0.0 copy-start
  30.8 2.1 %shard_map.129 = bf16[2048,128]{1,0:T(8,128)(2,1)} custom-call(s32[128,128]{1,0:T(8,128)S(1)} %bitcast.17, bf16[2048,128]{1,0:T(8,128)(2,1)S(1)} %get-tuple-element.22.table_ref), custom_call_target="tpu_custom_call" | custom-call | flops 1000000000 | tf_op jit(solution)/shard_map/pallas_call | solution.py:20
  32.9 6.2 %all-to-all-start.1 = ((bf16[128,16,128]{2,1,0:T(8,128)(2,1)}), bf16[128,16,128]{2,1,0:T(8,128)(2,1)S(1)}, u32[]{:S(2)}, u32[]{:S(2)}) async-start(bf16[128,16,128]{2,1,0:T(8,128)(2,1)} %bitcast.9), calls=%async_computation.1 | async-start | bytes 1048576 | tf_op jit(solution)/shard_map/all_to_all | solution.py:318
  39.1 0.0 copy-start.1
  39.1 0.0 copy-start.2
  39.1 0.0 copy-start.3
  39.1 20.4 %all-to-all-done.1 = bf16[128,16,128]{2,1,0:T(8,128)(2,1)S(1)} async-done(((bf16[128,16,128]{2,1,0:T(8,128)(2,1)}), bf16[128,16,128]{2,1,0:T(8,128)(2,1)S(1)}, u32[]{:S(2)}, u32[]{:S(2)}) %all-to-all-start.1) | async-done | bytes 524320 | tf_op jit(solution)/shard_map/all_to_all | solution.py:318
  59.6 0.0 copy-done
  59.6 2.5 %shard_map.133.part_ref = f32[40,1024]{1,0:T(8,128)S(1)} custom-call(s32[1]{0:T(128)} %bitcast.sec_ref, bf16[1024,1024]{1,0:T(8,128)(2,1)} %bitcast.18, s32[1,1024]{1,0:T(1,128)S(1)} %get-tuple-element.19.slot_ref, bf16[2048,128]{1,0:T(8,128)(2,1)S(1)} %bitcast.13, f32[1,1024]{1,0:T(1,128)S(1)} %copy-done), custom_call_target="tpu_custom_call" | custom-call | flops 1000000000 | tf_op jit(solution)/shard_map/pallas_call | solution.py:20
  62.1 1.3 %collective-permute-start.3 = (f32[40,1024]{1,0:T(8,128)S(1)}, f32[40,1024]{1,0:T(8,128)S(1)}, u32[]{:S(2)}, u32[]{:S(2)}) collective-permute-start(f32[40,1024]{1,0:T(8,128)S(1)} %shard_map.133.part_ref), channel_id=1, source_target_pairs={{256,384},{257,385},{258,386},{259,387},{260,388},{261,389},{262,3... | collective-permute-start | bytes 491528 | tf_op jit(solution)/shard_map/ppermute | solution.py:347
  63.4 0.0 copy-done.1
  63.4 0.0 copy-done.2
  63.4 0.0 copy-done.3
  63.4 0.1 shard_map.128
  63.5 0.7 collective-permute-start
  64.2 0.0 collective-permute-done.packet_ref
  64.2 0.7 collective-permute-start.1
  64.9 1.3 %collective-permute-start.2 = (bf16[32,1152]{1,0:T(8,128)(2,1)S(1)}, bf16[32,1152]{1,0:T(8,128)(2,1)S(1)}, u32[]{:S(2)}, u32[]{:S(2)}) collective-permute-start(bf16[32,1152]{1,0:T(8,128)(2,1)S(1)} %get-tuple-element.30), channel_id=1, source_target_pairs={{128,384},{129,385},{130,386},{131,387},{132,388},{133,389},{134,3... | collective-permute-start | bytes 221192 | tf_op jit(solution)/shard_map/ppermute | solution.py:339
  66.2 0.0 collective-permute-done.1.near_ref
  66.2 8.3 %collective-permute-done.2.far_ref = bf16[32,1152]{1,0:T(8,128)(2,1)S(1)} collective-permute-done((bf16[32,1152]{1,0:T(8,128)(2,1)S(1)}, bf16[32,1152]{1,0:T(8,128)(2,1)S(1)}, u32[]{:S(2)}, u32[]{:S(2)}) %collective-permute-start.2) | collective-permute-done | bytes 73760 | tf_op jit(solution)/shard_map/ppermute | solution.py:339
  74.5 0.0 collective-permute-done.3.before_ref
  74.5 0.7 shard_map.134
  (3 shorter events, 0.1 us)
Async XLA Ops:
  30.8 28.8 %copy-start = (f32[1,1024]{1,0:T(1,128)S(1)}, f32[1,1024]{1,0:T(1,128)}, u32[]{:S(2)}) copy-start(f32[1,1024]{1,0:T(1,128)} %head_ref.5) | copy-start | bytes 12292
  32.9 26.7 %all-to-all-start.1 = ((bf16[128,16,128]{2,1,0:T(8,128)(2,1)}), bf16[128,16,128]{2,1,0:T(8,128)(2,1)S(1)}, u32[]{:S(2)}, u32[]{:S(2)}) async-start(bf16[128,16,128]{2,1,0:T(8,128)(2,1)} %bitcast.9), calls=%async_computation.1 | async-start | bytes 1048576 | tf_op jit(solution)/shard_map/all_to_all | solution.py:318
  39.1 24.3 %copy-start.1 = (bf16[1,1024]{1,0:T(2,128)(2,1)S(1)}, bf16[1,1024]{1,0:T(2,128)(2,1)}, u32[]{:S(2)}) copy-start(bf16[1,1024]{1,0:T(2,128)(2,1)} %dense_ref.1) | copy-start | bytes 6148
  39.1 24.3 %copy-start.2 = (s32[1,256]{1,0:T(1,128)S(1)}, s32[1,256]{1,0:T(1,128)}, u32[]{:S(2)}) copy-start(s32[1,256]{1,0:T(1,128)} %first_ref.1) | copy-start | bytes 3076
  39.1 24.3 %copy-start.3 = (s32[1,32]{1,0:T(1,128)S(1)}, s32[1,32]{1,0:T(1,128)}, u32[]{:S(2)}) copy-start(s32[1,32]{1,0:T(1,128)} %second_ref.1) | copy-start | bytes 388
  62.1 12.4 %collective-permute-start.3 = (f32[40,1024]{1,0:T(8,128)S(1)}, f32[40,1024]{1,0:T(8,128)S(1)}, u32[]{:S(2)}, u32[]{:S(2)}) collective-permute-start(f32[40,1024]{1,0:T(8,128)S(1)} %shard_map.133.part_ref), channel_id=1, source_target_pairs={{256,384},{257,385},{258,386},{259,387},{260,388},{261,389},{262,3... | collective-permute-start | bytes 491528 | tf_op jit(solution)/shard_map/ppermute | solution.py:347
  63.5 0.7 collective-permute-start
  64.2 2.0 %collective-permute-start.1 = (bf16[32,1152]{1,0:T(8,128)(2,1)S(1)}, bf16[32,1152]{1,0:T(8,128)(2,1)S(1)}, u32[]{:S(2)}, u32[]{:S(2)}) collective-permute-start(bf16[32,1152]{1,0:T(8,128)(2,1)S(1)} %get-tuple-element.30), channel_id=1, source_target_pairs={{128,256},{129,257},{130,258},{131,259},{132,260},{133,261},{134,2... | collective-permute-start | bytes 221192 | tf_op jit(solution)/shard_map/ppermute | solution.py:340
  64.9 9.6 %collective-permute-start.2 = (bf16[32,1152]{1,0:T(8,128)(2,1)S(1)}, bf16[32,1152]{1,0:T(8,128)(2,1)S(1)}, u32[]{:S(2)}, u32[]{:S(2)}) collective-permute-start(bf16[32,1152]{1,0:T(8,128)(2,1)S(1)} %get-tuple-element.30), channel_id=1, source_target_pairs={{128,384},{129,385},{130,386},{131,387},{132,388},{133,389},{134,3... | collective-permute-start | bytes 221192 | tf_op jit(solution)/shard_map/ppermute | solution.py:339

commit v4 on v3

v4 whole, which is shorter than its diff:
```python
import math

import jax
import jax.numpy as jnp
from jax import lax
from jax.experimental import pallas as pl
from jax.experimental.pallas import tpu as pltpu
from jax.sharding import PartitionSpec as P


F32 = jnp.float32
BF16 = jnp.bfloat16
NT = (((1,), (1,)), ((), ()))
MARK = 1 << 14


def call(kernel, out_shape, *operands, smem=0, hbm=0, sems=0, flops=0, scratch=(), smem_out=False):
    specs = [pl.BlockSpec(memory_space=pltpu.SMEM)] * smem
    specs += [pl.BlockSpec(memory_space=pltpu.HBM)] * hbm
    specs += [pl.BlockSpec(memory_space=pltpu.VMEM)] * (len(operands) - smem - hbm)
    vmem, scalar = pl.BlockSpec(memory_space=pltpu.VMEM), pl.BlockSpec(memory_space=pltpu.SMEM)
    many = isinstance(out_shape, (tuple, list))
    return pl.pallas_call(
        kernel,
        out_shape=out_shape,
        out_specs=(vmem, scalar) if smem_out else (vmem,) * len(out_shape) if many else vmem,
        in_specs=specs,
        scratch_shapes=[*scratch, *([pltpu.SemaphoreType.DMA((sems,))] if sems else [])],
        cost_estimate=pl.CostEstimate(flops=flops, transcendentals=0, bytes_accessed=0),
        compiler_params=pltpu.CompilerParams(vmem_limit_bytes=20 << 20),
    )(*operands)


def copies(sources, targets, sem):
    return [pltpu.make_async_copy(a, b, sem.at[i]) for i, (a, b) in enumerate(zip(sources, targets))]


def in_hbm(*arrays):
    return [pltpu.with_memory_space_constraint(a, pltpu.HBM) for a in arrays]


def iota(shape, axis):
    return lax.broadcasted_iota(jnp.int32, shape, axis)


def ones_where(mask):
    return jnp.where(mask, 1.0, 0.0).astype(BF16)


def dot(a, b):
    return jnp.dot(a, b, preferred_element_type=F32)


def dot_nt(a, b):
    return lax.dot_general(a, b, NT, preferred_element_type=F32)


def column(row):
    return jnp.broadcast_to(row, (128, 128)).T


def lookup(at, row):
    lanes = iota((at.shape[0], row.shape[1]), 1).astype(F32)
    return jnp.sum(jnp.where(lanes == at, row.astype(F32), 0.0), axis=1, keepdims=True)


def request_kernel(sec_ref, user_ref, dense_ref, owner_hbm, row_hbm, table_hbm, first_hbm, second_hbm,
                   req_ref, slot_ref, spot_ref, table_ref, owner_ref, row_ref, first_ref, second_ref, sem):
    moves = copies((owner_hbm, row_hbm, first_hbm, second_hbm, table_hbm),
                   (owner_ref, row_ref, first_ref, second_ref, table_ref), sem)
    for move in moves:
        move.start()
    shards = req_ref.shape[0]
    cands = owner_ref.shape[1]
    final = second_ref.shape[1]
    slots = 2 * cands // shards
    base = (user_ref[0] % (128 // slots)) * slots
    sec = sec_ref[0]
    for move in moves[:4]:
        move.wait()

    @pl.when(dense_ref[0] == 1)
    def _():
        earlier = ones_where((iota((128, 256), 0) < iota((128, 256), 1)) | (iota((128, 256), 1) >= 128))
        seen = jnp.zeros((shards, 128), F32)
        ranks = []
        owner = owner_ref[...]
        hits = owner == iota((shards, cands), 0)
        hot = ones_where(hits)
        for b in range(cands // 128):
            part = slice(b * 128, b * 128 + 128)
            counts = dot(hot[:, part], earlier)
            ranks.append(jnp.sum(jnp.where(hits[:, part], counts[:, :128] + seen, 0.0), axis=0, keepdims=True))
            seen = seen + counts[:, 128:]
        rank = jnp.concatenate(ranks, axis=1).astype(jnp.int32)
        slot_ref[...] = owner * slots + rank
        row = row_ref[...]
        at_slot = rank + base == iota((128, cands), 0)
        high = jnp.where(at_slot, (row >> 4).astype(F32), 0.0).astype(BF16)
        low = jnp.where(at_slot, (row & 15).astype(F32), 0.0).astype(BF16)
        req_ref[...] = (dot_nt(hot, high) * 16.0 + dot_nt(hot, low)).astype(jnp.int32)

    @pl.when(dense_ref[0] == 0)
    def _():
        second = jnp.concatenate([second_ref[...], jnp.zeros((1, 128 - final), jnp.int32)], axis=1)
        second = column(second.astype(F32))[:final, :1]
        single = lookup(second, first_ref[...])
        fours = [second * 4.0 + float(f) for f in range(4)]
        none = jnp.full((final, 1), -1.0, F32)
        at = jnp.concatenate(
            [jnp.where(sec == 0, single if f == 0 else none, fours[f]) for f in range(4)], axis=0)
        owner = lookup(at, owner_ref[...] + 1) - 1.0
        row = lookup(at, row_ref[...]).astype(jnp.int32)
        count = at.shape[0]
        lanes = iota((count, 128), 1).astype(F32)
        hot = jnp.where(owner == lanes, 1.0, 0.0)
        before = ones_where(iota((count, count), 1) < iota((count, count), 0))
        rank = jnp.sum(hot * dot(before, hot.astype(BF16)), axis=1, keepdims=True)
        spot_ref[...] = jnp.broadcast_to(owner * slots + rank, spot_ref.shape).astype(jnp.int32)
        at_slot = rank + base.astype(F32) == lanes
        high = jnp.where(at_slot, (row >> 4).astype(F32), 0.0).astype(BF16)
        low = jnp.where(at_slot, (row & 15).astype(F32), 0.0).astype(BF16)
        turned = hot.T.astype(BF16)
        mine = (iota((1, 128), 1) >= base) & (iota((1, 128), 1) < base + slots)
        over = jnp.max(rank, axis=0, keepdims=True) >= slots // 2
        mark = jnp.where(mine & over, MARK, 0)
        req_ref[...] = (dot(turned, high) * 16.0 + dot(turned, low)).astype(jnp.int32) + mark

    moves[4].wait()


def halves(table):
    half = table.shape[0] // 2
    return jnp.concatenate([table[:half, :], table[half:, :]], axis=1)


def picked(col, wide):
    half, width = wide.shape[0], wide.shape[1] // 2
    fine = ones_where((col & 127) == iota(col.shape, 1))
    coarse = ((col & (half - 1)) >> 7).astype(F32).astype(BF16)
    hot = [jnp.where(coarse == float(r), fine, jnp.zeros_like(fine)) for r in range(half // 128)]
    both = dot(jnp.concatenate(hot, axis=1), wide)
    return jnp.where(col < half, both[:, :width], both[:, width:]).astype(BF16)


def served_rows(ids_ref, table_ref, out_ref, keep):
    users = ids_ref.shape[0]
    slots = out_ref.shape[0] // users * 16 // keep
    group = 128 // slots
    wide = halves(table_ref[...])
    count = group * keep
    step = 512 // count
    for first in range(0, users // group, step):
        cols = []
        for b in range(first, first + step):
            ids = jnp.sum(ids_ref[b * group:(b + 1) * group, :], axis=0, keepdims=True)
            col = column(ids & (MARK - 1))
            cols += [col[i * slots:i * slots + keep, :] for i in range(group)] if keep < slots else [col]
        out_ref[first * count:(first + step) * count, :] = picked(jnp.concatenate(cols, axis=0), wide)


def serve_kernel(ids_ref, table_ref, out_ref):
    served_rows(ids_ref, table_ref, out_ref, 16)


def serve_short_kernel(ids_ref, table_ref, out_ref, over_ref):
    over_ref[0] = jnp.max(ids_ref[...])
    served_rows(ids_ref, table_ref, out_ref, 8)


def nothing_kernel(*refs):
    pass


def prepare_kernel(sec_ref, in_hbm, out_hbm, weight_hbm, proj_hbm, dense_ref, head_ref,
                   vec_ref, in_ref, out_ref, weight_ref, proj_ref, sem):
    @pl.when(sec_ref[0] == 0)
    def _():
        moves = copies((in_hbm, out_hbm, weight_hbm, proj_hbm), (in_ref, out_ref, weight_ref, proj_ref), sem)
        for move in moves:
            move.start()
        for move in moves:
            move.wait()
        active = jax.nn.relu(dot(dense_ref[...], weight_ref[...]))
        query = (active * head_ref[...]).astype(BF16)
        vec_ref[...] = dot(query, proj_ref[...])


def as_row(col, lanes):
    n = col.shape[0]
    return jnp.sum(jnp.where(iota((n, lanes), 0) == iota((n, lanes), 1), col, 0.0), axis=0, keepdims=True)


def tower_kernel(sec_ref, spot_ref, rows_ref, vec_ref, in_ref, out_ref, packet_ref, score_ref):
    @pl.when(sec_ref[0] == 0)
    def _():
        n = packet_ref.shape[0] // 2
        embed = picked(spot_ref[:n, :], halves(rows_ref[...]))
        hidden = jax.nn.relu(dot(embed, in_ref[...])).astype(BF16)
        tower = dot(hidden, out_ref[...]).astype(BF16)
        logit = jnp.sum(tower.astype(F32) * vec_ref[...], axis=1, keepdims=True)
        packet_ref[:n, :] = tower
        packet_ref[n:, :] = jnp.broadcast_to(logit, (n, 128)).astype(BF16)
        score_ref[...] = as_row(logit, n)


def features_kernel(sec_ref, feat_hbm, item_hbm, weight_hbm, spot_ref, rows_ref,
                    part_ref, item_ref, weight_ref, feat_ref, sem):
    @pl.when(sec_ref[0] == 1)
    def _():
        n = part_ref.shape[0]
        moves = copies((feat_hbm, item_hbm, weight_hbm), (feat_ref, item_ref, weight_ref), sem)
        for move in moves:
            move.start()
        embed = picked(spot_ref[:4 * n, :], halves(rows_ref[...]))
        tall = jnp.concatenate([embed[f * n:(f + 1) * n, :] for f in range(4)], axis=1)
        moves[0].wait()
        part_ref[...] = dot(tall, feat_ref[...])
        for move in moves[1:]:
            move.wait()


def gram_kernel(sec_ref, weight_hbm, slot_ref, rows_ref, head_ref, part_ref, weight_ref, sem):
    @pl.when(sec_ref[0] >= 2)
    def _():
        n = part_ref.shape[0] - 8
        cands = slot_ref.shape[1]
        width = rows_ref.shape[1]
        move = pltpu.make_async_copy(weight_hbm, weight_ref, sem.at[0])
        move.start()
        wide = halves(rows_ref[...])
        embed = [
            picked(jnp.concatenate([column(slot_ref[:, b:b + 128]) for b in range(h, h + 512, 128)], axis=0), wide)
            for h in range(0, cands, 512)
        ]
        r, c = iota((128, 128), 0), iota((128, 128), 1)
        same_item = (r // 32) == (c // 32)
        spread = ones_where((r % 32) == (c % 32))
        own_lanes = (r % 4) == (c // 32)
        grams = []
        for b in range(cands // 128):
            block = embed[b // 4][b % 4 * 128:b % 4 * 128 + 128, :]
            gram = dot_nt(block, block) * (1.0 / math.sqrt(width))
            gram = jnp.where(same_item, gram, 0.0).astype(BF16)
            grams.append(jnp.where(own_lanes, dot(gram, spread), 0.0).astype(BF16))
        tall = jnp.concatenate(grams, axis=0)
        i, k = iota((8 * n, 32 * n), 0), iota((8 * n, 32 * n), 1)
        choose = ones_where(((k // 32) == (i % n)) & (((k % 32) // 4) == (i // n)))
        flat = dot(choose, tall).astype(BF16)
        flat = jnp.concatenate([flat[q * n:(q + 1) * n, :] for q in range(8)], axis=1)
        move.wait()
        part_ref[:n, :] = dot(flat, weight_ref[...])
        part_ref[n:n + 1, :] = head_ref[...]


def prerank_kernel(sec_ref, packet_ref, part_ref, item_ref, weight_ref, head_ref, carry_ref, score_ref):
    @pl.when(sec_ref[0] == 1)
    def _():
        n, hid = part_ref.shape
        pre = part_ref[...] + dot(packet_ref[:n, :], item_ref[...])
        inner = jax.nn.relu(pre).astype(BF16)
        hidden = jax.nn.relu(dot(inner, weight_ref[...]))
        prior = packet_ref[n:, :].astype(F32)[:, :1]
        logit = jnp.sum(hidden * head_ref[...], axis=1, keepdims=True) / math.sqrt(hid) + prior
        carry_ref[:, :hid] = hidden.astype(BF16)
        carry_ref[:, hid:] = jnp.broadcast_to(logit, (n, 128)).astype(BF16)
        score_ref[...] = as_row(logit, n)


def rank(part_ref, carry_ref):
    n, hid = part_ref.shape[0] - 8, part_ref.shape[1]
    carry = carry_ref[...].astype(F32)
    hidden = jax.nn.relu(part_ref[:n, :] + carry[:, :hid])
    logit = jnp.sum(hidden * part_ref[n:n + 1, :], axis=1, keepdims=True) / math.sqrt(hid)
    return hidden, logit + carry[:, hid:hid + 1]


def rank_kernel(sec_ref, near_ref, part_ref, carry_ref, score_ref):
    @pl.when(sec_ref[0] == 2)
    def _():
        n, hid = part_ref.shape[0] - 8, part_ref.shape[1]
        hidden, logit = rank(part_ref, near_ref)
        carry_ref[:, :hid] = hidden.astype(BF16)
        carry_ref[:, hid:] = jnp.broadcast_to(logit, (n, 128)).astype(BF16)
        score_ref[...] = as_row(logit, n)


def final_kernel(sec_ref, last_ref, part_ref, score0_ref, score1_ref, score2_ref, score_ref):
    sec = sec_ref[0]

    for s, from_ref in enumerate((score0_ref, score1_ref, score2_ref)):
        @pl.when(sec == s)
        def _():
            score_ref[...] = from_ref[...]

    @pl.when(sec == 3)
    def _():
        _, logit = rank(part_ref, last_ref)
        score_ref[...] = as_row(logit, logit.shape[0])


def cascade(
    user_dense,
    tables,
    feat_owner,
    feat_row,
    keep_first,
    keep_second,
    section_weight,
    section_head,
    user_proj,
    item_in,
    item_out,
    prerank_feat,
    prerank_item,
):
    shape = pltpu.VMEM
    shards = lax.axis_size("shard")
    cands = feat_row.shape[2]
    slots = 2 * cands // shards
    spots = shards * slots
    width = tables.shape[2]
    hid = section_weight.shape[1]
    final = keep_second.shape[1]
    sec = lax.axis_index("section").reshape(1).astype(jnp.int32)
    user = lax.axis_index("shard").reshape(1).astype(jnp.int32)
    dense = sec[0] >= 2
    like = lambda a: shape(a.shape, a.dtype)

    weight, feat, item, into, out_of, proj = in_hbm(
        section_weight[0], prerank_feat, prerank_item, item_in, item_out, user_proj)

    request, slot, spot, table = call(
        request_kernel,
        (shape((shards, 128), jnp.int32), shape((1, cands), jnp.int32), shape((128, 128), jnp.int32), like(tables[0])),
        sec, user, dense.astype(jnp.int32).reshape(1), *in_hbm(feat_owner.reshape(1, cands), feat_row.reshape(1, cands), tables[0], keep_first, keep_second),
        smem=3, hbm=5, sems=5, flops=10**8,
        scratch=[pltpu.VMEM(s, jnp.int32) for s in ((1, cands), (1, cands), keep_first.shape, keep_second.shape)],
    )
    asked = lax.all_to_all(request.reshape(shards, 1, 128), "shard", 0, 0, tiled=True).reshape(shards, 128)

    def exchanged(served):
        rows = lax.all_to_all(served.reshape(shards, -1, width), "shard", 0, 0, tiled=True)
        rows = jnp.pad(rows, ((0, 0), (0, slots - rows.shape[1]), (0, 0)))
        return rows.reshape(spots, width)

    def serve():
        return call(serve_kernel, shape((spots, width), BF16), asked, table, flops=10**9)

    def blank(*shapes):
        return pl.pallas_call(
            nothing_kernel,
            out_shape=shapes,
            in_specs=[pl.BlockSpec(memory_space=pl.ANY)],
            out_specs=(pl.BlockSpec(memory_space=pltpu.VMEM),) * len(shapes),
            compiler_params=pltpu.CompilerParams(vmem_limit_bytes=1 << 20),
        )(asked)

    scored = shape((1, final), F32)
    carried = shape((final, hid + 128), BF16)

    def sparse_sections():
        served, over = call(
            serve_short_kernel,
            (shape((spots // 2, width), BF16), jax.ShapeDtypeStruct((1,), jnp.int32)),
            asked, table, flops=10**9, smem_out=True,
        )

        def with_query(given):
            rows = exchanged(given)
            query = call(
                prepare_kernel,
                (shape((1, width), F32), like(item_in), like(item_out)),
                sec, into, out_of, weight, proj, user_dense, section_head,
                smem=1, hbm=4, sems=4, flops=10**9,
                scratch=[pltpu.VMEM(weight.shape, BF16), pltpu.VMEM(user_proj.shape, BF16)],
            )
            return rows, *query

        rows, *query = lax.cond(over[0] >= MARK, lambda: with_query(serve()), lambda: with_query(served))
        packet, score0 = call(
            tower_kernel,
            (shape((2 * final, width), BF16), scored),
            sec, spot, rows, *query,
            smem=1, flops=10**6,
        )
        packet = lax.ppermute(packet, "section", [(0, 1)])
        pre, item_near, weight_near = call(
            features_kernel,
            (shape((final, hid), F32), like(prerank_item), like(weight)),
            sec, feat, item, weight, spot, rows,
            smem=1, hbm=3, sems=3, scratch=[pltpu.VMEM(prerank_feat.shape, BF16)], flops=10**8,
        )
        carry, score1 = call(
            prerank_kernel,
            (carried, scored),
            sec, packet, pre, item_near, weight_near, section_head,
            smem=1, flops=10**8,
        )
        return carry, score0, score1

    def dense_sections():
        return call(
            gram_kernel,
            shape((final + 8, hid), F32),
            sec, weight, slot, exchanged(serve()), section_head,
            smem=1, hbm=1, sems=1, scratch=[pltpu.VMEM(weight.shape, BF16)], flops=10**9,
        )

    carry, score0, score1 = lax.cond(dense, lambda: tuple(blank(carried, scored, scored)), sparse_sections)
    near = lax.ppermute(carry, "section", [(1, 2)])
    part = lax.cond(dense, dense_sections, lambda: blank(shape((final + 8, hid), F32))[0])
    carry, score2 = call(rank_kernel, (carried, scored), sec, near, part, smem=1, flops=10**6)
    last = lax.ppermute(carry, "section", [(2, 3)])
    scores = call(
        final_kernel,
        jax.ShapeDtypeStruct((1, final), F32),
        sec, last, part, score0, score1, score2,
        smem=1, flops=10**6,
    )
    return scores[None]


def solution(mesh):
    placed = (
        P("shard", None),
        P("section", "shard", None),
        P("section", "shard", None, None),
        P("section", "shard", None),
        P("shard", None),
        P("shard", None),
        P("section", None, None),
        P("section", None),
        P(),
        P(),
        P(),
        P(),
        P(),
    )
    return jax.shard_map(
        cascade,
        mesh=mesh,
        in_specs=placed,
        out_specs=P("section", "shard", None),
        check_vma=False,
    )
```

time: 75.5 us -> 72.1 us (0.955)
  blocking collectives: 28.8 us -> 55 us
  waiting for transfers between devices: 28.7 us -> 8.6 us
  starting transfers between devices: 10.1 us -> 1.95 us
  Pallas kernels: 7.43 us -> 5.88 us
    all_to_all x0 -> x1, blocking collectives: none -> 26.2 us  [exchanged(): lax.all_to_all(served.reshape(shards, -1, width), 'shard', 0, 0, tiled=True)]
    all_to_all x1 -> x0, waiting for transfers between devices: 20.4 us -> none  [cascade(): lax.all_to_all(served.reshape(shards, slots, width), 'shard', 0, 0, tiled...]
    all_to_all x1 -> x0, starting transfers between devices: 6.17 us -> none  [cascade(): lax.all_to_all(served.reshape(shards, slots, width), 'shard', 0, 0, tiled...]
    ppermute x3 -> x1, starting transfers between devices: 3.25 us -> 1.29 us  [cascade(): last = lax.ppermute(carry, 'section', [(2, 3)])]
    pallas_call x8 -> x6, Pallas kernels: 7.43 us -> 5.88 us  [the longest x5 5.88 us: call(): pl.pallas_call(kernel, out_shape=out_shape, out_specs=(vmem, scalar) if s...]
    ppermute x3 -> x1, waiting for transfers between devices: 8.26 us -> 8.59 us  [cascade(): last = lax.ppermute(carry, 'section', [(2, 3)])]
  transfers between devices with their start and end apart: 5 -> 2, of which waited for: 2 -> 1; matrix products, arithmetic and copies ran while one was open for 0% -> 0% of each run, Pallas kernels for 0% -> 5%
where the time goes in v4:
time: 72.1 us; the launch traced here: 71.8 us
  blocking collectives  55 us (76%)
  waiting for transfers between devices  8.6 us (12%)
  Pallas kernels  5.88 us (8%)
  starting transfers between devices  1.95 us (3%)
    all_to_all x1, blocking collectives, cascade(): lax.all_to_all(request.reshape(shards, 1, 128), 'shard', 0, 0, tiled=True)  28.8 us
    all_to_all x1, blocking collectives, exchanged(): lax.all_to_all(served.reshape(shards, -1, width), 'shard', 0, 0, tiled=True)  26.2 us
    ppermute x1, waiting for transfers between devices, cascade(): last = lax.ppermute(carry, 'section', [(2, 3)])  8.59 us
    pallas_call x5, Pallas kernels, call(): pl.pallas_call(kernel, out_shape=out_shape, out_specs=(vmem, scalar) if s...  5.88 us
  transfers between devices with their start and end apart: 2, of which 1 were waited for; matrix products, arithmetic and copies ran while one was open for 0% of the time, Pallas kernels for 5%

profile of v4, /device:TPU:6, one launch (start us, length us, event | category | flops | bytes accessed | tf_op | source)
XLA Modules:
  0.0 71.8 jit_solution(13845943015536030152)
XLA Ops:
  0.0 1.3 %shard_map.133 = (s32[128,128]{1,0:T(8,128)S(1)}, s32[1,1024]{1,0:T(1,128)S(1)}, s32[128,128]{1,0:T(8,128)S(1)}, bf16[2048,128]{1,0:T(8,128)(2,1)S(1)}) custom-call(s32[1]{0:T(128)} %bitcast.7.sec_ref, s32[1]{0:T(128)} %bitcast.8.user_ref, s32[1]{0:T(128)} %bitcast.9.dense_ref, s32[1,1024]{1,0:T(1,128)} %bitcast.29, s32[1,1024]{1,0:T(1,128)} %bitcast.30, ...), custom_call_target="tpu_custom_call" | custom-call | flops 100000000 | tf_op jit(solution)/shard_map/pallas_call | solution.py:23
  1.3 28.8 %all_to_all.18 = s32[128,1,128]{2,1,0:T(1,128)S(1)} all-to-all(s32[128,1,128]{2,1,0:T(1,128)S(1)} %bitcast.21), channel_id=1, replica_groups=mesh['section'=4,'shard'=128] {'shard'}, dimensions={0} | all-to-all | bytes 131072 | tf_op jit(solution)/shard_map/all_to_all | solution.py:340
  30.1 0.7 collective-permute-start.1
  30.8 30.3 %conditional.4 = (f32[40,1024]{1,0:T(8,128)S(1)}) conditional(s32[]{:T(128)} %convert_element_type.13, s32[128,128]{1,0:T(8,128)S(1)} %bitcast.26, (s32[128,128]{1,0:T(8,128)S(1)}, bf16[2048,128]{1,0:T(8,128)(2,1)S(1)}, s32[1]{0:T(128)}, bf16[1024,1024]{1,0:T(8,128)(2,1)}, s32[1,1024]{1,0:T(1,128)S(1)}, /*index=5*/f32[1,1024]{1,0:T(1,128)}) %tuple.39), branch_computations={%region_4.5_spmd, %region_5.6_spmd} | conditional | flops 2000000000 | bytes 1064996 | solution.py:412
  30.8 0.0 copy-start.1
  30.8 1.4 %branch_1_fun.8 = bf16[2048,128]{1,0:T(8,128)(2,1)S(1)} custom-call(s32[128,128]{1,0:T(8,128)S(1)} %get-tuple-element.131.ids_ref, bf16[2048,128]{1,0:T(8,128)(2,1)S(1)} %get-tuple-element.132.table_ref), custom_call_target="tpu_custom_call" | custom-call | flops 1000000000 | tf_op jit(solution)/shard_map/cond/branch_1_fun/pallas_call | solution.py:23
  32.2 26.2 %all_to_all.17 = bf16[128,16,128]{2,1,0:T(8,128)(2,1)S(1)} all-to-all(bf16[128,16,128]{2,1,0:T(8,128)(2,1)S(1)} %bitcast.20), channel_id=1, replica_groups=mesh['section'=4,'shard'=128] {'shard'}, dimensions={0} | all-to-all | bytes 1048576 | tf_op jit(solution)/shard_map/cond/branch_1_fun/all_to_all | solution.py:343
  58.4 0.0 copy-done.1
  58.4 2.5 %branch_1_fun.9 = f32[40,1024]{1,0:T(8,128)S(1)} custom-call(s32[1]{0:T(128)} %get-tuple-element.128.sec_ref, bf16[1024,1024]{1,0:T(8,128)(2,1)} %get-tuple-element.129.weight_hbm, s32[1,1024]{1,0:T(1,128)S(1)} %get-tuple-element.130.slot_ref, bf16[2048,128]{1,0:T(8,128)(2,1)S(1)} %bitcast.19, f32[1,1024]{1,0:T(1,128)S(1)} %copy-done.1), custom_call_target="tpu_custom_call" | custom-call | flops 1000000000 | tf_op jit(solution)/shard_map/cond/branch_1_fun/pallas_call | solution.py:23
  61.1 0.0 collective-permute-done.1.near_ref
  61.1 1.3 %collective-permute-start.2 = (bf16[32,1152]{1,0:T(8,128)(2,1)S(1)}, bf16[32,1152]{1,0:T(8,128)(2,1)S(1)}, u32[]{:S(2)}, u32[]{:S(2)}) collective-permute-start(bf16[32,1152]{1,0:T(8,128)(2,1)S(1)} %get-tuple-element.148), channel_id=1, source_target_pairs={{256,384},{257,385},{258,386},{259,387},{260,388},{261,389},{262,3... | collective-permute-start | bytes 221192 | tf_op jit(solution)/shard_map/ppermute | solution.py:414
  62.4 8.6 %collective-permute-done.2.last_ref = bf16[32,1152]{1,0:T(8,128)(2,1)S(1)} collective-permute-done((bf16[32,1152]{1,0:T(8,128)(2,1)S(1)}, bf16[32,1152]{1,0:T(8,128)(2,1)S(1)}, u32[]{:S(2)}, u32[]{:S(2)}) %collective-permute-start.2) | collective-permute-done | bytes 73760 | tf_op jit(solution)/shard_map/ppermute | solution.py:414
  71.0 0.7 %shard_map.135 = f32[1,32]{1,0:T(1,128)} custom-call(s32[1]{0:T(128)} %bitcast.7.sec_ref, bf16[32,1152]{1,0:T(8,128)(2,1)S(1)} %collective-permute-done.2.last_ref, f32[40,1024]{1,0:T(8,128)S(1)} %get-tuple-element.179.part_ref, f32[1,32]{1,0:T(1,128)S(1)} %get-tuple-element.149.score0_ref, f32[1,32]{1,0:T(1,128)S(1)} %get-tuple-element.150.score1_ref, ...), custom_call_target="tpu_custom_call" | custom-call | flops 1000000 | tf_op jit(solution)/shard_map/pallas_call | solution.py:23
  (3 shorter events, 0.0 us)
Async XLA Ops:
  30.1 31.0 %collective-permute-start.1 = (bf16[32,1152]{1,0:T(8,128)(2,1)S(1)}, bf16[32,1152]{1,0:T(8,128)(2,1)S(1)}, u32[]{:S(2)}, u32[]{:S(2)}) collective-permute-start(bf16[32,1152]{1,0:T(8,128)(2,1)S(1)} %get-tuple-element.146), channel_id=1, source_target_pairs={{128,256},{129,257},{130,258},{131,259},{132,260},{133,261},{134,2... | collective-permute-start | bytes 221192 | tf_op jit(solution)/shard_map/ppermute | solution.py:411
  30.8 27.6 %copy-start.1 = (f32[1,1024]{1,0:T(1,128)S(1)}, f32[1,1024]{1,0:T(1,128)}, u32[]{:S(2)}) copy-start(f32[1,1024]{1,0:T(1,128)} %get-tuple-element.133.head_ref) | copy-start | bytes 12292 | tf_op jit(solution)/shard_map/cond
  61.1 9.9 %collective-permute-start.2 = (bf16[32,1152]{1,0:T(8,128)(2,1)S(1)}, bf16[32,1152]{1,0:T(8,128)(2,1)S(1)}, u32[]{:S(2)}, u32[]{:S(2)}) collective-permute-start(bf16[32,1152]{1,0:T(8,128)(2,1)S(1)} %get-tuple-element.148), channel_id=1, source_target_pairs={{256,384},{257,385},{258,386},{259,387},{260,388},{261,389},{262,3... | collective-permute-start | bytes 221192 | tf_op jit(solution)/shard_map/ppermute | solution.py:414

commit v5 on v4

--- a/solution.py
+++ b/solution.py
@@ -23,7 +23,7 @@
     return pl.pallas_call(
         kernel,
         out_shape=out_shape,
-        out_specs=(vmem, scalar) if smem_out else (vmem,) * len(out_shape) if many else vmem,
+        out_specs=(vmem,) * (len(out_shape) - 1) + (scalar,) if smem_out else (vmem,) * len(out_shape) if many else vmem,
         in_specs=specs,
         scratch_shapes=[*scratch, *([pltpu.SemaphoreType.DMA((sems,))] if sems else [])],
         cost_estimate=pl.CostEstimate(flops=flops, transcendentals=0, bytes_accessed=0),
@@ -65,11 +65,21 @@
 
 
 def request_kernel(sec_ref, user_ref, dense_ref, owner_hbm, row_hbm, table_hbm, first_hbm, second_hbm,
-                   req_ref, slot_ref, spot_ref, table_ref, owner_ref, row_ref, first_ref, second_ref, sem):
+                   weight_hbm, proj_hbm, into_hbm, out_of_hbm,
+                   req_ref, slot_ref, spot_ref, table_ref, weight_ref, proj_ref, into_ref, out_of_ref,
+                   owner_ref, row_ref, first_ref, second_ref, sem):
     moves = copies((owner_hbm, row_hbm, first_hbm, second_hbm, table_hbm),
                    (owner_ref, row_ref, first_ref, second_ref, table_ref), sem)
     for move in moves:
         move.start()
+    later = [pltpu.make_async_copy(a, b, sem.at[5 + i]) for i, (a, b) in enumerate((
+        (weight_hbm, weight_ref), (proj_hbm, proj_ref), (into_hbm, into_ref), (out_of_hbm, out_of_ref)))]
+
+    @pl.when(dense_ref[0] == 0)
+    def _():
+        for move in later:
+            move.start()
+
     shards = req_ref.shape[0]
     cands = owner_ref.shape[1]
     final = second_ref.shape[1]
@@ -125,6 +135,8 @@
         over = jnp.max(rank, axis=0, keepdims=True) >= slots // 2
         mark = jnp.where(mine & over, MARK, 0)
         req_ref[...] = (dot(turned, high) * 16.0 + dot(turned, low)).astype(jnp.int32) + mark
+        for move in later:
+            move.wait()
 
     moves[4].wait()
 
@@ -163,61 +175,54 @@
     served_rows(ids_ref, table_ref, out_ref, 16)
 
 
-def serve_short_kernel(ids_ref, table_ref, out_ref, over_ref):
+def serve_short_kernel(sec_ref, ids_ref, table_ref, dense_ref, weight_ref, head_ref, proj_ref,
+                       out_ref, vec_ref, over_ref):
     over_ref[0] = jnp.max(ids_ref[...])
     served_rows(ids_ref, table_ref, out_ref, 8)
 
-
-def nothing_kernel(*refs):
-    pass
-
-
-def prepare_kernel(sec_ref, in_hbm, out_hbm, weight_hbm, proj_hbm, dense_ref, head_ref,
-                   vec_ref, in_ref, out_ref, weight_ref, proj_ref, sem):
     @pl.when(sec_ref[0] == 0)
     def _():
-        moves = copies((in_hbm, out_hbm, weight_hbm, proj_hbm), (in_ref, out_ref, weight_ref, proj_ref), sem)
-        for move in moves:
-            move.start()
-        for move in moves:
-            move.wait()
         active = jax.nn.relu(dot(dense_ref[...], weight_ref[...]))
         query = (active * head_ref[...]).astype(BF16)
         vec_ref[...] = dot(query, proj_ref[...])
 
 
+def nothing_kernel(*refs):
+    pass
+
+
 def as_row(col, lanes):
     n = col.shape[0]
     return jnp.sum(jnp.where(iota((n, lanes), 0) == iota((n, lanes), 1), col, 0.0), axis=0, keepdims=True)
 
 
-def tower_kernel(sec_ref, spot_ref, rows_ref, vec_ref, in_ref, out_ref, packet_ref, score_ref):
+def survivors_kernel(sec_ref, feat_hbm, item_hbm, spot_ref, rows_ref, vec_ref, into_ref, out_of_ref,
+                     packet_ref, score_ref, part_ref, item_ref, feat_ref, sem):
+    n = part_ref.shape[0]
+    slots = rows_ref.shape[0] // 128
+    spot = spot_ref[...]
+    spot = (spot >> 4) * slots + (spot & 15)
+
     @pl.when(sec_ref[0] == 0)
     def _():
-        n = packet_ref.shape[0] // 2
-        embed = picked(spot_ref[:n, :], halves(rows_ref[...]))
-        hidden = jax.nn.relu(dot(embed, in_ref[...])).astype(BF16)
-        tower = dot(hidden, out_ref[...]).astype(BF16)
+        embed = picked(spot[:n, :], halves(rows_ref[...]))
+        hidden = jax.nn.relu(dot(embed, into_ref[...])).astype(BF16)
+        tower = dot(hidden, out_of_ref[...]).astype(BF16)
         logit = jnp.sum(tower.astype(F32) * vec_ref[...], axis=1, keepdims=True)
         packet_ref[:n, :] = tower
         packet_ref[n:, :] = jnp.broadcast_to(logit, (n, 128)).astype(BF16)
         score_ref[...] = as_row(logit, n)
 
-
-def features_kernel(sec_ref, feat_hbm, item_hbm, weight_hbm, spot_ref, rows_ref,
-                    part_ref, item_ref, weight_ref, feat_ref, sem):
     @pl.when(sec_ref[0] == 1)
     def _():
-        n = part_ref.shape[0]
-        moves = copies((feat_hbm, item_hbm, weight_hbm), (feat_ref, item_ref, weight_ref), sem)
+        moves = copies((feat_hbm, item_hbm), (feat_ref, item_ref), sem)
         for move in moves:
             move.start()
-        embed = picked(spot_ref[:4 * n, :], halves(rows_ref[...]))
+        embed = picked(spot[:4 * n, :], halves(rows_ref[...]))
         tall = jnp.concatenate([embed[f * n:(f + 1) * n, :] for f in range(4)], axis=1)
-        moves[0].wait()
+        for move in moves:
+            move.wait()
         part_ref[...] = dot(tall, feat_ref[...])
-        for move in moves[1:]:
-            move.wait()
 
 
 def gram_kernel(sec_ref, weight_hbm, slot_ref, rows_ref, head_ref, part_ref, weight_ref, sem):
@@ -330,19 +335,21 @@
     weight, feat, item, into, out_of, proj = in_hbm(
         section_weight[0], prerank_feat, prerank_item, item_in, item_out, user_proj)
 
-    request, slot, spot, table = call(
+    request, slot, spot, table, weight_near, proj_near, into_near, out_of_near = call(
         request_kernel,
-        (shape((shards, 128), jnp.int32), shape((1, cands), jnp.int32), shape((128, 128), jnp.int32), like(tables[0])),
-        sec, user, dense.astype(jnp.int32).reshape(1), *in_hbm(feat_owner.reshape(1, cands), feat_row.reshape(1, cands), tables[0], keep_first, keep_second),
-        smem=3, hbm=5, sems=5, flops=10**8,
+        (shape((shards, 128), jnp.int32), shape((1, cands), jnp.int32), shape((128, 128), jnp.int32), like(tables[0]),
+         like(weight), like(proj), like(into), like(out_of)),
+        sec, user, dense.astype(jnp.int32).reshape(1),
+        *in_hbm(feat_owner.reshape(1, cands), feat_row.reshape(1, cands), tables[0], keep_first, keep_second),
+        weight, proj, into, out_of,
+        smem=3, hbm=9, sems=9, flops=10**8,
         scratch=[pltpu.VMEM(s, jnp.int32) for s in ((1, cands), (1, cands), keep_first.shape, keep_second.shape)],
     )
     asked = lax.all_to_all(request.reshape(shards, 1, 128), "shard", 0, 0, tiled=True).reshape(shards, 128)
 
     def exchanged(served):
         rows = lax.all_to_all(served.reshape(shards, -1, width), "shard", 0, 0, tiled=True)
-        rows = jnp.pad(rows, ((0, 0), (0, slots - rows.shape[1]), (0, 0)))
-        return rows.reshape(spots, width)
+        return rows.reshape(-1, width)
 
     def serve():
         return call(serve_kernel, shape((spots, width), BF16), asked, table, flops=10**9)
@@ -360,37 +367,24 @@
     carried = shape((final, hid + 128), BF16)
 
     def sparse_sections():
-        served, over = call(
+        served, query, over = call(
             serve_short_kernel,
-            (shape((spots // 2, width), BF16), jax.ShapeDtypeStruct((1,), jnp.int32)),
-            asked, table, flops=10**9, smem_out=True,
+            (shape((spots // 2, width), BF16), shape((1, width), F32), jax.ShapeDtypeStruct((1,), jnp.int32)),
+            sec, asked, table, user_dense, weight_near, section_head, proj_near,
+            smem=1, flops=10**9, smem_out=True,
         )
 
-        def with_query(given):
-            rows = exchanged(given)
-            query = call(
-                prepare_kernel,
-                (shape((1, width), F32), like(item_in), like(item_out)),
-                sec, into, out_of, weight, proj, user_dense, section_head,
-                smem=1, hbm=4, sems=4, flops=10**9,
-                scratch=[pltpu.VMEM(weight.shape, BF16), pltpu.VMEM(user_proj.shape, BF16)],
-            )
-            return rows, *query
-
-        rows, *query = lax.cond(over[0] >= MARK, lambda: with_query(serve()), lambda: with_query(served))
-        packet, score0 = call(
-            tower_kernel,
-            (shape((2 * final, width), BF16), scored),
-            sec, spot, rows, *query,
-            smem=1, flops=10**6,
-        )
+        def survivors(given):
+            return tuple(call(
+                survivors_kernel,
+                (shape((2 * final, width), BF16), scored, shape((final, hid), F32), like(prerank_item)),
+                sec, feat, item, spot, exchanged(given), query, into_near, out_of_near,
+                smem=1, hbm=2, sems=2, scratch=[pltpu.VMEM(prerank_feat.shape, BF16)], flops=10**8,
+            ))
+
+        packet, score0, pre, item_near = lax.cond(
+            over[0] >= MARK, lambda: survivors(serve()), lambda: survivors(served))
         packet = lax.ppermute(packet, "section", [(0, 1)])
-        pre, item_near, weight_near = call(
-            features_kernel,
-            (shape((final, hid), F32), like(prerank_item), like(weight)),
-            sec, feat, item, weight, spot, rows,
-            smem=1, hbm=3, sems=3, scratch=[pltpu.VMEM(prerank_feat.shape, BF16)], flops=10**8,
-        )
         carry, score1 = call(
             prerank_kernel,
             (carried, scored),

time: 72.1 us -> 71.3 us (0.989)
  waiting for transfers between devices: 8.6 us -> 7.8 us
    ppermute x1, waiting for transfers between devices: 8.59 us -> 7.79 us  [cascade(): last = lax.ppermute(carry, 'section', [(2, 3)])]
where the time goes in v5:
time: 71.3 us; the launch traced here: 71 us
  blocking collectives  55 us (77%)
  waiting for transfers between devices  7.8 us (11%)
  Pallas kernels  5.94 us (8%)
  starting transfers between devices  1.95 us (3%)
    all_to_all x1, blocking collectives, cascade(): lax.all_to_all(request.reshape(shards, 1, 128), 'shard', 0, 0, tiled=True)  28.8 us
    all_to_all x1, blocking collectives, exchanged(): lax.all_to_all(served.reshape(shards, -1, width), 'shard', 0, 0, tiled=True)  26.2 us
    ppermute x1, waiting for transfers between devices, cascade(): last = lax.ppermute(carry, 'section', [(2, 3)])  7.79 us
    pallas_call x5, Pallas kernels, call(): pl.pallas_call(kernel, out_shape=out_shape, out_specs=(vmem,) * (len(out_...  5.94 us
  transfers between devices with their start and end apart: 2, of which 1 were waited for; matrix products, arithmetic and copies ran while one was open for 0% of the time, Pallas kernels for 5%

profile of v5, /device:TPU:6, one launch (start us, length us, event | category | flops | bytes accessed | tf_op | source)
XLA Modules:
  0.0 71.0 jit_solution(13999685820972866263)
XLA Ops:
  0.0 0.0 copy-start
  0.0 0.0 copy-start.1
  0.0 1.3 %shard_map.130 = (s32[128,128]{1,0:T(8,128)S(1)}, s32[1,1024]{1,0:T(1,128)S(1)}, s32[128,128]{1,0:T(8,128)S(1)}, bf16[2048,128]{1,0:T(8,128)(2,1)S(1)}, bf16[102...) custom-call(s32[1]{0:T(128)} %bitcast.7.sec_ref, ...), custom_call_target="tpu_custom_call" | custom-call | flops 100000000 | tf_op jit(solution)/shard_map/pallas_call | solution.py:23
  1.4 28.8 %all_to_all.20 = s32[128,1,128]{2,1,0:T(1,128)S(1)} all-to-all(s32[128,1,128]{2,1,0:T(1,128)S(1)} %bitcast.25), channel_id=1, replica_groups=mesh['section'=4,'shard'=128] {'shard'}, dimensions={0} | all-to-all | bytes 131072 | tf_op jit(solution)/shard_map/all_to_all | solution.py:348
  30.2 0.0 copy-done
  30.2 0.0 copy-done.1
  30.2 0.7 collective-permute-start.1
  30.9 30.3 %conditional.4 = (f32[40,1024]{1,0:T(8,128)S(1)}) conditional(s32[]{:T(128)} %convert_element_type.11, s32[128,128]{1,0:T(8,128)S(1)} %bitcast.30, (s32[128,128]{1,0:T(8,128)S(1)}, bf16[2048,128]{1,0:T(8,128)(2,1)S(1)}, s32[1]{0:T(128)}, bf16[1024,1024]{1,0:T(8,128)(2,1)}, s32[1,1024]{1,0:T(1,128)S(1)}, /*index=5*/f32[1,1024]{1,0:T(1,128)S(1)}) %tuple.40), branch_computations={%region_4.0_spmd, %region_5.0_spmd} | conditional | flops 2000000000 | bytes 1048584 | solution.py:406
  30.9 1.4 %branch_1_fun.8 = bf16[2048,128]{1,0:T(8,128)(2,1)S(1)} custom-call(s32[128,128]{1,0:T(8,128)S(1)} %get-tuple-element.121.ids_ref, bf16[2048,128]{1,0:T(8,128)(2,1)S(1)} %get-tuple-element.122.table_ref), custom_call_target="tpu_custom_call" | custom-call | flops 1000000000 | tf_op jit(solution)/shard_map/cond/branch_1_fun/pallas_call | solution.py:23
  32.3 26.2 %all_to_all.19 = bf16[128,16,128]{2,1,0:T(8,128)(2,1)S(1)} all-to-all(bf16[128,16,128]{2,1,0:T(8,128)(2,1)S(1)} %bitcast.23), channel_id=1, replica_groups=mesh['section'=4,'shard'=128] {'shard'}, dimensions={0} | all-to-all | bytes 1048576 | tf_op jit(solution)/shard_map/cond/branch_1_fun/all_to_all | solution.py:351
  58.4 2.5 %branch_1_fun.9 = f32[40,1024]{1,0:T(8,128)S(1)} custom-call(s32[1]{0:T(128)} %get-tuple-element.118.sec_ref, bf16[1024,1024]{1,0:T(8,128)(2,1)} %get-tuple-element.119.weight_hbm, s32[1,1024]{1,0:T(1,128)S(1)} %get-tuple-element.120.slot_ref, bf16[2048,128]{1,0:T(8,128)(2,1)S(1)} %bitcast.21, f32[1,1024]{1,0:T(1,128)S(1)} %get-tuple-element.123.head_ref), custom_call_target="tpu_custom_call" | custom-call | flops 1000000000 | tf_op jit(solution)/shard_map/cond/branch_1_fun/pallas_call | solution.py:23
  61.2 0.0 collective-permute-done.1.near_ref
  61.2 1.3 %collective-permute-start.2 = (bf16[32,1152]{1,0:T(8,128)(2,1)S(1)}, bf16[32,1152]{1,0:T(8,128)(2,1)S(1)}, u32[]{:S(2)}, u32[]{:S(2)}) collective-permute-start(bf16[32,1152]{1,0:T(8,128)(2,1)S(1)} %get-tuple-element.146), channel_id=1, source_target_pairs={{256,384},{257,385},{258,386},{259,387},{260,388},{261,389},{262,3... | collective-permute-start | bytes 221192 | tf_op jit(solution)/shard_map/ppermute | solution.py:408
  62.5 7.8 %collective-permute-done.2.last_ref = bf16[32,1152]{1,0:T(8,128)(2,1)S(1)} collective-permute-done((bf16[32,1152]{1,0:T(8,128)(2,1)S(1)}, bf16[32,1152]{1,0:T(8,128)(2,1)S(1)}, u32[]{:S(2)}, u32[]{:S(2)}) %collective-permute-start.2) | collective-permute-done | bytes 73760 | tf_op jit(solution)/shard_map/ppermute | solution.py:408
  70.3 0.7 %shard_map.132 = f32[1,32]{1,0:T(1,128)} custom-call(s32[1]{0:T(128)} %bitcast.7.sec_ref, bf16[32,1152]{1,0:T(8,128)(2,1)S(1)} %collective-permute-done.2.last_ref, f32[40,1024]{1,0:T(8,128)S(1)} %get-tuple-element.172.part_ref, f32[1,32]{1,0:T(1,128)S(1)} %get-tuple-element.147.score0_ref, f32[1,32]{1,0:T(1,128)S(1)} %get-tuple-element.148.score1_ref, ...), custom_call_target="tpu_custom_call" | custom-call | flops 1000000 | tf_op jit(solution)/shard_map/pallas_call | solution.py:23
  (3 shorter events, 0.0 us)
Async XLA Ops:
  0.0 30.2 %copy-start = (f32[1,1024]{1,0:T(1,128)S(1)}, f32[1,1024]{1,0:T(1,128)}, u32[]{:S(2)}) copy-start(f32[1,1024]{1,0:T(1,128)} %param.26) | copy-start | bytes 12292
  0.0 30.2 %copy-start.1 = (bf16[1,1024]{1,0:T(2,128)(2,1)S(1)}, bf16[1,1024]{1,0:T(2,128)(2,1)}, u32[]{:S(2)}) copy-start(bf16[1,1024]{1,0:T(2,128)(2,1)} %param.19) | copy-start | bytes 6148
  30.2 31.0 %collective-permute-start.1 = (bf16[32,1152]{1,0:T(8,128)(2,1)S(1)}, bf16[32,1152]{1,0:T(8,128)(2,1)S(1)}, u32[]{:S(2)}, u32[]{:S(2)}) collective-permute-start(bf16[32,1152]{1,0:T(8,128)(2,1)S(1)} %get-tuple-element.144), channel_id=1, source_target_pairs={{128,256},{129,257},{130,258},{131,259},{132,260},{133,261},{134,2... | collective-permute-start | bytes 221192 | tf_op jit(solution)/shard_map/ppermute | solution.py:405
  61.2 9.1 %collective-permute-start.2 = (bf16[32,1152]{1,0:T(8,128)(2,1)S(1)}, bf16[32,1152]{1,0:T(8,128)(2,1)S(1)}, u32[]{:S(2)}, u32[]{:S(2)}) collective-permute-start(bf16[32,1152]{1,0:T(8,128)(2,1)S(1)} %get-tuple-element.146), channel_id=1, source_target_pairs={{256,384},{257,385},{258,386},{259,387},{260,388},{261,389},{262,3... | collective-permute-start | bytes 221192 | tf_op jit(solution)/shard_map/ppermute | solution.py:408

commit v6 on v5

--- a/solution.py
+++ b/solution.py
@@ -64,28 +64,17 @@
     return jnp.sum(jnp.where(lanes == at, row.astype(F32), 0.0), axis=1, keepdims=True)
 
 
-def request_kernel(sec_ref, user_ref, dense_ref, owner_hbm, row_hbm, table_hbm, first_hbm, second_hbm,
-                   weight_hbm, proj_hbm, into_hbm, out_of_hbm,
-                   req_ref, slot_ref, spot_ref, table_ref, weight_ref, proj_ref, into_ref, out_of_ref,
-                   owner_ref, row_ref, first_ref, second_ref, sem):
+def request_kernel(user_ref, zero_ref, one_ref, dense_ref, owner_hbm, row_hbm, table_hbm, first_hbm, second_hbm,
+                   req_ref, slot_ref, spot_ref, table_ref, owner_ref, row_ref, first_ref, second_ref, sem):
     moves = copies((owner_hbm, row_hbm, first_hbm, second_hbm, table_hbm),
                    (owner_ref, row_ref, first_ref, second_ref, table_ref), sem)
     for move in moves:
         move.start()
-    later = [pltpu.make_async_copy(a, b, sem.at[5 + i]) for i, (a, b) in enumerate((
-        (weight_hbm, weight_ref), (proj_hbm, proj_ref), (into_hbm, into_ref), (out_of_hbm, out_of_ref)))]
-
-    @pl.when(dense_ref[0] == 0)
-    def _():
-        for move in later:
-            move.start()
-
     shards = req_ref.shape[0]
     cands = owner_ref.shape[1]
     final = second_ref.shape[1]
     slots = 2 * cands // shards
     base = (user_ref[0] % (128 // slots)) * slots
-    sec = sec_ref[0]
     for move in moves[:4]:
         move.wait()
 
@@ -110,7 +99,7 @@
         low = jnp.where(at_slot, (row & 15).astype(F32), 0.0).astype(BF16)
         req_ref[...] = (dot_nt(hot, high) * 16.0 + dot_nt(hot, low)).astype(jnp.int32)
 
-    @pl.when(dense_ref[0] == 0)
+    @pl.when(zero_ref[0] + one_ref[0] > 0)
     def _():
         second = jnp.concatenate([second_ref[...], jnp.zeros((1, 128 - final), jnp.int32)], axis=1)
         second = column(second.astype(F32))[:final, :1]
@@ -118,7 +107,7 @@
         fours = [second * 4.0 + float(f) for f in range(4)]
         none = jnp.full((final, 1), -1.0, F32)
         at = jnp.concatenate(
-            [jnp.where(sec == 0, single if f == 0 else none, fours[f]) for f in range(4)], axis=0)
+            [jnp.where(zero_ref[0] == 1, single if f == 0 else none, fours[f]) for f in range(4)], axis=0)
         owner = lookup(at, owner_ref[...] + 1) - 1.0
         row = lookup(at, row_ref[...]).astype(jnp.int32)
         count = at.shape[0]
@@ -135,8 +124,6 @@
         over = jnp.max(rank, axis=0, keepdims=True) >= slots // 2
         mark = jnp.where(mine & over, MARK, 0)
         req_ref[...] = (dot(turned, high) * 16.0 + dot(turned, low)).astype(jnp.int32) + mark
-        for move in later:
-            move.wait()
 
     moves[4].wait()
 
@@ -175,20 +162,38 @@
     served_rows(ids_ref, table_ref, out_ref, 16)
 
 
-def serve_short_kernel(sec_ref, ids_ref, table_ref, dense_ref, weight_ref, head_ref, proj_ref,
-                       out_ref, vec_ref, over_ref):
+def serve_zero_kernel(weight_hbm, proj_hbm, into_hbm, out_of_hbm, ids_ref, table_ref, dense_ref, head_ref,
+                      out_ref, vec_ref, into_ref, out_of_ref, over_ref, weight_ref, proj_ref, sem):
+    moves = copies((weight_hbm, proj_hbm, into_hbm, out_of_hbm), (weight_ref, proj_ref, into_ref, out_of_ref), sem)
+    for move in moves:
+        move.start()
     over_ref[0] = jnp.max(ids_ref[...])
     served_rows(ids_ref, table_ref, out_ref, 8)
-
-    @pl.when(sec_ref[0] == 0)
-    def _():
-        active = jax.nn.relu(dot(dense_ref[...], weight_ref[...]))
-        query = (active * head_ref[...]).astype(BF16)
-        vec_ref[...] = dot(query, proj_ref[...])
+    for move in moves:
+        move.wait()
+    active = jax.nn.relu(dot(dense_ref[...], weight_ref[...]))
+    query = (active * head_ref[...]).astype(BF16)
+    vec_ref[...] = dot(query, proj_ref[...])
+
+
+def serve_one_kernel(weight_hbm, item_hbm, ids_ref, table_ref, out_ref, weight_ref, item_ref, over_ref, sem):
+    moves = copies((weight_hbm, item_hbm), (weight_ref, item_ref), sem)
+    for move in moves:
+        move.start()
+    over_ref[0] = jnp.max(ids_ref[...])
+    served_rows(ids_ref, table_ref, out_ref, 8)
+    for move in moves:
+        move.wait()
 
 
 def nothing_kernel(*refs):
     pass
+
+
+def copy_kernel(*refs):
+    half = len(refs) // 2
+    for from_ref, to_ref in zip(refs[:half], refs[half:]):
+        to_ref[...] = from_ref[...]
 
 
 def as_row(col, lanes):
@@ -196,33 +201,30 @@
     return jnp.sum(jnp.where(iota((n, lanes), 0) == iota((n, lanes), 1), col, 0.0), axis=0, keepdims=True)
 
 
-def survivors_kernel(sec_ref, feat_hbm, item_hbm, spot_ref, rows_ref, vec_ref, into_ref, out_of_ref,
-                     packet_ref, score_ref, part_ref, item_ref, feat_ref, sem):
+def survivors(spot, rows):
+    slots = rows.shape[0] // 128
+    return picked((spot >> 4) * slots + (spot & 15), halves(rows))
+
+
+def tower_kernel(spot_ref, rows_ref, vec_ref, into_ref, out_of_ref, packet_ref, score_ref):
+    n = packet_ref.shape[0] // 2
+    embed = survivors(spot_ref[:n, :], rows_ref[...])
+    hidden = jax.nn.relu(dot(embed, into_ref[...])).astype(BF16)
+    tower = dot(hidden, out_of_ref[...]).astype(BF16)
+    logit = jnp.sum(tower.astype(F32) * vec_ref[...], axis=1, keepdims=True)
+    packet_ref[:n, :] = tower
+    packet_ref[n:, :] = jnp.broadcast_to(logit, (n, 128)).astype(BF16)
+    score_ref[...] = as_row(logit, n)
+
+
+def features_kernel(feat_hbm, spot_ref, rows_ref, part_ref, feat_ref, sem):
+    move = pltpu.make_async_copy(feat_hbm, feat_ref, sem.at[0])
+    move.start()
     n = part_ref.shape[0]
-    slots = rows_ref.shape[0] // 128
-    spot = spot_ref[...]
-    spot = (spot >> 4) * slots + (spot & 15)
-
-    @pl.when(sec_ref[0] == 0)
-    def _():
-        embed = picked(spot[:n, :], halves(rows_ref[...]))
-        hidden = jax.nn.relu(dot(embed, into_ref[...])).astype(BF16)
-        tower = dot(hidden, out_of_ref[...]).astype(BF16)
-        logit = jnp.sum(tower.astype(F32) * vec_ref[...], axis=1, keepdims=True)
-        packet_ref[:n, :] = tower
-        packet_ref[n:, :] = jnp.broadcast_to(logit, (n, 128)).astype(BF16)
-        score_ref[...] = as_row(logit, n)
-
-    @pl.when(sec_ref[0] == 1)
-    def _():
-        moves = copies((feat_hbm, item_hbm), (feat_ref, item_ref), sem)
-        for move in moves:
-            move.start()
-        embed = picked(spot[:4 * n, :], halves(rows_ref[...]))
-        tall = jnp.concatenate([embed[f * n:(f + 1) * n, :] for f in range(4)], axis=1)
-        for move in moves:
-            move.wait()
-        part_ref[...] = dot(tall, feat_ref[...])
+    embed = survivors(spot_ref[:4 * n, :], rows_ref[...])
+    tall = jnp.concatenate([embed[f * n:(f + 1) * n, :] for f in range(4)], axis=1)
+    move.wait()
+    part_ref[...] = dot(tall, feat_ref[...])
 
 
 def gram_kernel(sec_ref, weight_hbm, slot_ref, rows_ref, head_ref, part_ref, weight_ref, sem):
@@ -329,20 +331,18 @@
     final = keep_second.shape[1]
     sec = lax.axis_index("section").reshape(1).astype(jnp.int32)
     user = lax.axis_index("shard").reshape(1).astype(jnp.int32)
-    dense = sec[0] >= 2
+    turns = [sec[0] == 0, sec[0] == 1, sec[0] >= 2]
     like = lambda a: shape(a.shape, a.dtype)
 
     weight, feat, item, into, out_of, proj = in_hbm(
         section_weight[0], prerank_feat, prerank_item, item_in, item_out, user_proj)
 
-    request, slot, spot, table, weight_near, proj_near, into_near, out_of_near = call(
+    request, slot, spot, table = call(
         request_kernel,
-        (shape((shards, 128), jnp.int32), shape((1, cands), jnp.int32), shape((128, 128), jnp.int32), like(tables[0]),
-         like(weight), like(proj), like(into), like(out_of)),
-        sec, user, dense.astype(jnp.int32).reshape(1),
+        (shape((shards, 128), jnp.int32), shape((1, cands), jnp.int32), shape((128, 128), jnp.int32), like(tables[0])),
+        user, *(turn.astype(jnp.int32).reshape(1) for turn in turns),
         *in_hbm(feat_owner.reshape(1, cands), feat_row.reshape(1, cands), tables[0], keep_first, keep_second),
-        weight, proj, into, out_of,
-        smem=3, hbm=9, sems=9, flops=10**8,
+        smem=4, hbm=5, sems=5, flops=10**8,
         scratch=[pltpu.VMEM(s, jnp.int32) for s in ((1, cands), (1, cands), keep_first.shape, keep_second.shape)],
     )
     asked = lax.all_to_all(request.reshape(shards, 1, 128), "shard", 0, 0, tiled=True).reshape(shards, 128)
@@ -366,32 +366,39 @@
     scored = shape((1, final), F32)
     carried = shape((final, hid + 128), BF16)
 
-    def sparse_sections():
-        served, query, over = call(
-            serve_short_kernel,
-            (shape((spots // 2, width), BF16), shape((1, width), F32), jax.ShapeDtypeStruct((1,), jnp.int32)),
-            sec, asked, table, user_dense, weight_near, section_head, proj_near,
-            smem=1, flops=10**9, smem_out=True,
+    def either(over, served, then):
+        return lax.cond(over[0] >= MARK, lambda: then(exchanged(serve())), lambda: then(exchanged(served)))
+
+    def kept(*arrays):
+        return tuple(call(copy_kernel, tuple(like(a) for a in arrays), *arrays))
+
+    short = shape((spots // 2, width), BF16)
+    scalar = jax.ShapeDtypeStruct((1,), jnp.int32)
+    packed = shape((2 * final, width), BF16)
+    product = shape((final, hid), F32)
+
+    def section_zero():
+        served, query, into_near, out_of_near, over = call(
+            serve_zero_kernel,
+            (short, shape((1, width), F32), like(into), like(out_of), scalar),
+            weight, proj, into, out_of, asked, table, user_dense, section_head,
+            hbm=4, sems=4, flops=10**9, smem_out=True,
+            scratch=[pltpu.VMEM(weight.shape, BF16), pltpu.VMEM(proj.shape, BF16)],
         )
-
-        def survivors(given):
-            return tuple(call(
-                survivors_kernel,
-                (shape((2 * final, width), BF16), scored, shape((final, hid), F32), like(prerank_item)),
-                sec, feat, item, spot, exchanged(given), query, into_near, out_of_near,
-                smem=1, hbm=2, sems=2, scratch=[pltpu.VMEM(prerank_feat.shape, BF16)], flops=10**8,
-            ))
-
-        packet, score0, pre, item_near = lax.cond(
-            over[0] >= MARK, lambda: survivors(serve()), lambda: survivors(served))
-        packet = lax.ppermute(packet, "section", [(0, 1)])
-        carry, score1 = call(
-            prerank_kernel,
-            (carried, scored),
-            sec, packet, pre, item_near, weight_near, section_head,
-            smem=1, flops=10**8,
+        return kept(*either(over, served, lambda rows: tuple(call(
+            tower_kernel, (packed, scored), spot, rows, query, into_near, out_of_near, flops=10**7))))
+
+    def section_one():
+        served, weight_near, item_near, over = call(
+            serve_one_kernel,
+            (short, like(weight), like(item), scalar),
+            weight, item, asked, table,
+            hbm=2, sems=2, flops=10**9, smem_out=True,
         )
-        return carry, score0, score1
+        product_near = either(over, served, lambda rows: call(
+            features_kernel, product, feat, spot, rows,
+            hbm=1, sems=1, scratch=[pltpu.VMEM(feat.shape, BF16)], flops=10**8))
+        return *kept(product_near), weight_near, item_near
 
     def dense_sections():
         return call(
@@ -401,9 +408,18 @@
             smem=1, hbm=1, sems=1, scratch=[pltpu.VMEM(weight.shape, BF16)], flops=10**9,
         )
 
-    carry, score0, score1 = lax.cond(dense, lambda: tuple(blank(carried, scored, scored)), sparse_sections)
+    packet, score0 = lax.cond(turns[0], section_zero, lambda: tuple(blank(packed, scored)))
+    packet = lax.ppermute(packet, "section", [(0, 1)])
+    pre, weight_near, item_near = lax.cond(
+        turns[1], section_one, lambda: tuple(blank(product, like(weight), like(item))))
+    carry, score1 = call(
+        prerank_kernel,
+        (carried, scored),
+        sec, packet, pre, item_near, weight_near, section_head,
+        smem=1, flops=10**8,
+    )
     near = lax.ppermute(carry, "section", [(1, 2)])
-    part = lax.cond(dense, dense_sections, lambda: blank(shape((final + 8, hid), F32))[0])
+    part = lax.cond(turns[2], dense_sections, lambda: blank(shape((final + 8, hid), F32))[0])
     carry, score2 = call(rank_kernel, (carried, scored), sec, near, part, smem=1, flops=10**6)
     last = lax.ppermute(carry, "section", [(2, 3)])
     scores = call(

time: 71.3 us -> 69.8 us (0.979)
  waiting for transfers between devices: 7.8 us -> 5.46 us
    ppermute x1, waiting for transfers between devices: 7.79 us -> 5.45 us  [cascade(): last = lax.ppermute(carry, 'section', [(2, 3)])]
    pallas_call x5 -> x6, Pallas kernels: 5.94 us -> 5.87 us  [call(): pl.pallas_call(kernel, out_shape=out_shape, out_specs=(vmem,) * (len(out_...]
  transfers between devices with their start and end apart: 2 -> 3, of which waited for: 1 -> 1; matrix products, arithmetic and copies ran while one was open for 0% -> 0% of each run, Pallas kernels for 5% -> 6%
where the time goes in v6:
time: 69.8 us; the launch traced here: 69.5 us
  blocking collectives  54.8 us (79%)
  Pallas kernels  5.88 us (8%)
  waiting for transfers between devices  5.46 us (8%)
  starting transfers between devices  2.6 us (4%)
    all_to_all x1, blocking collectives, cascade(): lax.all_to_all(request.reshape(shards, 1, 128), 'shard', 0, 0, tiled=True)  28.8 us
    all_to_all x1, blocking collectives, exchanged(): lax.all_to_all(served.reshape(shards, -1, width), 'shard', 0, 0, tiled=True)  26 us
    pallas_call x6, Pallas kernels, call(): pl.pallas_call(kernel, out_shape=out_shape, out_specs=(vmem,) * (len(out_...  5.87 us
    ppermute x1, waiting for transfers between devices, cascade(): last = lax.ppermute(carry, 'section', [(2, 3)])  5.45 us
  transfers between devices with their start and end apart: 3, of which 1 were waited for; matrix products, arithmetic and copies ran while one was open for 0% of the time, Pallas kernels for 6%

profile of v6, /device:TPU:6, one launch (start us, length us, event | category | flops | bytes accessed | tf_op | source)
XLA Modules:
  0.0 69.5 jit_solution(8177379997456347415)
XLA Ops:
  0.0 1.3 %shard_map.133 = (s32[128,128]{1,0:T(8,128)S(1)}, s32[1,1024]{1,0:T(1,128)S(1)}, s32[128,128]{1,0:T(8,128)S(1)}, bf16[2048,128]{1,0:T(8,128)(2,1)S(1)}) custom-call(s32[1]{0:T(128)} %bitcast.13.user_ref, s32[1]{0:T(128)} %bitcast.14.zero_ref, s32[1]{0:T(128)} %bitcast.15.one_ref, s32[1]{0:T(128)} %bitcast.16.dense_ref, s32[1,1024]{1,0:T(1,128)} %bitcast.44, ...), custom_call_target="tpu_custom_call" | custom-call | flops 100000000 | tf_op jit(solution)/shard_map/pallas_call | solution.py:23
  1.3 28.8 %all_to_all.30 = s32[128,1,128]{2,1,0:T(1,128)S(1)} all-to-all(s32[128,1,128]{2,1,0:T(1,128)S(1)} %bitcast.36), channel_id=1, replica_groups=mesh['section'=4,'shard'=128] {'shard'}, dimensions={0} | all-to-all | bytes 131072 | tf_op jit(solution)/shard_map/all_to_all | solution.py:348
  30.1 0.7 collective-permute-start
  30.8 0.0 copy-start
  30.8 0.2 conditional.6
  31.1 0.0 collective-permute-done.packet_ref
  31.1 0.4 copy-done
  31.5 0.7 collective-permute-start.1
  32.1 29.9 %conditional.7 = (f32[40,1024]{1,0:T(8,128)S(1)}) conditional(s32[]{:T(128)} %convert_element_type.26, s32[128,128]{1,0:T(8,128)S(1)} %bitcast.41, (s32[128,128]{1,0:T(8,128)S(1)}, bf16[2048,128]{1,0:T(8,128)(2,1)S(1)}, s32[1]{0:T(128)}, bf16[1024,1024]{1,0:T(8,128)(2,1)}, s32[1,1024]{1,0:T(1,128)S(1)}, /*index=5*/f32[1,1024]{1,0:T(1,128)S(1)}) %tuple.61), branch_computations={%region_8.0_spmd, %region_9.0_spmd} | conditional | flops 2000000000 | bytes 1048584 | solution.py:422
  32.2 1.3 %branch_1_fun.18 = bf16[2048,128]{1,0:T(8,128)(2,1)S(1)} custom-call(s32[128,128]{1,0:T(8,128)S(1)} %get-tuple-element.139.ids_ref, bf16[2048,128]{1,0:T(8,128)(2,1)S(1)} %get-tuple-element.140.table_ref), custom_call_target="tpu_custom_call" | custom-call | flops 1000000000 | tf_op jit(solution)/shard_map/cond/branch_1_fun/pallas_call | solution.py:23
  33.5 26.0 %all_to_all.29 = bf16[128,16,128]{2,1,0:T(8,128)(2,1)S(1)} all-to-all(bf16[128,16,128]{2,1,0:T(8,128)(2,1)S(1)} %bitcast.33), channel_id=1, replica_groups=mesh['section'=4,'shard'=128] {'shard'}, dimensions={0} | all-to-all | bytes 1048576 | tf_op jit(solution)/shard_map/cond/branch_1_fun/all_to_all | solution.py:351
  59.5 2.5 %branch_1_fun.19 = f32[40,1024]{1,0:T(8,128)S(1)} custom-call(s32[1]{0:T(128)} %get-tuple-element.136.sec_ref, bf16[1024,1024]{1,0:T(8,128)(2,1)} %get-tuple-element.137.weight_hbm, s32[1,1024]{1,0:T(1,128)S(1)} %get-tuple-element.138.slot_ref, bf16[2048,128]{1,0:T(8,128)(2,1)S(1)} %bitcast.30, f32[1,1024]{1,0:T(1,128)S(1)} %get-tuple-element.141.head_ref), custom_call_target="tpu_custom_call" | custom-call | flops 1000000000 | tf_op jit(solution)/shard_map/cond/branch_1_fun/pallas_call | solution.py:23
  62.0 0.0 collective-permute-done.1.near_ref
  62.1 1.3 %collective-permute-start.2 = (bf16[32,1152]{1,0:T(8,128)(2,1)S(1)}, bf16[32,1152]{1,0:T(8,128)(2,1)S(1)}, u32[]{:S(2)}, u32[]{:S(2)}) collective-permute-start(bf16[32,1152]{1,0:T(8,128)(2,1)S(1)} %get-tuple-element.164), channel_id=1, source_target_pairs={{256,384},{257,385},{258,386},{259,387},{260,388},{261,389},{262,3... | collective-permute-start | bytes 221192 | tf_op jit(solution)/shard_map/ppermute | solution.py:424
  63.4 5.5 %collective-permute-done.2.last_ref = bf16[32,1152]{1,0:T(8,128)(2,1)S(1)} collective-permute-done((bf16[32,1152]{1,0:T(8,128)(2,1)S(1)}, bf16[32,1152]{1,0:T(8,128)(2,1)S(1)}, u32[]{:S(2)}, u32[]{:S(2)}) %collective-permute-start.2) | collective-permute-done | bytes 73760 | tf_op jit(solution)/shard_map/ppermute | solution.py:424
  68.8 0.7 %shard_map.136 = f32[1,32]{1,0:T(1,128)} custom-call(s32[1]{0:T(128)} %bitcast.12.sec_ref, bf16[32,1152]{1,0:T(8,128)(2,1)S(1)} %collective-permute-done.2.last_ref, f32[40,1024]{1,0:T(8,128)S(1)} %get-tuple-element.198.part_ref, f32[1,32]{1,0:T(1,128)S(1)} %get-tuple-element.165.score0_ref, f32[1,32]{1,0:T(1,128)S(1)} %get-tuple-element.166.score1_ref, ...), custom_call_target="tpu_custom_call" | custom-call | flops 1000000 | tf_op jit(solution)/shard_map/pallas_call | solution.py:23
  (5 shorter events, 0.0 us)
Async XLA Ops:
  30.1 0.9 %collective-permute-start = (bf16[64,128]{1,0:T(8,128)(2,1)S(1)}, bf16[64,128]{1,0:T(8,128)(2,1)S(1)}, u32[]{:S(2)}, u32[]{:S(2)}) collective-permute-start(bf16[64,128]{1,0:T(8,128)(2,1)S(1)} %get-tuple-element.158), channel_id=1, source_target_pairs={{0,128},{1,129},{2,130},{3,131},{4,132},{5,133},{6,134},{7,135},{8... | collective-permute-start | bytes 49160 | tf_op jit(solution)/shard_map/ppermute | solution.py:412
  30.8 0.7 copy-start
  31.5 30.6 %collective-permute-start.1 = (bf16[32,1152]{1,0:T(8,128)(2,1)S(1)}, bf16[32,1152]{1,0:T(8,128)(2,1)S(1)}, u32[]{:S(2)}, u32[]{:S(2)}) collective-permute-start(bf16[32,1152]{1,0:T(8,128)(2,1)S(1)} %get-tuple-element.162), channel_id=1, source_target_pairs={{128,256},{129,257},{130,258},{131,259},{132,260},{133,261},{134,2... | collective-permute-start | bytes 221192 | tf_op jit(solution)/shard_map/ppermute | solution.py:421
  62.1 6.8 %collective-permute-start.2 = (bf16[32,1152]{1,0:T(8,128)(2,1)S(1)}, bf16[32,1152]{1,0:T(8,128)(2,1)S(1)}, u32[]{:S(2)}, u32[]{:S(2)}) collective-permute-start(bf16[32,1152]{1,0:T(8,128)(2,1)S(1)} %get-tuple-element.164), channel_id=1, source_target_pairs={{256,384},{257,385},{258,386},{259,387},{260,388},{261,389},{262,3... | collective-permute-start | bytes 221192 | tf_op jit(solution)/shard_map/ppermute | solution.py:424

commit v7 on v6

--- a/solution.py
+++ b/solution.py
@@ -64,10 +64,11 @@
     return jnp.sum(jnp.where(lanes == at, row.astype(F32), 0.0), axis=1, keepdims=True)
 
 
-def request_kernel(user_ref, zero_ref, one_ref, dense_ref, owner_hbm, row_hbm, table_hbm, first_hbm, second_hbm,
-                   req_ref, slot_ref, spot_ref, table_ref, owner_ref, row_ref, first_ref, second_ref, sem):
-    moves = copies((owner_hbm, row_hbm, first_hbm, second_hbm, table_hbm),
-                   (owner_ref, row_ref, first_ref, second_ref, table_ref), sem)
+def request_kernel(user_ref, zero_ref, one_ref, dense_ref, owner_hbm, row_hbm, table_hbm, first_hbm, second_hbm, head_hbm,
+                   weight_hbm, req_ref, slot_ref, spot_ref, table_ref, head_ref,
+                   owner_ref, row_ref, first_ref, second_ref, sem):
+    moves = copies((owner_hbm, row_hbm, first_hbm, second_hbm, table_hbm, head_hbm),
+                   (owner_ref, row_ref, first_ref, second_ref, table_ref, head_ref), sem)
     for move in moves:
         move.start()
     shards = req_ref.shape[0]
@@ -125,7 +126,8 @@
         mark = jnp.where(mine & over, MARK, 0)
         req_ref[...] = (dot(turned, high) * 16.0 + dot(turned, low)).astype(jnp.int32) + mark
 
-    moves[4].wait()
+    for move in moves[4:]:
+        move.wait()
 
 
 def halves(table):
@@ -162,9 +164,9 @@
     served_rows(ids_ref, table_ref, out_ref, 16)
 
 
-def serve_zero_kernel(weight_hbm, proj_hbm, into_hbm, out_of_hbm, ids_ref, table_ref, dense_ref, head_ref,
-                      out_ref, vec_ref, into_ref, out_of_ref, over_ref, weight_ref, proj_ref, sem):
-    moves = copies((weight_hbm, proj_hbm, into_hbm, out_of_hbm), (weight_ref, proj_ref, into_ref, out_of_ref), sem)
+def serve_zero_kernel(proj_hbm, into_hbm, out_of_hbm, ids_ref, table_ref, dense_ref, head_ref, weight_ref,
+                      out_ref, vec_ref, into_ref, out_of_ref, over_ref, proj_ref, sem):
+    moves = copies((proj_hbm, into_hbm, out_of_hbm), (proj_ref, into_ref, out_of_ref), sem)
     for move in moves:
         move.start()
     over_ref[0] = jnp.max(ids_ref[...])
@@ -176,14 +178,12 @@
     vec_ref[...] = dot(query, proj_ref[...])
 
 
-def serve_one_kernel(weight_hbm, item_hbm, ids_ref, table_ref, out_ref, weight_ref, item_ref, over_ref, sem):
-    moves = copies((weight_hbm, item_hbm), (weight_ref, item_ref), sem)
-    for move in moves:
-        move.start()
+def serve_one_kernel(item_hbm, ids_ref, table_ref, out_ref, item_ref, over_ref, sem):
+    move = pltpu.make_async_copy(item_hbm, item_ref, sem.at[0])
+    move.start()
     over_ref[0] = jnp.max(ids_ref[...])
     served_rows(ids_ref, table_ref, out_ref, 8)
-    for move in moves:
-        move.wait()
+    move.wait()
 
 
 def nothing_kernel(*refs):
@@ -227,37 +227,32 @@
     part_ref[...] = dot(tall, feat_ref[...])
 
 
-def gram_kernel(sec_ref, weight_hbm, slot_ref, rows_ref, head_ref, part_ref, weight_ref, sem):
-    @pl.when(sec_ref[0] >= 2)
-    def _():
-        n = part_ref.shape[0] - 8
-        cands = slot_ref.shape[1]
-        width = rows_ref.shape[1]
-        move = pltpu.make_async_copy(weight_hbm, weight_ref, sem.at[0])
-        move.start()
-        wide = halves(rows_ref[...])
-        embed = [
-            picked(jnp.concatenate([column(slot_ref[:, b:b + 128]) for b in range(h, h + 512, 128)], axis=0), wide)
-            for h in range(0, cands, 512)
-        ]
-        r, c = iota((128, 128), 0), iota((128, 128), 1)
-        same_item = (r // 32) == (c // 32)
-        spread = ones_where((r % 32) == (c % 32))
-        own_lanes = (r % 4) == (c // 32)
-        grams = []
-        for b in range(cands // 128):
-            block = embed[b // 4][b % 4 * 128:b % 4 * 128 + 128, :]
-            gram = dot_nt(block, block) * (1.0 / math.sqrt(width))
-            gram = jnp.where(same_item, gram, 0.0).astype(BF16)
-            grams.append(jnp.where(own_lanes, dot(gram, spread), 0.0).astype(BF16))
-        tall = jnp.concatenate(grams, axis=0)
-        i, k = iota((8 * n, 32 * n), 0), iota((8 * n, 32 * n), 1)
-        choose = ones_where(((k // 32) == (i % n)) & (((k % 32) // 4) == (i // n)))
-        flat = dot(choose, tall).astype(BF16)
-        flat = jnp.concatenate([flat[q * n:(q + 1) * n, :] for q in range(8)], axis=1)
-        move.wait()
-        part_ref[:n, :] = dot(flat, weight_ref[...])
-        part_ref[n:n + 1, :] = head_ref[...]
+def gram_kernel(slot_ref, rows_ref, head_ref, weight_ref, part_ref):
+    n = part_ref.shape[0] - 8
+    cands = slot_ref.shape[1]
+    width = rows_ref.shape[1]
+    wide = halves(rows_ref[...])
+    embed = [
+        picked(jnp.concatenate([column(slot_ref[:, b:b + 128]) for b in range(h, h + 512, 128)], axis=0), wide)
+        for h in range(0, cands, 512)
+    ]
+    r, c = iota((128, 128), 0), iota((128, 128), 1)
+    same_item = (r // 32) == (c // 32)
+    spread = ones_where((r % 32) == (c % 32))
+    own_lanes = (r % 4) == (c // 32)
+    grams = []
+    for b in range(cands // 128):
+        block = embed[b // 4][b % 4 * 128:b % 4 * 128 + 128, :]
+        gram = dot_nt(block, block) * (1.0 / math.sqrt(width))
+        gram = jnp.where(same_item, gram, 0.0).astype(BF16)
+        grams.append(jnp.where(own_lanes, dot(gram, spread), 0.0).astype(BF16))
+    tall = jnp.concatenate(grams, axis=0)
+    i, k = iota((8 * n, 32 * n), 0), iota((8 * n, 32 * n), 1)
+    choose = ones_where(((k // 32) == (i % n)) & (((k % 32) // 4) == (i // n)))
+    flat = dot(choose, tall).astype(BF16)
+    flat = jnp.concatenate([flat[q * n:(q + 1) * n, :] for q in range(8)], axis=1)
+    part_ref[:n, :] = dot(flat, weight_ref[...])
+    part_ref[n:n + 1, :] = head_ref[...]
 
 
 def prerank_kernel(sec_ref, packet_ref, part_ref, item_ref, weight_ref, head_ref, carry_ref, score_ref):
@@ -334,15 +329,21 @@
     turns = [sec[0] == 0, sec[0] == 1, sec[0] >= 2]
     like = lambda a: shape(a.shape, a.dtype)
 
-    weight, feat, item, into, out_of, proj = in_hbm(
-        section_weight[0], prerank_feat, prerank_item, item_in, item_out, user_proj)
-
-    request, slot, spot, table = call(
+    feat, item, into, out_of, proj = in_hbm(prerank_feat, prerank_item, item_in, item_out, user_proj)
+    weight = section_weight[0]
+
+    def weight_near():
+        return pltpu.with_memory_space_constraint(weight, pltpu.VMEM)
+
+
+    request, slot, spot, table, head = call(
         request_kernel,
-        (shape((shards, 128), jnp.int32), shape((1, cands), jnp.int32), shape((128, 128), jnp.int32), like(tables[0])),
+        (shape((shards, 128), jnp.int32), shape((1, cands), jnp.int32), shape((128, 128), jnp.int32), like(tables[0]),
+         like(section_head)),
         user, *(turn.astype(jnp.int32).reshape(1) for turn in turns),
-        *in_hbm(feat_owner.reshape(1, cands), feat_row.reshape(1, cands), tables[0], keep_first, keep_second),
-        smem=4, hbm=5, sems=5, flops=10**8,
+        *in_hbm(feat_owner.reshape(1, cands), feat_row.reshape(1, cands), tables[0], keep_first, keep_second, section_head,
+                section_weight[0]),
+        smem=4, hbm=7, sems=6, flops=10**8,
         scratch=[pltpu.VMEM(s, jnp.int32) for s in ((1, cands), (1, cands), keep_first.shape, keep_second.shape)],
     )
     asked = lax.all_to_all(request.reshape(shards, 1, 128), "shard", 0, 0, tiled=True).reshape(shards, 128)
@@ -373,7 +374,7 @@
         return tuple(call(copy_kernel, tuple(like(a) for a in arrays), *arrays))
 
     short = shape((spots // 2, width), BF16)
-    scalar = jax.ShapeDtypeStruct((1,), jnp.int32)
+    scalar = pltpu.SMEM((1,), jnp.int32)
     packed = shape((2 * final, width), BF16)
     product = shape((final, hid), F32)
 
@@ -381,43 +382,41 @@
         served, query, into_near, out_of_near, over = call(
             serve_zero_kernel,
             (short, shape((1, width), F32), like(into), like(out_of), scalar),
-            weight, proj, into, out_of, asked, table, user_dense, section_head,
-            hbm=4, sems=4, flops=10**9, smem_out=True,
-            scratch=[pltpu.VMEM(weight.shape, BF16), pltpu.VMEM(proj.shape, BF16)],
+            proj, into, out_of, asked, table, user_dense, head, weight_near(),
+            hbm=3, sems=3, flops=10**9, smem_out=True,
+            scratch=[pltpu.VMEM(proj.shape, BF16)],
         )
         return kept(*either(over, served, lambda rows: tuple(call(
             tower_kernel, (packed, scored), spot, rows, query, into_near, out_of_near, flops=10**7))))
 
     def section_one():
-        served, weight_near, item_near, over = call(
+        served, item_near, over = call(
             serve_one_kernel,
-            (short, like(weight), like(item), scalar),
-            weight, item, asked, table,
-            hbm=2, sems=2, flops=10**9, smem_out=True,
+            (short, like(item), scalar),
+            item, asked, table,
+            hbm=1, sems=1, flops=10**9, smem_out=True,
         )
         product_near = either(over, served, lambda rows: call(
             features_kernel, product, feat, spot, rows,
             hbm=1, sems=1, scratch=[pltpu.VMEM(feat.shape, BF16)], flops=10**8))
-        return *kept(product_near), weight_near, item_near
+        return *kept(product_near), item_near
 
     def dense_sections():
         return call(
-            gram_kernel,
-            shape((final + 8, hid), F32),
-            sec, weight, slot, exchanged(serve()), section_head,
-            smem=1, hbm=1, sems=1, scratch=[pltpu.VMEM(weight.shape, BF16)], flops=10**9,
-        )
-
-    packet, score0 = lax.cond(turns[0], section_zero, lambda: tuple(blank(packed, scored)))
-    packet = lax.ppermute(packet, "section", [(0, 1)])
-    pre, weight_near, item_near = lax.cond(
-        turns[1], section_one, lambda: tuple(blank(product, like(weight), like(item))))
-    carry, score1 = call(
-        prerank_kernel,
-        (carried, scored),
-        sec, packet, pre, item_near, weight_near, section_head,
-        smem=1, flops=10**8,
-    )
+            gram_kernel, shape((final + 8, hid), F32), slot, exchanged(serve()), head, weight_near(), flops=10**9)
+
+    def sparse_sections():
+        packet, score0 = lax.cond(turns[0], section_zero, lambda: tuple(blank(packed, scored)))
+        packet = lax.ppermute(packet, "section", [(0, 1)])
+        pre, item_near = lax.cond(turns[1], section_one, lambda: tuple(blank(product, like(item))))
+        return *call(
+            prerank_kernel,
+            (carried, scored),
+            sec, packet, pre, item_near, weight_near(), head,
+            smem=1, flops=10**8,
+        ), score0
+
+    carry, score1, score0 = lax.cond(turns[2], lambda: tuple(blank(carried, scored, scored)), sparse_sections)
     near = lax.ppermute(carry, "section", [(1, 2)])
     part = lax.cond(turns[2], dense_sections, lambda: blank(shape((final + 8, hid), F32))[0])
     carry, score2 = call(rank_kernel, (carried, scored), sec, near, part, smem=1, flops=10**6)

time: 69.8 us -> 68 us (0.974)
    pallas_call x6 -> x5, Pallas kernels: 5.87 us -> 5.93 us  [call(): pl.pallas_call(kernel, out_shape=out_shape, out_specs=(vmem,) * (len(out_...]
  transfers between devices with their start and end apart: 3 -> 2, of which waited for: 1 -> 1; matrix products, arithmetic and copies ran while one was open for 0% -> 0% of each run, Pallas kernels for 6% -> 6%
where the time goes in v7:
time: 68 us; the launch traced here: 67.8 us
  blocking collectives  54.8 us (81%)
  Pallas kernels  5.93 us (9%)
  waiting for transfers between devices  4.95 us (7%)
  starting transfers between devices  1.96 us (3%)
    all_to_all x1, blocking collectives, cascade(): lax.all_to_all(request.reshape(shards, 1, 128), 'shard', 0, 0, tiled=True)  28.8 us
    all_to_all x1, blocking collectives, exchanged(): lax.all_to_all(served.reshape(shards, -1, width), 'shard', 0, 0, tiled=True)  26 us
    pallas_call x5, Pallas kernels, call(): pl.pallas_call(kernel, out_shape=out_shape, out_specs=(vmem,) * (len(out_...  5.93 us
    ppermute x1, waiting for transfers between devices, cascade(): last = lax.ppermute(carry, 'section', [(2, 3)])  4.95 us
  transfers between devices with their start and end apart: 2, of which 1 were waited for; matrix products, arithmetic and copies ran while one was open for 0% of the time, Pallas kernels for 6%

profile of v7, /device:TPU:6, one launch (start us, length us, event | category | flops | bytes accessed | tf_op | source)
XLA Modules:
  0.0 67.8 jit_solution(9607851605379253991)
XLA Ops:
  0.0 0.0 copy-start
  0.0 0.0 copy-start.1
  0.0 1.4 %shard_map.133 = (s32[128,128]{1,0:T(8,128)S(1)}, s32[1,1024]{1,0:T(1,128)S(1)}, s32[128,128]{1,0:T(8,128)S(1)}, bf16[2048,128]{1,0:T(8,128)(2,1)S(1)}, f32[1,1024]{1,0:T(1,128)S(1)}) custom-call(s32[1]{0:T(128)} %bitcast.13.user_ref, s32[1]{0:T(128)} %bitcast.14.zero_ref, s32[1]{0:T(128)} %bitcast.15.one_ref, s32[1]{0:T(128)} %bitcast.16.dense_ref, ...), custom_call_target="tpu_custom_call" | custom-call | flops 100000000 | tf_op jit(solution)/shard_map/pallas_call | solution.py:23
  1.5 28.8 %all_to_all.30 = s32[128,1,128]{2,1,0:T(1,128)S(1)} all-to-all(s32[128,1,128]{2,1,0:T(1,128)S(1)} %bitcast.39), channel_id=1, replica_groups=mesh['section'=4,'shard'=128] {'shard'}, dimensions={0} | all-to-all | bytes 131072 | tf_op jit(solution)/shard_map/all_to_all | solution.py:349
  30.3 0.0 copy-done
  30.3 0.0 copy-done.1
  30.3 0.7 collective-permute-start.1
  31.0 29.8 %conditional.7 = (f32[40,1024]{1,0:T(8,128)S(1)}) conditional(s32[]{:T(128)} %convert_element_type.25, s32[128,128]{1,0:T(8,128)S(1)} %bitcast.42, (s32[128,128]{1,0:T(8,128)S(1)}, bf16[2048,128]{1,0:T(8,128)(2,1)S(1)}, s32[1,1024]{1,0:T(1,128)S(1)}, f32[1,1024]{1,0:T(1,128)S(1)}, bf16[1024,1024]{1,0:T(8,128)(2,1)S(1)}) %tuple.68), branch_computations={%region_10.0_spmd, %region_11.0_spmd} | conditional | flops 2000000000 | bytes 1048584 | solution.py:421
  31.0 1.4 %branch_1_fun.20 = bf16[2048,128]{1,0:T(8,128)(2,1)S(1)} custom-call(s32[128,128]{1,0:T(8,128)S(1)} %get-tuple-element.180.ids_ref, bf16[2048,128]{1,0:T(8,128)(2,1)S(1)} %get-tuple-element.181.table_ref), custom_call_target="tpu_custom_call" | custom-call | flops 1000000000 | tf_op jit(solution)/shard_map/cond/branch_1_fun/pallas_call | solution.py:23
  32.4 26.0 %all_to_all.29 = bf16[128,16,128]{2,1,0:T(8,128)(2,1)S(1)} all-to-all(bf16[128,16,128]{2,1,0:T(8,128)(2,1)S(1)} %bitcast.36), channel_id=1, replica_groups=mesh['section'=4,'shard'=128] {'shard'}, dimensions={0} | all-to-all | bytes 1048576 | tf_op jit(solution)/shard_map/cond/branch_1_fun/all_to_all | solution.py:352
  58.4 2.4 %branch_1_fun.21 = f32[40,1024]{1,0:T(8,128)S(1)} custom-call(s32[1,1024]{1,0:T(1,128)S(1)} %get-tuple-element.179.slot_ref, bf16[2048,128]{1,0:T(8,128)(2,1)S(1)} %bitcast.33, f32[1,1024]{1,0:T(1,128)S(1)} %get-tuple-element.182.head_ref, bf16[1024,1024]{1,0:T(8,128)(2,1)S(1)} %get-tuple-element.183.weight_ref), custom_call_target="tpu_custom_call" | custom-call | flops 1000000000 | tf_op jit(solution)/shard_map/cond/branch_1_fun/pallas_call | solution.py:23
  60.8 0.0 collective-permute-done.1.near_ref
  60.8 1.3 %collective-permute-start.2 = (bf16[32,1152]{1,0:T(8,128)(2,1)S(1)}, bf16[32,1152]{1,0:T(8,128)(2,1)S(1)}, u32[]{:S(2)}, u32[]{:S(2)}) collective-permute-start(bf16[32,1152]{1,0:T(8,128)(2,1)S(1)} %get-tuple-element.200), channel_id=1, source_target_pairs={{256,384},{257,385},{258,386},{259,387},{260,388},{261,389},{262,3... | collective-permute-start | bytes 221192 | tf_op jit(solution)/shard_map/ppermute | solution.py:423
  62.1 4.9 %collective-permute-done.2.last_ref = bf16[32,1152]{1,0:T(8,128)(2,1)S(1)} collective-permute-done((bf16[32,1152]{1,0:T(8,128)(2,1)S(1)}, bf16[32,1152]{1,0:T(8,128)(2,1)S(1)}, u32[]{:S(2)}, u32[]{:S(2)}) %collective-permute-start.2) | collective-permute-done | bytes 73760 | tf_op jit(solution)/shard_map/ppermute | solution.py:423
  67.0 0.7 %shard_map.135 = f32[1,32]{1,0:T(1,128)} custom-call(s32[1]{0:T(128)} %bitcast.12.sec_ref, bf16[32,1152]{1,0:T(8,128)(2,1)S(1)} %collective-permute-done.2.last_ref, f32[40,1024]{1,0:T(8,128)S(1)} %get-tuple-element.239.part_ref, f32[1,32]{1,0:T(1,128)S(1)} %get-tuple-element.201.score0_ref, f32[1,32]{1,0:T(1,128)S(1)} %get-tuple-element.202.score1_ref, ...), custom_call_target="tpu_custom_call" | custom-call | flops 1000000 | tf_op jit(solution)/shard_map/pallas_call | solution.py:23
  (3 shorter events, 0.0 us)
Async XLA Ops:
  0.0 30.3 %copy-start = (bf16[1,1024,1024]{2,1,0:T(8,128)(2,1)S(1)}, bf16[1,1024,1024]{2,1,0:T(8,128)(2,1)}, u32[]{:S(2)}) copy-start(bf16[1,1024,1024]{2,1,0:T(8,128)(2,1)} %param.31) | copy-start | bytes 6291460
  0.0 30.3 %copy-start.1 = (bf16[1,1024]{1,0:T(2,128)(2,1)S(1)}, bf16[1,1024]{1,0:T(2,128)(2,1)}, u32[]{:S(2)}) copy-start(bf16[1,1024]{1,0:T(2,128)(2,1)} %param.25) | copy-start | bytes 6148
  30.3 30.5 %collective-permute-start.1 = (bf16[32,1152]{1,0:T(8,128)(2,1)S(1)}, bf16[32,1152]{1,0:T(8,128)(2,1)S(1)}, u32[]{:S(2)}, u32[]{:S(2)}) collective-permute-start(bf16[32,1152]{1,0:T(8,128)(2,1)S(1)} %get-tuple-element.198), channel_id=1, source_target_pairs={{128,256},{129,257},{130,258},{131,259},{132,260},{133,261},{134,2... | collective-permute-start | bytes 221192 | tf_op jit(solution)/shard_map/ppermute | solution.py:420
  60.8 6.2 %collective-permute-start.2 = (bf16[32,1152]{1,0:T(8,128)(2,1)S(1)}, bf16[32,1152]{1,0:T(8,128)(2,1)S(1)}, u32[]{:S(2)}, u32[]{:S(2)}) collective-permute-start(bf16[32,1152]{1,0:T(8,128)(2,1)S(1)} %get-tuple-element.200), channel_id=1, source_target_pairs={{256,384},{257,385},{258,386},{259,387},{260,388},{261,389},{262,3... | collective-permute-start | bytes 221192 | tf_op jit(solution)/shard_map/ppermute | solution.py:423

commit v8 on v7

--- a/solution.py
+++ b/solution.py
@@ -76,11 +76,10 @@
     final = second_ref.shape[1]
     slots = 2 * cands // shards
     base = (user_ref[0] % (128 // slots)) * slots
-    for move in moves[:4]:
-        move.wait()
 
     @pl.when(dense_ref[0] == 1)
     def _():
+        moves[0].wait()
         earlier = ones_where((iota((128, 256), 0) < iota((128, 256), 1)) | (iota((128, 256), 1) >= 128))
         seen = jnp.zeros((shards, 128), F32)
         ranks = []
@@ -94,14 +93,19 @@
             seen = seen + counts[:, 128:]
         rank = jnp.concatenate(ranks, axis=1).astype(jnp.int32)
         slot_ref[...] = owner * slots + rank
+        for move in moves[1:4]:
+            move.wait()
         row = row_ref[...]
         at_slot = rank + base == iota((128, cands), 0)
         high = jnp.where(at_slot, (row >> 4).astype(F32), 0.0).astype(BF16)
         low = jnp.where(at_slot, (row & 15).astype(F32), 0.0).astype(BF16)
-        req_ref[...] = (dot_nt(hot, high) * 16.0 + dot_nt(hot, low)).astype(jnp.int32)
+        both = dot_nt(hot, jnp.concatenate([high, low], axis=0))
+        req_ref[...] = (both[:, :128] * 16.0 + both[:, 128:]).astype(jnp.int32)
 
     @pl.when(zero_ref[0] + one_ref[0] > 0)
     def _():
+        for move in moves[:4]:
+            move.wait()
         second = jnp.concatenate([second_ref[...], jnp.zeros((1, 128 - final), jnp.int32)], axis=1)
         second = column(second.astype(F32))[:final, :1]
         single = lookup(second, first_ref[...])
@@ -124,7 +128,8 @@
         mine = (iota((1, 128), 1) >= base) & (iota((1, 128), 1) < base + slots)
         over = jnp.max(rank, axis=0, keepdims=True) >= slots // 2
         mark = jnp.where(mine & over, MARK, 0)
-        req_ref[...] = (dot(turned, high) * 16.0 + dot(turned, low)).astype(jnp.int32) + mark
+        both = dot(turned, jnp.concatenate([high, low], axis=1))
+        req_ref[...] = (both[:, :128] * 16.0 + both[:, 128:]).astype(jnp.int32) + mark
 
     for move in moves[4:]:
         move.wait()
@@ -236,21 +241,24 @@
         picked(jnp.concatenate([column(slot_ref[:, b:b + 128]) for b in range(h, h + 512, 128)], axis=0), wide)
         for h in range(0, cands, 512)
     ]
-    r, c = iota((128, 128), 0), iota((128, 128), 1)
-    same_item = (r // 32) == (c // 32)
-    spread = ones_where((r % 32) == (c % 32))
-    own_lanes = (r % 4) == (c // 32)
+    own_lanes = (iota((32, 128), 0) % 4) == (iota((32, 128), 1) // 32)
     grams = []
     for b in range(cands // 128):
         block = embed[b // 4][b % 4 * 128:b % 4 * 128 + 128, :]
-        gram = dot_nt(block, block) * (1.0 / math.sqrt(width))
-        gram = jnp.where(same_item, gram, 0.0).astype(BF16)
-        grams.append(jnp.where(own_lanes, dot(gram, spread), 0.0).astype(BF16))
-    tall = jnp.concatenate(grams, axis=0)
-    i, k = iota((8 * n, 32 * n), 0), iota((8 * n, 32 * n), 1)
-    choose = ones_where(((k // 32) == (i % n)) & (((k % 32) // 4) == (i // n)))
-    flat = dot(choose, tall).astype(BF16)
-    flat = jnp.concatenate([flat[q * n:(q + 1) * n, :] for q in range(8)], axis=1)
+        items = [block[i * 32:i * 32 + 32, :] for i in range(4)]
+        four = []
+        for i in (0, 2):
+            wide_pair = jnp.concatenate([items[i]] * 4 + [items[i + 1]] * 4, axis=0)
+            both = dot_nt(block[i * 32:i * 32 + 64, :], wide_pair) * (1.0 / math.sqrt(width))
+            four += [jnp.where(own_lanes, both[:32, :128], 0.0), jnp.where(own_lanes, both[32:, 128:], 0.0)]
+        grams.append(jnp.concatenate(four, axis=0).astype(BF16))
+    i, k = iota((64, 256), 0), iota((64, 256), 1)
+    choose = ones_where(((k // 32) == (i % 8)) & (((k % 32) // 4) == (i // 8)))
+    flat = []
+    for b in range(0, len(grams), 2):
+        eight = dot(choose, jnp.concatenate(grams[b:b + 2], axis=0))
+        flat.append(jnp.concatenate([eight[q * 8:q * 8 + 8, :] for q in range(8)], axis=1))
+    flat = jnp.concatenate(flat, axis=0).astype(BF16)
     part_ref[:n, :] = dot(flat, weight_ref[...])
     part_ref[n:n + 1, :] = head_ref[...]
 

time: 68 us -> 67.6 us (level)
  Pallas kernels: 5.93 us -> 5.18 us
    pallas_call x5, Pallas kernels: 5.93 us -> 5.18 us  [call(): pl.pallas_call(kernel, out_shape=out_shape, out_specs=(vmem,) * (len(out_...]
  transfers between devices with their start and end apart: 2 -> 2, of which waited for: 1 -> 1; matrix products, arithmetic and copies ran while one was open for 0% -> 0% of each run, Pallas kernels for 6% -> 4%
where the time goes in v8:
time: 67.6 us; the launch traced here: 67.3 us
  blocking collectives  54.9 us (81%)
  waiting for transfers between devices  5.25 us (8%)
  Pallas kernels  5.18 us (8%)
  starting transfers between devices  1.96 us (3%)
    all_to_all x1, blocking collectives, cascade(): lax.all_to_all(request.reshape(shards, 1, 128), 'shard', 0, 0, tiled=True)  28.8 us
    all_to_all x1, blocking collectives, exchanged(): lax.all_to_all(served.reshape(shards, -1, width), 'shard', 0, 0, tiled=True)  26 us
    ppermute x1, waiting for transfers between devices, cascade(): last = lax.ppermute(carry, 'section', [(2, 3)])  5.24 us
    pallas_call x5, Pallas kernels, call(): pl.pallas_call(kernel, out_shape=out_shape, out_specs=(vmem,) * (len(out_...  5.18 us
  transfers between devices with their start and end apart: 2, of which 1 were waited for; matrix products, arithmetic and copies ran while one was open for 0% of the time, Pallas kernels for 4%

profile of v8, /device:TPU:6, one launch (start us, length us, event | category | flops | bytes accessed | tf_op | source)
XLA Modules:
  0.0 67.3 jit_solution(843825142614981777)
XLA Ops:
  0.0 0.0 copy-start
  0.0 0.0 copy-start.1
  0.0 1.5 %shard_map.133 = (s32[128,128]{1,0:T(8,128)S(1)}, s32[1,1024]{1,0:T(1,128)S(1)}, s32[128,128]{1,0:T(8,128)S(1)}, bf16[2048,128]{1,0:T(8,128)(2,1)S(1)}, f32[1,1024]{1,0:T(1,128)S(1)}) custom-call(s32[1]{0:T(128)} %bitcast.13.user_ref, s32[1]{0:T(128)} %bitcast.14.zero_ref, s32[1]{0:T(128)} %bitcast.15.one_ref, s32[1]{0:T(128)} %bitcast.16.dense_ref, ...), custom_call_target="tpu_custom_call" | custom-call | flops 100000000 | tf_op jit(solution)/shard_map/pallas_call | solution.py:23
  1.5 28.8 %all_to_all.30 = s32[128,1,128]{2,1,0:T(1,128)S(1)} all-to-all(s32[128,1,128]{2,1,0:T(1,128)S(1)} %bitcast.39), channel_id=1, replica_groups=mesh['section'=4,'shard'=128] {'shard'}, dimensions={0} | all-to-all | bytes 131072 | tf_op jit(solution)/shard_map/all_to_all | solution.py:357
  30.4 0.0 copy-done
  30.4 0.0 copy-done.1
  30.4 0.7 collective-permute-start.1
  31.1 29.0 %conditional.7 = (f32[40,1024]{1,0:T(8,128)S(1)}) conditional(s32[]{:T(128)} %convert_element_type.25, s32[128,128]{1,0:T(8,128)S(1)} %bitcast.42, (s32[128,128]{1,0:T(8,128)S(1)}, bf16[2048,128]{1,0:T(8,128)(2,1)S(1)}, s32[1,1024]{1,0:T(1,128)S(1)}, f32[1,1024]{1,0:T(1,128)S(1)}, bf16[1024,1024]{1,0:T(8,128)(2,1)S(1)}) %tuple.68), branch_computations={%region_10.0_spmd, %region_11.0_spmd} | conditional | flops 2000000000 | bytes 1048584 | solution.py:429
  31.1 1.4 %branch_1_fun.20 = bf16[2048,128]{1,0:T(8,128)(2,1)S(1)} custom-call(s32[128,128]{1,0:T(8,128)S(1)} %get-tuple-element.180.ids_ref, bf16[2048,128]{1,0:T(8,128)(2,1)S(1)} %get-tuple-element.181.table_ref), custom_call_target="tpu_custom_call" | custom-call | flops 1000000000 | tf_op jit(solution)/shard_map/cond/branch_1_fun/pallas_call | solution.py:23
  32.4 26.0 %all_to_all.29 = bf16[128,16,128]{2,1,0:T(8,128)(2,1)S(1)} all-to-all(bf16[128,16,128]{2,1,0:T(8,128)(2,1)S(1)} %bitcast.36), channel_id=1, replica_groups=mesh['section'=4,'shard'=128] {'shard'}, dimensions={0} | all-to-all | bytes 1048576 | tf_op jit(solution)/shard_map/cond/branch_1_fun/all_to_all | solution.py:360
  58.5 1.6 %branch_1_fun.21 = f32[40,1024]{1,0:T(8,128)S(1)} custom-call(s32[1,1024]{1,0:T(1,128)S(1)} %get-tuple-element.179.slot_ref, bf16[2048,128]{1,0:T(8,128)(2,1)S(1)} %bitcast.33, f32[1,1024]{1,0:T(1,128)S(1)} %get-tuple-element.182.head_ref, bf16[1024,1024]{1,0:T(8,128)(2,1)S(1)} %get-tuple-element.183.weight_ref), custom_call_target="tpu_custom_call" | custom-call | flops 1000000000 | tf_op jit(solution)/shard_map/cond/branch_1_fun/pallas_call | solution.py:23
  60.0 0.0 collective-permute-done.1.near_ref
  60.1 1.3 %collective-permute-start.2 = (bf16[32,1152]{1,0:T(8,128)(2,1)S(1)}, bf16[32,1152]{1,0:T(8,128)(2,1)S(1)}, u32[]{:S(2)}, u32[]{:S(2)}) collective-permute-start(bf16[32,1152]{1,0:T(8,128)(2,1)S(1)} %get-tuple-element.200), channel_id=1, source_target_pairs={{256,384},{257,385},{258,386},{259,387},{260,388},{261,389},{262,3... | collective-permute-start | bytes 221192 | tf_op jit(solution)/shard_map/ppermute | solution.py:431
  61.4 5.2 %collective-permute-done.2.last_ref = bf16[32,1152]{1,0:T(8,128)(2,1)S(1)} collective-permute-done((bf16[32,1152]{1,0:T(8,128)(2,1)S(1)}, bf16[32,1152]{1,0:T(8,128)(2,1)S(1)}, u32[]{:S(2)}, u32[]{:S(2)}) %collective-permute-start.2) | collective-permute-done | bytes 73760 | tf_op jit(solution)/shard_map/ppermute | solution.py:431
  66.6 0.7 %shard_map.135 = f32[1,32]{1,0:T(1,128)} custom-call(s32[1]{0:T(128)} %bitcast.12.sec_ref, bf16[32,1152]{1,0:T(8,128)(2,1)S(1)} %collective-permute-done.2.last_ref, f32[40,1024]{1,0:T(8,128)S(1)} %get-tuple-element.239.part_ref, f32[1,32]{1,0:T(1,128)S(1)} %get-tuple-element.201.score0_ref, f32[1,32]{1,0:T(1,128)S(1)} %get-tuple-element.202.score1_ref, ...), custom_call_target="tpu_custom_call" | custom-call | flops 1000000 | tf_op jit(solution)/shard_map/pallas_call | solution.py:23
  (3 shorter events, 0.0 us)
Async XLA Ops:
  0.0 30.4 %copy-start = (bf16[1,1024,1024]{2,1,0:T(8,128)(2,1)S(1)}, bf16[1,1024,1024]{2,1,0:T(8,128)(2,1)}, u32[]{:S(2)}) copy-start(bf16[1,1024,1024]{2,1,0:T(8,128)(2,1)} %param.31) | copy-start | bytes 6291460
  0.0 30.4 %copy-start.1 = (bf16[1,1024]{1,0:T(2,128)(2,1)S(1)}, bf16[1,1024]{1,0:T(2,128)(2,1)}, u32[]{:S(2)}) copy-start(bf16[1,1024]{1,0:T(2,128)(2,1)} %param.25) | copy-start | bytes 6148
  30.4 29.6 %collective-permute-start.1 = (bf16[32,1152]{1,0:T(8,128)(2,1)S(1)}, bf16[32,1152]{1,0:T(8,128)(2,1)S(1)}, u32[]{:S(2)}, u32[]{:S(2)}) collective-permute-start(bf16[32,1152]{1,0:T(8,128)(2,1)S(1)} %get-tuple-element.198), channel_id=1, source_target_pairs={{128,256},{129,257},{130,258},{131,259},{132,260},{133,261},{134,2... | collective-permute-start | bytes 221192 | tf_op jit(solution)/shard_map/ppermute | solution.py:428
  60.1 6.5 %collective-permute-start.2 = (bf16[32,1152]{1,0:T(8,128)(2,1)S(1)}, bf16[32,1152]{1,0:T(8,128)(2,1)S(1)}, u32[]{:S(2)}, u32[]{:S(2)}) collective-permute-start(bf16[32,1152]{1,0:T(8,128)(2,1)S(1)} %get-tuple-element.200), channel_id=1, source_target_pairs={{256,384},{257,385},{258,386},{259,387},{260,388},{261,389},{262,3... | collective-permute-start | bytes 221192 | tf_op jit(solution)/shard_map/ppermute | solution.py:431

commit v9 on v8

--- a/solution.py
+++ b/solution.py
@@ -102,17 +102,7 @@
         both = dot_nt(hot, jnp.concatenate([high, low], axis=0))
         req_ref[...] = (both[:, :128] * 16.0 + both[:, 128:]).astype(jnp.int32)
 
-    @pl.when(zero_ref[0] + one_ref[0] > 0)
-    def _():
-        for move in moves[:4]:
-            move.wait()
-        second = jnp.concatenate([second_ref[...], jnp.zeros((1, 128 - final), jnp.int32)], axis=1)
-        second = column(second.astype(F32))[:final, :1]
-        single = lookup(second, first_ref[...])
-        fours = [second * 4.0 + float(f) for f in range(4)]
-        none = jnp.full((final, 1), -1.0, F32)
-        at = jnp.concatenate(
-            [jnp.where(zero_ref[0] == 1, single if f == 0 else none, fours[f]) for f in range(4)], axis=0)
+    def request_rows(at):
         owner = lookup(at, owner_ref[...] + 1) - 1.0
         row = lookup(at, row_ref[...]).astype(jnp.int32)
         count = at.shape[0]
@@ -120,7 +110,7 @@
         hot = jnp.where(owner == lanes, 1.0, 0.0)
         before = ones_where(iota((count, count), 1) < iota((count, count), 0))
         rank = jnp.sum(hot * dot(before, hot.astype(BF16)), axis=1, keepdims=True)
-        spot_ref[...] = jnp.broadcast_to(owner * slots + rank, spot_ref.shape).astype(jnp.int32)
+        spot_ref[:count, :] = jnp.broadcast_to(owner * slots + rank, (count, 128)).astype(jnp.int32)
         at_slot = rank + base.astype(F32) == lanes
         high = jnp.where(at_slot, (row >> 4).astype(F32), 0.0).astype(BF16)
         low = jnp.where(at_slot, (row & 15).astype(F32), 0.0).astype(BF16)
@@ -130,6 +120,23 @@
         mark = jnp.where(mine & over, MARK, 0)
         both = dot(turned, jnp.concatenate([high, low], axis=1))
         req_ref[...] = (both[:, :128] * 16.0 + both[:, 128:]).astype(jnp.int32) + mark
+
+    def second_column():
+        second = jnp.concatenate([second_ref[...], jnp.zeros((1, 128 - final), jnp.int32)], axis=1)
+        return column(second.astype(F32))[:final, :1]
+
+    @pl.when(zero_ref[0] == 1)
+    def _():
+        for move in moves[:4]:
+            move.wait()
+        request_rows(lookup(second_column(), first_ref[...]))
+
+    @pl.when(one_ref[0] == 1)
+    def _():
+        for move in moves[:4]:
+            move.wait()
+        second = second_column() * 4.0
+        request_rows(jnp.concatenate([second + float(f) for f in range(4)], axis=0))
 
     for move in moves[4:]:
         move.wait()
@@ -175,11 +182,11 @@
     for move in moves:
         move.start()
     over_ref[0] = jnp.max(ids_ref[...])
+    active = jax.nn.relu(dot(dense_ref[...], weight_ref[...]))
+    query = (active * head_ref[...]).astype(BF16)
     served_rows(ids_ref, table_ref, out_ref, 8)
     for move in moves:
         move.wait()
-    active = jax.nn.relu(dot(dense_ref[...], weight_ref[...]))
-    query = (active * head_ref[...]).astype(BF16)
     vec_ref[...] = dot(query, proj_ref[...])
 
 

time: 67.6 us -> 67.3 us (level)
  no operation moved by 1% of the time
where the time goes in v9:
time: 67.3 us; the launch traced here: 67 us
  blocking collectives  54.9 us (82%)
  Pallas kernels  5.19 us (8%)
  waiting for transfers between devices  4.95 us (7%)
  starting transfers between devices  1.96 us (3%)
    all_to_all x1, blocking collectives, cascade(): lax.all_to_all(request.reshape(shards, 1, 128), 'shard', 0, 0, tiled=True)  28.8 us
    all_to_all x1, blocking collectives, exchanged(): lax.all_to_all(served.reshape(shards, -1, width), 'shard', 0, 0, tiled=True)  26 us
    pallas_call x5, Pallas kernels, call(): pl.pallas_call(kernel, out_shape=out_shape, out_specs=(vmem,) * (len(out_...  5.18 us
    ppermute x1, waiting for transfers between devices, cascade(): last = lax.ppermute(carry, 'section', [(2, 3)])  4.95 us
  transfers between devices with their start and end apart: 2, of which 1 were waited for; matrix products, arithmetic and copies ran while one was open for 0% of the time, Pallas kernels for 4%

profile of v9, /device:TPU:6, one launch (start us, length us, event | category | flops | bytes accessed | tf_op | source)
XLA Modules:
  0.0 67.0 jit_solution(17503589942096440560)
XLA Ops:
  0.0 0.0 copy-start
  0.0 0.0 copy-start.1
  0.0 1.5 %shard_map.133 = (s32[128,128]{1,0:T(8,128)S(1)}, s32[1,1024]{1,0:T(1,128)S(1)}, s32[128,128]{1,0:T(8,128)S(1)}, bf16[2048,128]{1,0:T(8,128)(2,1)S(1)}, f32[1,1024]{1,0:T(1,128)S(1)}) custom-call(s32[1]{0:T(128)} %bitcast.13.user_ref, s32[1]{0:T(128)} %bitcast.14.zero_ref, s32[1]{0:T(128)} %bitcast.15.one_ref, s32[1]{0:T(128)} %bitcast.16.dense_ref, ...), custom_call_target="tpu_custom_call" | custom-call | flops 100000000 | tf_op jit(solution)/shard_map/pallas_call | solution.py:23
  1.5 28.8 %all_to_all.30 = s32[128,1,128]{2,1,0:T(1,128)S(1)} all-to-all(s32[128,1,128]{2,1,0:T(1,128)S(1)} %bitcast.39), channel_id=1, replica_groups=mesh['section'=4,'shard'=128] {'shard'}, dimensions={0} | all-to-all | bytes 131072 | tf_op jit(solution)/shard_map/all_to_all | solution.py:364
  30.4 0.0 copy-done
  30.4 0.0 copy-done.1
  30.4 0.7 collective-permute-start.1
  31.1 29.0 %conditional.7 = (f32[40,1024]{1,0:T(8,128)S(1)}) conditional(s32[]{:T(128)} %convert_element_type.25, s32[128,128]{1,0:T(8,128)S(1)} %bitcast.42, (s32[128,128]{1,0:T(8,128)S(1)}, bf16[2048,128]{1,0:T(8,128)(2,1)S(1)}, s32[1,1024]{1,0:T(1,128)S(1)}, f32[1,1024]{1,0:T(1,128)S(1)}, bf16[1024,1024]{1,0:T(8,128)(2,1)S(1)}) %tuple.68), branch_computations={%region_10.0_spmd, %region_11.0_spmd} | conditional | flops 2000000000 | bytes 1048584 | solution.py:436
  31.1 1.4 %branch_1_fun.20 = bf16[2048,128]{1,0:T(8,128)(2,1)S(1)} custom-call(s32[128,128]{1,0:T(8,128)S(1)} %get-tuple-element.180.ids_ref, bf16[2048,128]{1,0:T(8,128)(2,1)S(1)} %get-tuple-element.181.table_ref), custom_call_target="tpu_custom_call" | custom-call | flops 1000000000 | tf_op jit(solution)/shard_map/cond/branch_1_fun/pallas_call | solution.py:23
  32.5 26.0 %all_to_all.29 = bf16[128,16,128]{2,1,0:T(8,128)(2,1)S(1)} all-to-all(bf16[128,16,128]{2,1,0:T(8,128)(2,1)S(1)} %bitcast.36), channel_id=1, replica_groups=mesh['section'=4,'shard'=128] {'shard'}, dimensions={0} | all-to-all | bytes 1048576 | tf_op jit(solution)/shard_map/cond/branch_1_fun/all_to_all | solution.py:367
  58.5 1.6 %branch_1_fun.21 = f32[40,1024]{1,0:T(8,128)S(1)} custom-call(s32[1,1024]{1,0:T(1,128)S(1)} %get-tuple-element.179.slot_ref, bf16[2048,128]{1,0:T(8,128)(2,1)S(1)} %bitcast.33, f32[1,1024]{1,0:T(1,128)S(1)} %get-tuple-element.182.head_ref, bf16[1024,1024]{1,0:T(8,128)(2,1)S(1)} %get-tuple-element.183.weight_ref), custom_call_target="tpu_custom_call" | custom-call | flops 1000000000 | tf_op jit(solution)/shard_map/cond/branch_1_fun/pallas_call | solution.py:23
  60.0 0.0 collective-permute-done.1.near_ref
  60.1 1.3 %collective-permute-start.2 = (bf16[32,1152]{1,0:T(8,128)(2,1)S(1)}, bf16[32,1152]{1,0:T(8,128)(2,1)S(1)}, u32[]{:S(2)}, u32[]{:S(2)}) collective-permute-start(bf16[32,1152]{1,0:T(8,128)(2,1)S(1)} %get-tuple-element.200), channel_id=1, source_target_pairs={{256,384},{257,385},{258,386},{259,387},{260,388},{261,389},{262,3... | collective-permute-start | bytes 221192 | tf_op jit(solution)/shard_map/ppermute | solution.py:438
  61.4 4.9 %collective-permute-done.2.last_ref = bf16[32,1152]{1,0:T(8,128)(2,1)S(1)} collective-permute-done((bf16[32,1152]{1,0:T(8,128)(2,1)S(1)}, bf16[32,1152]{1,0:T(8,128)(2,1)S(1)}, u32[]{:S(2)}, u32[]{:S(2)}) %collective-permute-start.2) | collective-permute-done | bytes 73760 | tf_op jit(solution)/shard_map/ppermute | solution.py:438
  66.3 0.7 %shard_map.135 = f32[1,32]{1,0:T(1,128)} custom-call(s32[1]{0:T(128)} %bitcast.12.sec_ref, bf16[32,1152]{1,0:T(8,128)(2,1)S(1)} %collective-permute-done.2.last_ref, f32[40,1024]{1,0:T(8,128)S(1)} %get-tuple-element.239.part_ref, f32[1,32]{1,0:T(1,128)S(1)} %get-tuple-element.201.score0_ref, f32[1,32]{1,0:T(1,128)S(1)} %get-tuple-element.202.score1_ref, ...), custom_call_target="tpu_custom_call" | custom-call | flops 1000000 | tf_op jit(solution)/shard_map/pallas_call | solution.py:23
  (3 shorter events, 0.0 us)
Async XLA Ops:
  0.0 30.4 %copy-start = (bf16[1,1024,1024]{2,1,0:T(8,128)(2,1)S(1)}, bf16[1,1024,1024]{2,1,0:T(8,128)(2,1)}, u32[]{:S(2)}) copy-start(bf16[1,1024,1024]{2,1,0:T(8,128)(2,1)} %param.31) | copy-start | bytes 6291460
  0.0 30.4 %copy-start.1 = (bf16[1,1024]{1,0:T(2,128)(2,1)S(1)}, bf16[1,1024]{1,0:T(2,128)(2,1)}, u32[]{:S(2)}) copy-start(bf16[1,1024]{1,0:T(2,128)(2,1)} %param.25) | copy-start | bytes 6148
  30.4 29.6 %collective-permute-start.1 = (bf16[32,1152]{1,0:T(8,128)(2,1)S(1)}, bf16[32,1152]{1,0:T(8,128)(2,1)S(1)}, u32[]{:S(2)}, u32[]{:S(2)}) collective-permute-start(bf16[32,1152]{1,0:T(8,128)(2,1)S(1)} %get-tuple-element.198), channel_id=1, source_target_pairs={{128,256},{129,257},{130,258},{131,259},{132,260},{133,261},{134,2... | collective-permute-start | bytes 221192 | tf_op jit(solution)/shard_map/ppermute | solution.py:435
  60.1 6.2 %collective-permute-start.2 = (bf16[32,1152]{1,0:T(8,128)(2,1)S(1)}, bf16[32,1152]{1,0:T(8,128)(2,1)S(1)}, u32[]{:S(2)}, u32[]{:S(2)}) collective-permute-start(bf16[32,1152]{1,0:T(8,128)(2,1)S(1)} %get-tuple-element.200), channel_id=1, source_target_pairs={{256,384},{257,385},{258,386},{259,387},{260,388},{261,389},{262,3... | collective-permute-start | bytes 221192 | tf_op jit(solution)/shard_map/ppermute | solution.py:438

commit v10 on v9

--- a/solution.py
+++ b/solution.py
@@ -177,17 +177,16 @@
 
 
 def serve_zero_kernel(proj_hbm, into_hbm, out_of_hbm, ids_ref, table_ref, dense_ref, head_ref, weight_ref,
-                      out_ref, vec_ref, into_ref, out_of_ref, over_ref, proj_ref, sem):
+                      out_ref, query_ref, into_ref, out_of_ref, proj_ref, over_ref, sem):
     moves = copies((proj_hbm, into_hbm, out_of_hbm), (proj_ref, into_ref, out_of_ref), sem)
     for move in moves:
         move.start()
     over_ref[0] = jnp.max(ids_ref[...])
     active = jax.nn.relu(dot(dense_ref[...], weight_ref[...]))
-    query = (active * head_ref[...]).astype(BF16)
+    query_ref[...] = (active * head_ref[...]).astype(BF16)
     served_rows(ids_ref, table_ref, out_ref, 8)
     for move in moves:
         move.wait()
-    vec_ref[...] = dot(query, proj_ref[...])
 
 
 def serve_one_kernel(item_hbm, ids_ref, table_ref, out_ref, item_ref, over_ref, sem):
@@ -218,12 +217,13 @@
     return picked((spot >> 4) * slots + (spot & 15), halves(rows))
 
 
-def tower_kernel(spot_ref, rows_ref, vec_ref, into_ref, out_of_ref, packet_ref, score_ref):
+def tower_kernel(spot_ref, rows_ref, query_ref, proj_ref, into_ref, out_of_ref, packet_ref, score_ref):
     n = packet_ref.shape[0] // 2
+    vec = dot(query_ref[...], proj_ref[...])
     embed = survivors(spot_ref[:n, :], rows_ref[...])
     hidden = jax.nn.relu(dot(embed, into_ref[...])).astype(BF16)
     tower = dot(hidden, out_of_ref[...]).astype(BF16)
-    logit = jnp.sum(tower.astype(F32) * vec_ref[...], axis=1, keepdims=True)
+    logit = jnp.sum(tower.astype(F32) * vec, axis=1, keepdims=True)
     packet_ref[:n, :] = tower
     packet_ref[n:, :] = jnp.broadcast_to(logit, (n, 128)).astype(BF16)
     score_ref[...] = as_row(logit, n)
@@ -394,15 +394,14 @@
     product = shape((final, hid), F32)
 
     def section_zero():
-        served, query, into_near, out_of_near, over = call(
+        served, query, into_near, out_of_near, proj_near, over = call(
             serve_zero_kernel,
-            (short, shape((1, width), F32), like(into), like(out_of), scalar),
+            (short, like(user_dense), like(into), like(out_of), like(proj), scalar),
             proj, into, out_of, asked, table, user_dense, head, weight_near(),
             hbm=3, sems=3, flops=10**9, smem_out=True,
-            scratch=[pltpu.VMEM(proj.shape, BF16)],
         )
         return kept(*either(over, served, lambda rows: tuple(call(
-            tower_kernel, (packed, scored), spot, rows, query, into_near, out_of_near, flops=10**7))))
+            tower_kernel, (packed, scored), spot, rows, query, proj_near, into_near, out_of_near, flops=10**7))))
 
     def section_one():
         served, item_near, over = call(

time: 67.3 us -> 67.8 us (level)
  no operation moved by 1% of the time
where the time goes in v10:
time: 67.8 us; the launch traced here: 67.5 us
  blocking collectives  54.9 us (81%)
  waiting for transfers between devices  5.46 us (8%)
  Pallas kernels  5.19 us (8%)
  starting transfers between devices  1.96 us (3%)
    all_to_all x1, blocking collectives, cascade(): lax.all_to_all(request.reshape(shards, 1, 128), 'shard', 0, 0, tiled=True)  28.8 us
    all_to_all x1, blocking collectives, exchanged(): lax.all_to_all(served.reshape(shards, -1, width), 'shard', 0, 0, tiled=True)  26 us
    ppermute x1, waiting for transfers between devices, cascade(): last = lax.ppermute(carry, 'section', [(2, 3)])  5.46 us
    pallas_call x5, Pallas kernels, call(): pl.pallas_call(kernel, out_shape=out_shape, out_specs=(vmem,) * (len(out_...  5.18 us
  transfers between devices with their start and end apart: 2, of which 1 were waited for; matrix products, arithmetic and copies ran while one was open for 0% of the time, Pallas kernels for 4%

profile of v10, /device:TPU:6, one launch (start us, length us, event | category | flops | bytes accessed | tf_op | source)
XLA Modules:
  0.0 67.5 jit_solution(3529511523549810818)
XLA Ops:
  0.0 0.0 copy-start
  0.0 0.0 copy-start.1
  0.0 1.5 %shard_map.133 = (s32[128,128]{1,0:T(8,128)S(1)}, s32[1,1024]{1,0:T(1,128)S(1)}, s32[128,128]{1,0:T(8,128)S(1)}, bf16[2048,128]{1,0:T(8,128)(2,1)S(1)}, f32[1,1024]{1,0:T(1,128)S(1)}) custom-call(s32[1]{0:T(128)} %bitcast.13.user_ref, s32[1]{0:T(128)} %bitcast.14.zero_ref, s32[1]{0:T(128)} %bitcast.15.one_ref, s32[1]{0:T(128)} %bitcast.16.dense_ref, ...), custom_call_target="tpu_custom_call" | custom-call | flops 100000000 | tf_op jit(solution)/shard_map/pallas_call | solution.py:23
  1.5 28.8 %all_to_all.30 = s32[128,1,128]{2,1,0:T(1,128)S(1)} all-to-all(s32[128,1,128]{2,1,0:T(1,128)S(1)} %bitcast.39), channel_id=1, replica_groups=mesh['section'=4,'shard'=128] {'shard'}, dimensions={0} | all-to-all | bytes 131072 | tf_op jit(solution)/shard_map/all_to_all | solution.py:364
  30.4 0.0 copy-done
  30.4 0.0 copy-done.1
  30.4 0.7 collective-permute-start.1
  31.1 29.0 %conditional.7 = (f32[40,1024]{1,0:T(8,128)S(1)}) conditional(s32[]{:T(128)} %convert_element_type.25, s32[128,128]{1,0:T(8,128)S(1)} %bitcast.42, (s32[128,128]{1,0:T(8,128)S(1)}, bf16[2048,128]{1,0:T(8,128)(2,1)S(1)}, s32[1,1024]{1,0:T(1,128)S(1)}, f32[1,1024]{1,0:T(1,128)S(1)}, bf16[1024,1024]{1,0:T(8,128)(2,1)S(1)}) %tuple.68), branch_computations={%region_10.0_spmd, %region_11.0_spmd} | conditional | flops 2000000000 | bytes 1048584 | solution.py:435
  31.1 1.4 %branch_1_fun.20 = bf16[2048,128]{1,0:T(8,128)(2,1)S(1)} custom-call(s32[128,128]{1,0:T(8,128)S(1)} %get-tuple-element.187.ids_ref, bf16[2048,128]{1,0:T(8,128)(2,1)S(1)} %get-tuple-element.188.table_ref), custom_call_target="tpu_custom_call" | custom-call | flops 1000000000 | tf_op jit(solution)/shard_map/cond/branch_1_fun/pallas_call | solution.py:23
  32.5 26.0 %all_to_all.29 = bf16[128,16,128]{2,1,0:T(8,128)(2,1)S(1)} all-to-all(bf16[128,16,128]{2,1,0:T(8,128)(2,1)S(1)} %bitcast.36), channel_id=1, replica_groups=mesh['section'=4,'shard'=128] {'shard'}, dimensions={0} | all-to-all | bytes 1048576 | tf_op jit(solution)/shard_map/cond/branch_1_fun/all_to_all | solution.py:367
  58.5 1.6 %branch_1_fun.21 = f32[40,1024]{1,0:T(8,128)S(1)} custom-call(s32[1,1024]{1,0:T(1,128)S(1)} %get-tuple-element.186.slot_ref, bf16[2048,128]{1,0:T(8,128)(2,1)S(1)} %bitcast.33, f32[1,1024]{1,0:T(1,128)S(1)} %get-tuple-element.189.head_ref, bf16[1024,1024]{1,0:T(8,128)(2,1)S(1)} %get-tuple-element.190.weight_ref), custom_call_target="tpu_custom_call" | custom-call | flops 1000000000 | tf_op jit(solution)/shard_map/cond/branch_1_fun/pallas_call | solution.py:23
  60.0 0.0 collective-permute-done.1.near_ref
  60.1 1.3 %collective-permute-start.2 = (bf16[32,1152]{1,0:T(8,128)(2,1)S(1)}, bf16[32,1152]{1,0:T(8,128)(2,1)S(1)}, u32[]{:S(2)}, u32[]{:S(2)}) collective-permute-start(bf16[32,1152]{1,0:T(8,128)(2,1)S(1)} %get-tuple-element.207), channel_id=1, source_target_pairs={{256,384},{257,385},{258,386},{259,387},{260,388},{261,389},{262,3... | collective-permute-start | bytes 221192 | tf_op jit(solution)/shard_map/ppermute | solution.py:437
  61.4 5.5 %collective-permute-done.2.last_ref = bf16[32,1152]{1,0:T(8,128)(2,1)S(1)} collective-permute-done((bf16[32,1152]{1,0:T(8,128)(2,1)S(1)}, bf16[32,1152]{1,0:T(8,128)(2,1)S(1)}, u32[]{:S(2)}, u32[]{:S(2)}) %collective-permute-start.2) | collective-permute-done | bytes 73760 | tf_op jit(solution)/shard_map/ppermute | solution.py:437
  66.8 0.7 %shard_map.135 = f32[1,32]{1,0:T(1,128)} custom-call(s32[1]{0:T(128)} %bitcast.12.sec_ref, bf16[32,1152]{1,0:T(8,128)(2,1)S(1)} %collective-permute-done.2.last_ref, f32[40,1024]{1,0:T(8,128)S(1)} %get-tuple-element.246.part_ref, f32[1,32]{1,0:T(1,128)S(1)} %get-tuple-element.208.score0_ref, f32[1,32]{1,0:T(1,128)S(1)} %get-tuple-element.209.score1_ref, ...), custom_call_target="tpu_custom_call" | custom-call | flops 1000000 | tf_op jit(solution)/shard_map/pallas_call | solution.py:23
  (3 shorter events, 0.0 us)
Async XLA Ops:
  0.0 30.4 %copy-start = (bf16[1,1024,1024]{2,1,0:T(8,128)(2,1)S(1)}, bf16[1,1024,1024]{2,1,0:T(8,128)(2,1)}, u32[]{:S(2)}) copy-start(bf16[1,1024,1024]{2,1,0:T(8,128)(2,1)} %param.31) | copy-start | bytes 6291460
  0.0 30.4 %copy-start.1 = (bf16[1,1024]{1,0:T(2,128)(2,1)S(1)}, bf16[1,1024]{1,0:T(2,128)(2,1)}, u32[]{:S(2)}) copy-start(bf16[1,1024]{1,0:T(2,128)(2,1)} %param.25) | copy-start | bytes 6148
  30.4 29.6 %collective-permute-start.1 = (bf16[32,1152]{1,0:T(8,128)(2,1)S(1)}, bf16[32,1152]{1,0:T(8,128)(2,1)S(1)}, u32[]{:S(2)}, u32[]{:S(2)}) collective-permute-start(bf16[32,1152]{1,0:T(8,128)(2,1)S(1)} %get-tuple-element.205), channel_id=1, source_target_pairs={{128,256},{129,257},{130,258},{131,259},{132,260},{133,261},{134,2... | collective-permute-start | bytes 221192 | tf_op jit(solution)/shard_map/ppermute | solution.py:434
  60.1 6.8 %collective-permute-start.2 = (bf16[32,1152]{1,0:T(8,128)(2,1)S(1)}, bf16[32,1152]{1,0:T(8,128)(2,1)S(1)}, u32[]{:S(2)}, u32[]{:S(2)}) collective-permute-start(bf16[32,1152]{1,0:T(8,128)(2,1)S(1)} %get-tuple-element.207), channel_id=1, source_target_pairs={{256,384},{257,385},{258,386},{259,387},{260,388},{261,389},{262,3... | collective-permute-start | bytes 221192 | tf_op jit(solution)/shard_map/ppermute | solution.py:437

commit v11 on v9

--- a/solution.py
+++ b/solution.py
@@ -65,10 +65,10 @@
 
 
 def request_kernel(user_ref, zero_ref, one_ref, dense_ref, owner_hbm, row_hbm, table_hbm, first_hbm, second_hbm, head_hbm,
-                   weight_hbm, req_ref, slot_ref, spot_ref, table_ref, head_ref,
+                   weight_hbm, req_ref, slot_ref, spot_ref, head_ref,
                    owner_ref, row_ref, first_ref, second_ref, sem):
-    moves = copies((owner_hbm, row_hbm, first_hbm, second_hbm, table_hbm, head_hbm),
-                   (owner_ref, row_ref, first_ref, second_ref, table_ref, head_ref), sem)
+    moves = copies((owner_hbm, row_hbm, first_hbm, second_hbm, head_hbm),
+                   (owner_ref, row_ref, first_ref, second_ref, head_ref), sem)
     for move in moves:
         move.start()
     shards = req_ref.shape[0]
@@ -351,14 +351,15 @@
         return pltpu.with_memory_space_constraint(weight, pltpu.VMEM)
 
 
-    request, slot, spot, table, head = call(
+    table = pltpu.with_memory_space_constraint(tables[0], pltpu.VMEM)
+    request, slot, spot, head = call(
         request_kernel,
-        (shape((shards, 128), jnp.int32), shape((1, cands), jnp.int32), shape((128, 128), jnp.int32), like(tables[0]),
+        (shape((shards, 128), jnp.int32), shape((1, cands), jnp.int32), shape((128, 128), jnp.int32),
          like(section_head)),
         user, *(turn.astype(jnp.int32).reshape(1) for turn in turns),
         *in_hbm(feat_owner.reshape(1, cands), feat_row.reshape(1, cands), tables[0], keep_first, keep_second, section_head,
                 section_weight[0]),
-        smem=4, hbm=7, sems=6, flops=10**8,
+        smem=4, hbm=7, sems=5, flops=10**8,
         scratch=[pltpu.VMEM(s, jnp.int32) for s in ((1, cands), (1, cands), keep_first.shape, keep_second.shape)],
     )
     asked = lax.all_to_all(request.reshape(shards, 1, 128), "shard", 0, 0, tiled=True).reshape(shards, 128)

time: 67.3 us -> 67.6 us (level)
  no operation moved by 1% of the time
where the time goes in v11:
time: 67.6 us; the launch traced here: 67.3 us
  blocking collectives  54.8 us (81%)
  Pallas kernels  5.19 us (8%)
  waiting for transfers between devices  4.95 us (7%)
  starting transfers between devices  1.96 us (3%)
    all_to_all x1, blocking collectives, cascade(): lax.all_to_all(request.reshape(shards, 1, 128), 'shard', 0, 0, tiled=True)  28.8 us
    all_to_all x1, blocking collectives, exchanged(): lax.all_to_all(served.reshape(shards, -1, width), 'shard', 0, 0, tiled=True)  26 us
    pallas_call x5, Pallas kernels, call(): pl.pallas_call(kernel, out_shape=out_shape, out_specs=(vmem,) * (len(out_...  5.19 us
    ppermute x1, waiting for transfers between devices, cascade(): last = lax.ppermute(carry, 'section', [(2, 3)])  4.95 us
  transfers between devices with their start and end apart: 2, of which 1 were waited for; matrix products, arithmetic and copies ran while one was open for 0% of the time, Pallas kernels for 4%

profile of v11, /device:TPU:6, one launch (start us, length us, event | category | flops | bytes accessed | tf_op | source)
XLA Modules:
  0.0 67.3 jit_solution(3023679617870676600)
XLA Ops:
  0.0 0.0 copy-start
  0.0 0.0 copy-start.1
  0.0 0.0 copy-start.2
  0.0 1.5 %shard_map.133 = (s32[128,128]{1,0:T(8,128)S(1)}, s32[1,1024]{1,0:T(1,128)S(1)}, s32[128,128]{1,0:T(8,128)S(1)}, f32[1,1024]{1,0:T(1,128)S(1)}) custom-call(s32[1]{0:T(128)} %bitcast.13.user_ref, s32[1]{0:T(128)} %bitcast.14.zero_ref, s32[1]{0:T(128)} %bitcast.15.one_ref, s32[1]{0:T(128)} %bitcast.16.dense_ref, s32[1,1024]{1,0:T(1,128)} %bitcast.47, ...), custom_call_target="tpu_custom_call" | custom-call | flops 100000000 | tf_op jit(solution)/shard_map/pallas_call | solution.py:23
  1.6 28.8 %all_to_all.30 = s32[128,1,128]{2,1,0:T(1,128)S(1)} all-to-all(s32[128,1,128]{2,1,0:T(1,128)S(1)} %bitcast.42), channel_id=1, replica_groups=mesh['section'=4,'shard'=128] {'shard'}, dimensions={0} | all-to-all | bytes 131072 | tf_op jit(solution)/shard_map/all_to_all | solution.py:365
  30.4 0.0 copy-done
  30.4 0.0 copy-done.1
  30.4 0.0 copy-done.2
  30.4 0.2 conditional.6
  30.7 0.7 collective-permute-start.1
  31.3 29.0 %conditional.7 = (f32[40,1024]{1,0:T(8,128)S(1)}) conditional(s32[]{:T(128)} %convert_element_type.25, s32[128,128]{1,0:T(8,128)S(1)} %bitcast.45, (s32[128,128]{1,0:T(8,128)S(1)}, bf16[2048,128]{1,0:T(8,128)(2,1)S(1)}, s32[1,1024]{1,0:T(1,128)S(1)}, f32[1,1024]{1,0:T(1,128)S(1)}, bf16[1024,1024]{1,0:T(8,128)(2,1)S(1)}) %tuple.70), branch_computations={%region_10.0_spmd, %region_11.0_spmd} | conditional | flops 2000000000 | bytes 1048584 | solution.py:437
  31.4 1.3 %branch_1_fun.20 = bf16[2048,128]{1,0:T(8,128)(2,1)S(1)} custom-call(s32[128,128]{1,0:T(8,128)S(1)} %get-tuple-element.180.ids_ref, bf16[2048,128]{1,0:T(8,128)(2,1)S(1)} %get-tuple-element.181.table_ref), custom_call_target="tpu_custom_call" | custom-call | flops 1000000000 | tf_op jit(solution)/shard_map/cond/branch_1_fun/pallas_call | solution.py:23
  32.7 26.0 %all_to_all.29 = bf16[128,16,128]{2,1,0:T(8,128)(2,1)S(1)} all-to-all(bf16[128,16,128]{2,1,0:T(8,128)(2,1)S(1)} %bitcast.36), channel_id=1, replica_groups=mesh['section'=4,'shard'=128] {'shard'}, dimensions={0} | all-to-all | bytes 1048576 | tf_op jit(solution)/shard_map/cond/branch_1_fun/all_to_all | solution.py:368
  58.7 1.6 %branch_1_fun.21 = f32[40,1024]{1,0:T(8,128)S(1)} custom-call(s32[1,1024]{1,0:T(1,128)S(1)} %get-tuple-element.179.slot_ref, bf16[2048,128]{1,0:T(8,128)(2,1)S(1)} %bitcast.33, f32[1,1024]{1,0:T(1,128)S(1)} %get-tuple-element.182.head_ref, bf16[1024,1024]{1,0:T(8,128)(2,1)S(1)} %get-tuple-element.183.weight_ref), custom_call_target="tpu_custom_call" | custom-call | flops 1000000000 | tf_op jit(solution)/shard_map/cond/branch_1_fun/pallas_call | solution.py:23
  60.3 0.0 collective-permute-done.1.near_ref
  60.3 1.3 %collective-permute-start.2 = (bf16[32,1152]{1,0:T(8,128)(2,1)S(1)}, bf16[32,1152]{1,0:T(8,128)(2,1)S(1)}, u32[]{:S(2)}, u32[]{:S(2)}) collective-permute-start(bf16[32,1152]{1,0:T(8,128)(2,1)S(1)} %get-tuple-element.198), channel_id=1, source_target_pairs={{256,384},{257,385},{258,386},{259,387},{260,388},{261,389},{262,3... | collective-permute-start | bytes 221192 | tf_op jit(solution)/shard_map/ppermute | solution.py:439
  61.6 4.9 %collective-permute-done.2.last_ref = bf16[32,1152]{1,0:T(8,128)(2,1)S(1)} collective-permute-done((bf16[32,1152]{1,0:T(8,128)(2,1)S(1)}, bf16[32,1152]{1,0:T(8,128)(2,1)S(1)}, u32[]{:S(2)}, u32[]{:S(2)}) %collective-permute-start.2) | collective-permute-done | bytes 73760 | tf_op jit(solution)/shard_map/ppermute | solution.py:439
  66.6 0.7 %shard_map.135 = f32[1,32]{1,0:T(1,128)} custom-call(s32[1]{0:T(128)} %bitcast.12.sec_ref, bf16[32,1152]{1,0:T(8,128)(2,1)S(1)} %collective-permute-done.2.last_ref, f32[40,1024]{1,0:T(8,128)S(1)} %get-tuple-element.237.part_ref, f32[1,32]{1,0:T(1,128)S(1)} %get-tuple-element.199.score0_ref, f32[1,32]{1,0:T(1,128)S(1)} %get-tuple-element.200.score1_ref, ...), custom_call_target="tpu_custom_call" | custom-call | flops 1000000 | tf_op jit(solution)/shard_map/pallas_call | solution.py:23
  (2 shorter events, 0.0 us)
Async XLA Ops:
  0.0 30.4 %copy-start = (bf16[1,1024,1024]{2,1,0:T(8,128)(2,1)S(1)}, bf16[1,1024,1024]{2,1,0:T(8,128)(2,1)}, u32[]{:S(2)}) copy-start(bf16[1,1024,1024]{2,1,0:T(8,128)(2,1)} %param.31) | copy-start | bytes 6291460
  0.0 30.4 %copy-start.1 = (bf16[1,2048,128]{2,1,0:T(8,128)(2,1)S(1)}, bf16[1,2048,128]{2,1,0:T(8,128)(2,1)}, u32[]{:S(2)}) copy-start(bf16[1,2048,128]{2,1,0:T(8,128)(2,1)} %param.26) | copy-start | bytes 1572868
  0.0 30.4 %copy-start.2 = (bf16[1,1024]{1,0:T(2,128)(2,1)S(1)}, bf16[1,1024]{1,0:T(2,128)(2,1)}, u32[]{:S(2)}) copy-start(bf16[1,1024]{1,0:T(2,128)(2,1)} %param.25) | copy-start | bytes 6148
  30.7 29.6 %collective-permute-start.1 = (bf16[32,1152]{1,0:T(8,128)(2,1)S(1)}, bf16[32,1152]{1,0:T(8,128)(2,1)S(1)}, u32[]{:S(2)}, u32[]{:S(2)}) collective-permute-start(bf16[32,1152]{1,0:T(8,128)(2,1)S(1)} %get-tuple-element.196), channel_id=1, source_target_pairs={{128,256},{129,257},{130,258},{131,259},{132,260},{133,261},{134,2... | collective-permute-start | bytes 221192 | tf_op jit(solution)/shard_map/ppermute | solution.py:436
  60.3 6.2 %collective-permute-start.2 = (bf16[32,1152]{1,0:T(8,128)(2,1)S(1)}, bf16[32,1152]{1,0:T(8,128)(2,1)S(1)}, u32[]{:S(2)}, u32[]{:S(2)}) collective-permute-start(bf16[32,1152]{1,0:T(8,128)(2,1)S(1)} %get-tuple-element.198), channel_id=1, source_target_pairs={{256,384},{257,385},{258,386},{259,387},{260,388},{261,389},{262,3... | collective-permute-start | bytes 221192 | tf_op jit(solution)/shard_map/ppermute | solution.py:439
